TPU v7x, 512 devices: a 8x2x16 block of a 8x16x16 slice. The times are simulated.
512 devices in a mesh: job: 2 (over y), ta: 16 (over z), xyz: 8 (over x), src: 2 (over core).
Axes of the slice: x: 8, y: 2, z: 16, core: 2. Of those that a mesh axis runs over, the one named last changes fastest.
The devices are a block of a 8x16x16 slice.
Arguments:
- spinors: float32 [64, 32, 2, 8, 3, 2048], P('src', 'ta', None, 'job', None, 'xyz'), parts along dimension 3, may hold values from -6 to 6
- eigvecs: float32 [32, 256, 2, 3, 2048], P('ta', 'job', None, None, 'xyz'), parts along dimension 1, may hold values from -0.0546875 to 0.0546875
- group_of: int32 [32], replicated, may hold values from 0 to 15, as said below
- source_ids: int32 [64], P('src'), may hold values from 0 to 63, as said below
Outputs:
- perambulator: float32 [32, 2, 8, 64, 128], P('ta', None, 'job', 'src', 'xyz'), parts along dimension 2
There are 2 independent parts, one for each index of `job`. A program takes and returns all parts, laid end to end along the dimension named above; an argument that names none is the same for every part. Nothing has to cross between parts.
Inputs may be any that keep to these rules, and one draw needn't show every extreme that they name: `group_of`: every group number appears exactly 2 times. `source_ids`: the 32 entries held by index i of src are a permutation of i * 32 to (i + 1) * 32 - 1.
All inputs are finite; a program needn't handle non-finite values.
Results may differ from a plain program's by a relative error of at most 0.00007.
Values sent between devices are 32-bit elements; how exact they have to be, the bound alone decides.
No kernel may reach another device: no remote copies, remote signals or barrier semaphores. Data moves between devices by JAX's collectives and lax.ppermute only.
A program may use at most 64 MiB of HBM per device.

v0:
```python
import jax
import jax.numpy as jnp
from jax import lax
from jax.sharding import PartitionSpec as P


def in_blocks(x, dim, size):
    dims = x.shape
    pieces = x.reshape(*dims[:dim], size, dims[dim] // size, *dims[dim + 1 :])
    return jnp.moveaxis(pieces, dim, 0)


def sent_and_summed(x, axis, dim):
    size = lax.axis_size(axis)
    pieces = lax.all_to_all(in_blocks(x, dim, size), axis, 0, 0, tiled=True)
    return jnp.sum(pieces, axis=0)


def contract_pair(vectors, spinor):
    vector_real = vectors[:, :, 0]
    vector_imag = vectors[:, :, 1]
    spinor_real = spinor[:, :, 0]
    spinor_imag = spinor[:, :, 1]

    def contract(left_side, right_side):
        return jnp.einsum(
            "tkcx,ntscx->tsnk", left_side, right_side, precision=lax.Precision.HIGHEST
        )

    real_part = contract(vector_real, spinor_real) + contract(vector_imag, spinor_imag)
    imag_part = contract(vector_real, spinor_imag) - contract(vector_imag, spinor_real)
    return jnp.stack([real_part, imag_part], axis=1)


def local(spinors, eigvecs, group_of, source_ids):
    extent = group_of.shape[0]
    sort_keys = group_of * extent + jnp.arange(extent, dtype=jnp.int32)
    ordering = jnp.argsort(sort_keys)
    spread = lax.all_to_all(spinors, "ta", split_axis=0, concat_axis=1, tiled=True)
    grouped = jnp.take(spread, ordering, axis=1)
    regrouped = lax.all_to_all(grouped, "ta", split_axis=1, concat_axis=0, tiled=True)
    partial_sums = contract_pair(eigvecs, regrouped)
    summed = sent_and_summed(partial_sums, "xyz", 4)
    inverse = jnp.argsort(source_ids)
    return jnp.take(summed, inverse, axis=3)


def solution(mesh):
    in_specs = (
        P("src", "ta", None, "job", None, "xyz"),
        P("ta", "job", None, None, "xyz"),
        P(),
        P("src"),
    )
    out_specs = P("ta", None, "job", "src", "xyz")
    return jax.shard_map(local, mesh=mesh, in_specs=in_specs, out_specs=out_specs, check_vma=False)
```

profile of v0, /device:TPU:80, one launch (start us, length us, event | category | flops | bytes accessed | tf_op | source)
XLA Modules:
  0.0 233.5 jit_solution(13181395401285672478)
XLA Ops:
  0.0 43.9 %all-to-all-start = ((f32[32,2,2,4,3,256]{5,3,4,2,1,0:T(4,128)}), f32[32,2,2,4,3,256]{5,3,4,2,1,0:T(4,128)S(1)}, u32[]{:S(2)}, u32[]{:S(2)}) async-start(f32[32,2,2,4,3,256]{5,3,4,2,1,0:T(4,128)} %param.4), calls=%async_computation | async-start | bytes 3145728 | tf_op jit(solution)/shard_map/all_to_all | solution.py:39
  43.9 0.0 copy-done
  43.9 1.6 sort.32
  45.5 72.4 %all-to-all-done = f32[32,2,2,4,3,256]{5,3,4,2,1,0:T(4,128)S(1)} async-done(((f32[32,2,2,4,3,256]{5,3,4,2,1,0:T(4,128)}), f32[32,2,2,4,3,256]{5,3,4,2,1,0:T(4,128)S(1)}, u32[]{:S(2)}, u32[]{:S(2)}) %all-to-all-start) | async-done | bytes 1572896 | tf_op jit(solution)/shard_map/all_to_all | solution.py:39
  117.9 0.3 copy.15
  118.2 1.5 gather_fusion
  119.7 1.6 select_bitcast_fusion
  121.4 6.4 %all-to-all-start.1 = ((f32[2,32,2,4,3,256]{5,3,4,2,0,1:T(4,128)}), f32[2,32,2,4,3,256]{5,3,4,2,0,1:T(4,128)S(1)}, u32[]{:S(2)}, u32[]{:S(2)}) async-start(f32[2,32,2,4,3,256]{5,3,4,2,0,1:T(4,128)} %select_bitcast_fusion), calls=%async_computation.1 | async-start | bytes 3145728 | tf_op jit(solution)/shard_map/all_to_all | solution.py:41
  127.8 0.0 copy-done.1
  127.8 1.6 sort.31
  129.4 3.4 %fusion.4 = (f32[2,128,1,3,256]{4,2,3,1,0:T(1,128)S(1)}, f32[2,128,1,3,256]{4,2,3,1,0:T(1,128)S(1)}) fusion(f32[2,128,2,3,256]{4,2,3,1,0:T(2,128)} %param.5), kind=kLoop, calls=%fused_computation.24 | loop fusion | bytes 3145728 | tf_op jit(solution)/shard_map/slice | solution.py:20
  132.8 69.2 %all-to-all-done.1 = f32[2,32,2,4,3,256]{5,3,4,2,0,1:T(4,128)S(1)} async-done(((f32[2,32,2,4,3,256]{5,3,4,2,0,1:T(4,128)}), f32[2,32,2,4,3,256]{5,3,4,2,0,1:T(4,128)S(1)}, u32[]{:S(2)}, u32[]{:S(2)}) %all-to-all-start.1) | async-done | bytes 1572896 | tf_op jit(solution)/shard_map/all_to_all | solution.py:41
  202.0 2.0 copy.17
  204.0 2.4 %all_to_all.36 = f32[32,2,2,4,3,256]{5,0,4,3,1,2:T(8,128)S(1)} reshape(f32[16,2,2,2,4,3,256]{6,1,0,5,4,2,3:T(2,128)} %copy.17) | data formatting | bytes 3145728 | tf_op jit(solution)/shard_map/all_to_all | solution.py:41
  206.4 0.9 convolution_bitcast_fusion
  207.2 0.9 convolution_bitcast_fusion.2
  208.1 0.9 fusion.1
  209.0 0.9 fusion.3
  209.9 0.2 copy.21
  210.1 0.2 copy.20
  210.3 0.1 copy_bitcast_fusion.6
  210.5 1.2 reshape.39
  211.6 7.3 %all-to-all-start.2 = ((f32[8,1,8192]{2,1,0:T(1,128)}), f32[8,1,8192]{2,1,0:T(1,128)S(1)}, u32[]{:S(2)}, u32[]{:S(2)}) async-start(f32[8,1,8192]{2,1,0:T(1,128)} %reshape.39), calls=%async_computation.2 | async-start | bytes 524288 | tf_op jit(solution)/shard_map/all_to_all | solution.py:15
  219.0 10.4 %all-to-all-done.2 = f32[8,1,8192]{2,1,0:T(1,128)S(1)} async-done(((f32[8,1,8192]{2,1,0:T(1,128)}), f32[8,1,8192]{2,1,0:T(1,128)S(1)}, u32[]{:S(2)}, u32[]{:S(2)}) %all-to-all-start.2) | async-done | bytes 262176 | tf_op jit(solution)/shard_map/all_to_all | solution.py:15
  229.4 0.5 broadcast.24
  229.9 1.3 reduce
  231.2 0.3 reshape.40
  231.5 0.1 bitcast_reduce_fusion
  231.6 0.1 copy.24
  231.8 0.7 gather_fusion.1
  232.5 0.1 select_bitcast_fusion.1
  232.7 0.8 copy.25
  (11 shorter events, 0.0 us)
Async XLA Ops:
  0.0 43.9 %copy-start = (s32[32]{0:T(128)S(1)}, s32[32]{0:T(128)}, u32[]{:S(2)}) copy-start(s32[32]{0:T(128)} %param.6) | copy-start | bytes 388
  0.0 117.9 %all-to-all-start = ((f32[32,2,2,4,3,256]{5,3,4,2,1,0:T(4,128)}), f32[32,2,2,4,3,256]{5,3,4,2,1,0:T(4,128)S(1)}, u32[]{:S(2)}, u32[]{:S(2)}) async-start(f32[32,2,2,4,3,256]{5,3,4,2,1,0:T(4,128)} %param.4), calls=%async_computation | async-start | bytes 3145728 | tf_op jit(solution)/shard_map/all_to_all | solution.py:39
  121.4 6.5 %copy-start.1 = (s32[32]{0:T(128)S(1)}, s32[32]{0:T(128)}, u32[]{:S(2)}) copy-start(s32[32]{0:T(128)} %param.7) | copy-start | bytes 388
  121.4 80.7 %all-to-all-start.1 = ((f32[2,32,2,4,3,256]{5,3,4,2,0,1:T(4,128)}), f32[2,32,2,4,3,256]{5,3,4,2,0,1:T(4,128)S(1)}, u32[]{:S(2)}, u32[]{:S(2)}) async-start(f32[2,32,2,4,3,256]{5,3,4,2,0,1:T(4,128)} %select_bitcast_fusion), calls=%async_computation.1 | async-start | bytes 3145728 | tf_op jit(solution)/shard_map/all_to_all | solution.py:41
  211.6 17.8 %all-to-all-start.2 = ((f32[8,1,8192]{2,1,0:T(1,128)}), f32[8,1,8192]{2,1,0:T(1,128)S(1)}, u32[]{:S(2)}, u32[]{:S(2)}) async-start(f32[8,1,8192]{2,1,0:T(1,128)} %reshape.39), calls=%async_computation.2 | async-start | bytes 524288 | tf_op jit(solution)/shard_map/all_to_all | solution.py:15
where the time goes:
time: 234 us; the launch traced here: 233 us
  waiting for transfers between devices  152 us (65%)
  starting transfers between devices  57.6 us (25%)
  local copies, waits for them, and re-layouts  13.6 us (6%)
  other arithmetic  6.47 us (3%)
  matrix products  3.51 us (2%)
    all_to_all x1, waiting for transfers between devices, local(): lax.all_to_all(spinors, 'ta', split_axis=0, concat_axis=1, tiled=True)  72.4 us
    all_to_all x1, waiting for transfers between devices, local(): lax.all_to_all(grouped, 'ta', split_axis=1, concat_axis=0, tiled=True)  69.2 us
    all_to_all x1, starting transfers between devices, local(): lax.all_to_all(spinors, 'ta', split_axis=0, concat_axis=1, tiled=True)  43.9 us
    all_to_all x1, waiting for transfers between devices, sent_and_summed(): pieces = lax.all_to_all(in_blocks(x, dim, size), axis, 0, 0, tiled=True)  10.4 us
    all_to_all x1, starting transfers between devices, sent_and_summed(): pieces = lax.all_to_all(in_blocks(x, dim, size), axis, 0, 0, tiled=True)  7.32 us
    all_to_all x1, starting transfers between devices, local(): lax.all_to_all(grouped, 'ta', split_axis=1, concat_axis=0, tiled=True)  6.44 us
  transfers between devices with their start and end apart: 3, of which 3 were waited for; matrix products, arithmetic and copies ran while one was open for 3% of the time, Pallas kernels for 0%

commit v1 on v0

v1 whole, which is shorter than its diff:
```python
import jax
import jax.numpy as jnp
from jax import lax
from jax.sharding import PartitionSpec as P


def rank_of(keys):
    extent = keys.shape[0]
    index = jnp.arange(extent, dtype=jnp.int32)
    before = (keys[None, :] < keys[:, None]) | (
        (keys[None, :] == keys[:, None]) & (index[None, :] < index[:, None])
    )
    return jnp.sum(before.astype(jnp.int32), axis=1)


def inverse_of(rank):
    extent = rank.shape[0]
    index = jnp.arange(extent, dtype=jnp.int32)
    hit = rank[None, :] == index[:, None]
    return jnp.sum(jnp.where(hit, index[None, :], 0), axis=1)


def project(vectors, spinor):
    def contract(left, right):
        return jnp.einsum("bticx,ntscx->tsnbi", left, right, precision=lax.Precision.HIGHEST)

    vr, vi = vectors[:, :, :, 0], vectors[:, :, :, 1]
    pr, pi = spinor[:, :, 0], spinor[:, :, 1]
    real = contract(vr, pr) + contract(vi, pi)
    imag = contract(vr, pi) - contract(vi, pr)
    return jnp.stack([real, imag], axis=1)


def local(spinors, eigvecs, group_of, source_ids):
    nta, nx, nsrc = lax.axis_size("ta"), lax.axis_size("xyz"), lax.axis_size("src")
    core = lax.axis_index("src")
    ta = lax.axis_index("ta")
    rows, k = eigvecs.shape[0], eigvecs.shape[1]
    rest = eigvecs.shape[2:]
    n, tl = spinors.shape[0], spinors.shape[1]
    mine = k // nsrc
    part = mine // nta
    per_x = mine // nx

    rank = rank_of(group_of)
    ordering = inverse_of(rank)

    share = eigvecs.reshape(rows, nx, nsrc, per_x, *rest)
    share = lax.dynamic_index_in_dim(share, core, 2, keepdims=False)
    share = share.reshape(rows, nta, part, *rest)
    spread = lax.all_to_all(share, "ta", split_axis=1, concat_axis=0, tiled=False)
    spread = spread.reshape(nta * rows, part, *rest)
    picked = jnp.take(spread, rank, axis=0)
    sent = lax.all_to_all(picked.reshape(nta, tl, part, *rest), "ta", 0, 0, tiled=True)

    held = jnp.take(spinors, inverse_of(source_ids - n * core), axis=0)
    swap = [(i, nsrc - 1 - i) for i in range(nsrc)]
    other = lax.ppermute(held, "src", swap)

    mine_out = project(sent, held)
    other_out = project(sent, other)
    first = core == 0
    pair = jnp.stack(
        [jnp.where(first, mine_out, other_out), jnp.where(first, other_out, mine_out)], axis=0
    )
    s = spinors.shape[3]
    pair = pair.reshape(nsrc, tl, 2, s, n, nx, per_x)
    pair = jnp.moveaxis(pair, 5, 0).reshape(nx * nsrc, tl, 2, s, n, per_x)
    got = lax.all_to_all(pair, ("xyz", "src"), 0, 0, tiled=True)
    summed = jnp.sum(got.reshape(nx, nsrc, tl, 2, s, n, per_x), axis=0)
    summed = jnp.moveaxis(summed, 0, 4).reshape(tl, 2, s, n, nsrc * per_x)
    everyone = lax.all_gather(summed, "ta", axis=0, tiled=True)
    wanted = lax.dynamic_slice_in_dim(ordering, ta * tl, tl, 0)
    return jnp.take(everyone, wanted, axis=0)


def solution(mesh):
    in_specs = (
        P("src", "ta", None, "job", None, "xyz"),
        P("ta", "job", None, None, "xyz"),
        P(),
        P("src"),
    )
    out_specs = P("ta", None, "job", "src", "xyz")
    return jax.shard_map(local, mesh=mesh, in_specs=in_specs, out_specs=out_specs, check_vma=False)
```

time: 234 us -> 234 us (level)
  waiting for transfers between devices: 152 us -> 81 us
  blocking collectives: 0 us -> 49.6 us
  matrix products: 3.51 us -> 21 us
  starting transfers between devices: 57.6 us -> 61.2 us
    all_to_all x3, waiting for transfers between devices: 152 us -> 81 us  [the longest x1 38.6 us: local(): lax.all_to_all(share, 'ta', split_axis=1, concat_axis=0, tiled=False)]
    all_gather x0 -> x1, blocking collectives: none -> 49.6 us  [local(): everyone = lax.all_gather(summed, 'ta', axis=0, tiled=True)]
    dot_general x4 -> x8, matrix products: 3.51 us -> 21 us  [contract(): jnp.einsum('bticx,ntscx->tsnbi', left, right, precision=lax.Precision.HIG...]
    all_to_all x4 -> x1, local copies, waits for them, and re-layouts: 5.13 us -> 0.51 us  [local(): got = lax.all_to_all(pair, ('xyz', 'src'), 0, 0, tiled=True)]
    gather x2 -> x3, local copies, waits for them, and re-layouts: 2.24 us -> 6.07 us  [the longest x1 2.54 us: local(): held = jnp.take(spinors, inverse_of(source_ids - n * core), axis=0)]
    sort x2 -> x0, other arithmetic: 3.21 us -> none  [the longest x1 1.61 us: local(): inverse = jnp.argsort(source_ids)]
  transfers between devices with their start and end apart: 3 -> 4, of which waited for: 3 -> 3; matrix products, arithmetic and copies ran while one was open for 3% -> 5% of each run, Pallas kernels for 0% -> 0%
where the time goes in v1:
time: 234 us; the launch traced here: 233 us
  waiting for transfers between devices  81 us (35%)
  starting transfers between devices  61.2 us (26%)
  blocking collectives  49.6 us (21%)
  matrix products  21 us (9%)
  local copies, waits for them, and re-layouts  14 us (6%)
  other arithmetic  5.77 us (2%)
    all_gather x1, blocking collectives, local(): everyone = lax.all_gather(summed, 'ta', axis=0, tiled=True)  49.6 us
    all_to_all x1, starting transfers between devices, local(): lax.all_to_all(share, 'ta', split_axis=1, concat_axis=0, tiled=False)  43.7 us
    all_to_all x1, waiting for transfers between devices, local(): lax.all_to_all(share, 'ta', split_axis=1, concat_axis=0, tiled=False)  38.6 us
    all_to_all x1, waiting for transfers between devices, local(): lax.all_to_all(picked.reshape(nta, tl, part, *rest), 'ta', 0, 0, tiled=True)  31.7 us
    dot_general x8, matrix products, contract(): jnp.einsum('bticx,ntscx->tsnbi', left, right, precision=lax.Precision.HIG...  21 us
    all_to_all x1, waiting for transfers between devices, local(): got = lax.all_to_all(pair, ('xyz', 'src'), 0, 0, tiled=True)  10.7 us
    all_to_all x1, starting transfers between devices, local(): lax.all_to_all(picked.reshape(nta, tl, part, *rest), 'ta', 0, 0, tiled=True)  7.79 us
    all_to_all x1, starting transfers between devices, local(): got = lax.all_to_all(pair, ('xyz', 'src'), 0, 0, tiled=True)  7.62 us
  transfers between devices with their start and end apart: 4, of which 3 were waited for; matrix products, arithmetic and copies ran while one was open for 5% of the time, Pallas kernels for 0%

profile of v1, /device:TPU:80, one launch (start us, length us, event | category | flops | bytes accessed | tf_op | source)
XLA Modules:
  0.0 233.0 jit_solution(10280203703258376125)
XLA Ops:
  0.0 1.4 copy-done
  1.4 0.3 constant_dynamic-slice_fusion
  1.7 1.3 copy.50
  3.0 43.7 %all-to-all-start = ((f32[1,2,16,4,2,3,256]{6,4,5,3,1,0,2:T(2,128)}), f32[1,2,16,4,2,3,256]{6,4,5,3,1,0,2:T(2,128)S(1)}, u32[]{:S(2)}, u32[]{:S(2)}) async-start(f32[1,2,16,4,2,3,256]{6,4,5,3,1,0,2:T(2,128)} %copy.50), calls=%async_computation | async-start | bytes 1572864 | tf_op jit(solution)/shard_map/all_to_all | solution.py:51
  46.7 0.2 convert_reduce_fusion
  47.0 38.6 %all-to-all-done = f32[1,2,16,4,2,3,256]{6,4,5,3,1,0,2:T(2,128)S(1)} async-done(((f32[1,2,16,4,2,3,256]{6,4,5,3,1,0,2:T(2,128)}), f32[1,2,16,4,2,3,256]{6,4,5,3,1,0,2:T(2,128)S(1)}, u32[]{:S(2)}, u32[]{:S(2)}) %all-to-all-start) | async-done | bytes 786464 | tf_op jit(solution)/shard_map/all_to_all | solution.py:51
  85.6 1.4 gather_fusion.1
  87.0 0.5 broadcast_select_fusion
  87.5 1.1 copy.51
  88.6 7.8 %all-to-all-start.1 = ((f32[16,2,4,2,3,256]{5,2,4,3,1,0:T(4,128)}), f32[16,2,4,2,3,256]{5,2,4,3,1,0:T(4,128)}, u32[]{:S(2)}, u32[]{:S(2)}) async-start(f32[16,2,4,2,3,256]{5,2,4,3,1,0:T(4,128)} %copy.51), calls=%async_computation.1 | async-start | bytes 1572864 | tf_op jit(solution)/shard_map/all_to_all | solution.py:54
  96.6 2.5 %gather_fusion = f32[32,2,2,4,3,256]{5,3,4,2,1,0:T(4,128)} fusion(f32[32,2,2,4,3,256]{5,3,4,2,1,0:T(4,128)S(1)} %copy-done.1, s32[1024]{0:T(1024)S(1)} %pad_clamp_fusion.2), kind=kCustom, calls=%fused_computation | custom fusion | bytes 3145856 | tf_op jit(solution)/shard_map/jit(_take)/gather | solution.py:56
  99.1 2.4 %copy_select_fusion = f32[32,2,2,4,3,256]{5,0,4,3,1,2:T(8,128)S(1)} fusion(f32[32,2,2,4,3,256]{5,3,4,2,1,0:T(4,128)} %gather_fusion, pred[32]{0:T(512)(128)(4,1)S(1)} %compare_and_fusion.1), kind=kLoop, calls=%fused_computation.3 | loop fusion | flops 393216 | bytes 3145760 | tf_op jit(solution)/shard_map/jit(_take)/select_n | solution.py:56
  101.6 2.1 collective-permute-start
  103.7 31.7 %all-to-all-done.1 = f32[16,2,4,2,3,256]{5,2,4,3,1,0:T(4,128)} async-done(((f32[16,2,4,2,3,256]{5,2,4,3,1,0:T(4,128)}), f32[16,2,4,2,3,256]{5,2,4,3,1,0:T(4,128)}, u32[]{:S(2)}, u32[]{:S(2)}) %all-to-all-start.1) | async-done | bytes 786464 | tf_op jit(solution)/shard_map/all_to_all | solution.py:54
  135.4 1.2 fusion.14
  136.6 2.1 convolution_bitcast_fusion.6
  138.7 2.1 convolution_bitcast_fusion.4
  140.7 3.2 %convolution_bitcast_fusion.2 = f32[2,32,4,16,4]{1,3,4,2,0:T(8,128)S(1)} fusion(f32[32,2,2,4,3,256]{5,0,4,3,1,2:T(8,128)} %collective-permute-done, f32[16,2,4,1,3,256]{5,2,4,3,1,0:T(4,128)S(1)} %get-tuple-element.10), kind=kOutput, calls=%fused_computation.6 | convolution fusion | flops 150994944 | bytes 1245184 | tf_op jit(solution)/shard_map/bticx,ntscx->tsnbi/dot_general | solution.py:25
  143.9 3.2 %fusion.5 = f32[2,4,32,16,4]{2,3,4,1,0:T(8,128)S(1)} fusion(f32[2,32,4,16,4]{1,3,4,2,0:T(8,128)S(1)} %convolution_bitcast_fusion.2, f32[32,2,2,4,3,256]{5,0,4,3,1,2:T(8,128)} %collective-permute-done, f32[16,2,4,1,3,256]{5,2,4,3,1,0:T(4,128)S(1)} %get-tuple-element.9), kind=kOutput, calls=%fused_computation.17 | convolution fusion | flops 151011328 | bytes 1310720 | tf_op jit(solution)/shard_map/bticx,ntscx->tsnbi/dot_general | solution.py:25
  147.2 3.2 %convolution_bitcast_fusion = f32[2,32,4,16,4]{1,3,4,2,0:T(8,128)S(1)} fusion(f32[32,2,2,4,3,256]{5,0,4,3,1,2:T(8,128)} %collective-permute-done, f32[16,2,4,1,3,256]{5,2,4,3,1,0:T(4,128)S(1)} %get-tuple-element.10), kind=kOutput, calls=%fused_computation.4 | convolution fusion | flops 150994944 | bytes 1245184 | tf_op jit(solution)/shard_map/bticx,ntscx->tsnbi/dot_general | solution.py:25
  150.4 3.2 %fusion.7 = f32[2,4,32,16,4]{2,3,4,1,0:T(8,128)S(1)} fusion(f32[2,32,4,16,4]{1,3,4,2,0:T(8,128)S(1)} %convolution_bitcast_fusion, f32[32,2,2,4,3,256]{5,0,4,3,1,2:T(8,128)} %collective-permute-done, f32[16,2,4,1,3,256]{5,2,4,3,1,0:T(4,128)S(1)} %get-tuple-element.9), kind=kOutput, calls=%fused_computation.19 | convolution fusion | flops 151011328 | bytes 1310720 | tf_op jit(solution)/shard_map/bticx,ntscx->tsnbi/dot_general | solution.py:25
  153.7 2.1 fusion.1
  155.9 2.1 fusion.3
  158.5 1.2 reshape.243
  159.6 7.6 %all-to-all-start.2 = ((f32[16,1,4096]{2,1,0:T(1,128)}), f32[16,1,4096]{2,1,0:T(1,128)S(1)}, u32[]{:S(2)}, u32[]{:S(2)}) async-start(f32[16,1,4096]{2,1,0:T(1,128)} %reshape.243), calls=%async_computation.2 | async-start | bytes 524288 | tf_op jit(solution)/shard_map/all_to_all | solution.py:69
  167.5 10.7 %all-to-all-done.2 = f32[16,1,4096]{2,1,0:T(1,128)S(1)} async-done(((f32[16,1,4096]{2,1,0:T(1,128)}), f32[16,1,4096]{2,1,0:T(1,128)S(1)}, u32[]{:S(2)}, u32[]{:S(2)}) %all-to-all-start.2) | async-done | bytes 262176 | tf_op jit(solution)/shard_map/all_to_all | solution.py:69
  178.2 0.5 broadcast.97
  178.7 1.3 reduce
  180.0 0.3 reshape.244
  180.5 49.6 %all_gather.3 = f32[32,2,4,32,16]{3,4,2,1,0:T(8,128)} all-gather(f32[2,2,4,32,16]{3,4,2,1,0:T(8,128)S(1)} %copy_bitcast_fusion.10), channel_id=1, replica_groups=mesh['job'=2,'ta'=16,'xyz'=8,'src'=2] {'ta'}, dimensions={0}, use_global_device_ids=true | all-gather | bytes 557056 | tf_op jit(solution)/shard_map/all_gather | solution.py:72
  230.1 2.1 gather_fusion.2
  232.3 0.7 broadcast_select_fusion.1
  (29 shorter events, 1.4 us)
Async XLA Ops:
  0.0 1.4 copy-start
  1.7 45.0 %copy-start.2 = (s32[32]{0:T(128)S(1)}, s32[32]{0:T(128)}, u32[]{:S(2)}) copy-start(s32[32]{0:T(128)} %param.6) | copy-start | bytes 388
  3.0 82.6 %all-to-all-start = ((f32[1,2,16,4,2,3,256]{6,4,5,3,1,0,2:T(2,128)}), f32[1,2,16,4,2,3,256]{6,4,5,3,1,0,2:T(2,128)S(1)}, u32[]{:S(2)}, u32[]{:S(2)}) async-start(f32[1,2,16,4,2,3,256]{6,4,5,3,1,0,2:T(2,128)} %copy.50), calls=%async_computation | async-start | bytes 1572864 | tf_op jit(solution)/shard_map/all_to_all | solution.py:51
  87.5 8.9 %copy-start.3 = (s32[32]{0:T(128)S(1)}, s32[32]{0:T(128)}, u32[]{:S(2)}) copy-start(s32[32]{0:T(128)} %param.7) | copy-start | bytes 388
  87.5 9.1 %copy-start.1 = (f32[32,2,2,4,3,256]{5,3,4,2,1,0:T(4,128)S(1)}, f32[32,2,2,4,3,256]{5,3,4,2,1,0:T(4,128)}, u32[]{:S(2)}) copy-start(f32[32,2,2,4,3,256]{5,3,4,2,1,0:T(4,128)} %param.4) | copy-start | bytes 4718596
  88.6 46.8 %all-to-all-start.1 = ((f32[16,2,4,2,3,256]{5,2,4,3,1,0:T(4,128)}), f32[16,2,4,2,3,256]{5,2,4,3,1,0:T(4,128)}, u32[]{:S(2)}, u32[]{:S(2)}) async-start(f32[16,2,4,2,3,256]{5,2,4,3,1,0:T(4,128)} %copy.51), calls=%async_computation.1 | async-start | bytes 1572864 | tf_op jit(solution)/shard_map/all_to_all | solution.py:54
  101.6 39.2 %collective-permute-start = (f32[32,2,2,4,3,256]{5,0,4,3,1,2:T(8,128)S(1)}, f32[32,2,2,4,3,256]{5,0,4,3,1,2:T(8,128)}, u32[]{:S(2)}, u32[]{:S(2)}) collective-permute-start(f32[32,2,2,4,3,256]{5,0,4,3,1,2:T(8,128)S(1)} %copy_select_fusion), channel_id=1, source_target_pairs={{0,1},{1,0},{2,3},{3,2},{4,5},{5,4},{6,7},{7,6},{8,9},{9,8},{10,11... | collective-permute-start | bytes 4718600 | tf_op jit(solution)/shard_map/ppermute | solution.py:58
  159.6 18.6 %all-to-all-start.2 = ((f32[16,1,4096]{2,1,0:T(1,128)}), f32[16,1,4096]{2,1,0:T(1,128)S(1)}, u32[]{:S(2)}, u32[]{:S(2)}) async-start(f32[16,1,4096]{2,1,0:T(1,128)} %reshape.243), calls=%async_computation.2 | async-start | bytes 524288 | tf_op jit(solution)/shard_map/all_to_all | solution.py:69

commit v2 on v1

v2 whole, which is shorter than its diff:
```python
import functools

import jax
import jax.numpy as jnp
from jax import lax
from jax.experimental import pallas as pl
from jax.experimental.pallas import tpu as pltpu
from jax.sharding import PartitionSpec as P

LANES = 128


def rank_of(keys):
    extent = keys.shape[0]
    index = jnp.arange(extent, dtype=jnp.int32)
    before = (keys[None, :] < keys[:, None]) | (
        (keys[None, :] == keys[:, None]) & (index[None, :] < index[:, None])
    )
    return jnp.sum(before.astype(jnp.int32), axis=1)


def inverse_of(rank):
    extent = rank.shape[0]
    index = jnp.arange(extent, dtype=jnp.int32)
    hit = rank[None, :] == index[:, None]
    return jnp.sum(jnp.where(hit, index[None, :], 0), axis=1)


def pick_rows_kernel(index_ref, table_ref, out_ref, sem):
    count = out_ref.shape[0]
    copies = [
        pltpu.make_async_copy(table_ref.at[index_ref[i]], out_ref.at[i], sem.at[i])
        for i in range(count)
    ]
    for copy in copies:
        copy.start()
    for copy in copies:
        copy.wait()


def pick_rows(table, index):
    count = index.shape[0]
    return pl.pallas_call(
        pick_rows_kernel,
        out_shape=jax.ShapeDtypeStruct((count, *table.shape[1:]), table.dtype),
        in_specs=[
            pl.BlockSpec(memory_space=pltpu.SMEM),
            pl.BlockSpec(memory_space=pl.ANY),
        ],
        out_specs=pl.BlockSpec(memory_space=pl.ANY),
        scratch_shapes=[pltpu.SemaphoreType.DMA((count,))],
        name="pick_rows",
    )(index, table)


def halves(x):
    high = x.astype(jnp.bfloat16)
    low = (x - high.astype(jnp.float32)).astype(jnp.bfloat16)
    return high, low


def product_kernel(tl, parts, cols, core_ref, v_ref, hh, hl, oh, ol, out_ref, a_hi, a_lo, b_hi, b_lo):
    nz = v_ref.shape[0] // (tl * parts * cols * 2)
    stride = tl * parts * cols * 2
    half = parts * nz
    core = core_ref[0]

    def dot(left, right):
        return lax.dot_general(
            left, right, (((1,), (1,)), ((), ())), preferred_element_type=jnp.float32
        )

    for t in range(tl):
        for i in range(parts):
            for b in range(cols):
                start = ((t * parts + i) * cols + b) * 2
                real = v_ref[pl.ds(start, nz, stride=stride), :]
                imag = v_ref[pl.ds(start + 1, nz, stride=stride), :]
                real_hi, real_lo = halves(real)
                imag_hi, imag_lo = halves(imag)
                top = pl.ds(i * nz, nz)
                low = pl.ds(half + i * nz, nz)
                lane = pl.ds(b * LANES, LANES)
                a_hi[t, top, lane] = real_hi
                a_lo[t, top, lane] = real_lo
                a_hi[t, low, lane] = -imag_hi
                a_lo[t, low, lane] = -imag_lo
                b_hi[t, top, lane] = imag_hi
                b_lo[t, top, lane] = imag_lo
                b_hi[t, low, lane] = real_hi
                b_lo[t, low, lane] = real_lo
        ah, al, bh, bl = a_hi[t], a_lo[t], b_hi[t], b_lo[t]
        for slot, high, low in ((core, hh, hl), (1 - core, oh, ol)):
            total = dot(ah, high[t, 0]) + dot(bh, high[t, 1])
            total += dot(ah, low[t, 0]) + dot(bh, low[t, 1])
            total += dot(al, high[t, 0]) + dot(bl, high[t, 1])
            nx = out_ref.shape[0]
            per = half // nx
            for ri in range(2):
                for x in range(nx):
                    out_ref[x, slot, t, ri] = total[ri * half + x * per : ri * half + (x + 1) * per]


def final_kernel(order_ref, in_ref, out_ref):
    nsk, nri, nj = in_ref.shape[1], in_ref.shape[3], in_ref.shape[4]
    ns, n = out_ref.shape[2], out_ref.shape[4]
    for sk in range(nsk):
        for ri in range(nri):
            value = in_ref[0, sk, 0, ri]
            for s in range(ns):
                out_ref[0, ri, s, sk * nj : (sk + 1) * nj, :] = value[:, s * n : (s + 1) * n]


def local(spinors, eigvecs, group_of, source_ids):
    nta, nx, nsrc = lax.axis_size("ta"), lax.axis_size("xyz"), lax.axis_size("src")
    core = lax.axis_index("src").astype(jnp.int32)
    ta = lax.axis_index("ta").astype(jnp.int32)
    rows, k, _, nc, sites = eigvecs.shape
    n, tl, _, ns = spinors.shape[:4]
    mine = k // nsrc
    part = mine // nta
    per_x = mine // nx
    fold = nta // per_x
    blocks = sites // LANES
    cols = nc * blocks

    rank = rank_of(group_of)
    ordering = inverse_of(rank)

    share = eigvecs.reshape(rows, part, fold, nsrc, per_x, 2, nc, blocks, LANES)
    share = lax.dynamic_index_in_dim(share, core, 3, keepdims=False)
    share = share.transpose(2, 3, 0, 1, 5, 6, 4, 7)
    share = share.reshape(nta, rows * part * cols * 2, LANES)
    spread = lax.all_to_all(share, "ta", 0, 0, tiled=True)
    spread = spread.reshape(nta * rows, part * cols * 2, LANES)
    picked = pick_rows(spread, rank)
    picked = picked.reshape(nta, tl * part * cols * 2, LANES)
    sent = lax.all_to_all(picked, "ta", 0, 0, tiled=True)
    sent = sent.reshape(nta * tl * part * cols * 2, LANES)

    inverse = inverse_of(source_ids - n * core)
    held = spinors.at[inverse].get(mode="promise_in_bounds")
    held = held.transpose(1, 2, 3, 0, 4, 5).reshape(tl, 2, ns * n, nc * sites)
    other = lax.ppermute(held, "src", [(i, nsrc - 1 - i) for i in range(nsrc)])

    def split(x):
        high = lax.reduce_precision(x, 8, 7)
        return high.astype(jnp.bfloat16), (x - high).astype(jnp.bfloat16)

    held_hi, held_lo = split(held)
    other_hi, other_lo = split(other)

    wide = nc * sites
    pair = pl.pallas_call(
        functools.partial(product_kernel, tl, part, cols),
        out_shape=jax.ShapeDtypeStruct((nx, nsrc, tl, 2, per_x, ns * n), jnp.float32),
        in_specs=[pl.BlockSpec(memory_space=pltpu.SMEM)]
        + [pl.BlockSpec(memory_space=pltpu.VMEM)] * 5,
        out_specs=pl.BlockSpec(memory_space=pltpu.VMEM),
        scratch_shapes=[pltpu.VMEM((tl, 2 * mine, wide), jnp.bfloat16)] * 4,
        name="product",
    )(core[None], sent, held_hi, held_lo, other_hi, other_lo)

    pair = pair.reshape(nx * nsrc, tl * 2 * per_x, ns * n)
    got = lax.all_to_all(pair, ("xyz", "src"), 0, 0, tiled=True)
    summed = jnp.sum(got.reshape(nx, nsrc * tl * 2 * per_x, ns * n), axis=0)
    everyone = lax.all_gather(summed, "ta", axis=0, tiled=False)
    everyone = everyone.reshape(nta, nsrc, tl, 2, per_x, ns * n)
    wanted = lax.dynamic_slice_in_dim(ordering, ta * rows, rows, 0)
    out = pl.pallas_call(
        final_kernel,
        out_shape=jax.ShapeDtypeStruct((rows, 2, ns, nsrc * per_x, n), jnp.float32),
        grid_spec=pltpu.PrefetchScalarGridSpec(
            num_scalar_prefetch=1,
            grid=(rows,),
            in_specs=[
                pl.BlockSpec(
                    (1, nsrc, 1, 2, per_x, ns * n),
                    lambda r, order: (order[r] // tl, 0, order[r] % tl, 0, 0, 0),
                )
            ],
            out_specs=pl.BlockSpec((1, 2, ns, nsrc * per_x, n), lambda r, order: (r, 0, 0, 0, 0)),
        ),
        name="final",
    )(wanted, everyone)
    return out.transpose(0, 1, 2, 4, 3)


def solution(mesh):
    in_specs = (
        P("src", "ta", None, "job", None, "xyz"),
        P("ta", "job", None, None, "xyz"),
        P(),
        P("src"),
    )
    out_specs = P("ta", None, "job", "src", "xyz")
    return jax.shard_map(local, mesh=mesh, in_specs=in_specs, out_specs=out_specs, check_vma=False)
```

time: 234 us -> 224 us (0.957)
  Pallas kernels: 0 us -> 32.8 us
  matrix products: 21 us -> 0 us
  blocking collectives: 49.6 us -> 37 us
  waiting for transfers between devices: 81 us -> 76.2 us
    pallas_call x0 -> x3, Pallas kernels: none -> 32.8 us  [the longest x1 26 us: pick_rows(): pl.pallas_call(pick_rows_kernel, out_shape=jax.ShapeDtypeStruct((count, *...]
    dot_general x8 -> x0, matrix products: 21 us -> none  [contract(): jnp.einsum('bticx,ntscx->tsnbi', left, right, precision=lax.Precision.HIG...]
    all_gather x1, blocking collectives: 49.6 us -> 37 us  [local(): everyone = lax.all_gather(summed, 'ta', axis=0, tiled=False)]
    reshape x1 -> x3, local copies, waits for them, and re-layouts: 0.01 us -> 7.22 us  [the longest x1 3.2 us: local(): share = eigvecs.reshape(rows, part, fold, nsrc, per_x, 2, nc, blocks, LANES)]
    all_to_all x2, waiting for transfers between devices: 70.3 us -> 64 us  [the longest x1 38.2 us: local(): spread = lax.all_to_all(share, 'ta', 0, 0, tiled=True)]
    gather x3 -> x1, local copies, waits for them, and re-layouts: 6.07 us -> 1.49 us  [local(): held = spinors.at[inverse].get(mode='promise_in_bounds')]
    select_n x6 -> x1, other arithmetic: 3.76 us -> 0.01 us  [local(): held = spinors.at[inverse].get(mode='promise_in_bounds')]
    convert_element_type x0 -> x2, other arithmetic: none -> 2.74 us  [split(): return (high.astype(jnp.bfloat16), (x - high).astype(jnp.bfloat16))]
  transfers between devices with their start and end apart: 4 -> 4, of which waited for: 3 -> 4; matrix products, arithmetic and copies ran while one was open for 5% -> 5% of each run, Pallas kernels for 0% -> 0%
where the time goes in v2:
time: 224 us; the launch traced here: 223 us
  waiting for transfers between devices  76.2 us (34%)
  starting transfers between devices  61 us (27%)
  blocking collectives  37 us (17%)
  Pallas kernels  32.8 us (15%)
  local copies, waits for them, and re-layouts  12.6 us (6%)
  other arithmetic  3.69 us (2%)
    all_to_all x1, starting transfers between devices, local(): spread = lax.all_to_all(share, 'ta', 0, 0, tiled=True)  43.7 us
    all_to_all x1, waiting for transfers between devices, local(): spread = lax.all_to_all(share, 'ta', 0, 0, tiled=True)  38.2 us
    all_gather x1, blocking collectives, local(): everyone = lax.all_gather(summed, 'ta', axis=0, tiled=False)  37 us
    pallas_call x1, Pallas kernels, pick_rows(): pl.pallas_call(pick_rows_kernel, out_shape=jax.ShapeDtypeStruct((count, *...  26 us
    all_to_all x1, waiting for transfers between devices, local(): sent = lax.all_to_all(picked, 'ta', 0, 0, tiled=True)  25.8 us
    all_to_all x1, waiting for transfers between devices, local(): got = lax.all_to_all(pair, ('xyz', 'src'), 0, 0, tiled=True)  10.2 us
    all_to_all x1, starting transfers between devices, local(): sent = lax.all_to_all(picked, 'ta', 0, 0, tiled=True)  7.75 us
    all_to_all x1, starting transfers between devices, local(): got = lax.all_to_all(pair, ('xyz', 'src'), 0, 0, tiled=True)  7.62 us
  transfers between devices with their start and end apart: 4, of which 4 were waited for; matrix products, arithmetic and copies ran while one was open for 5% of the time, Pallas kernels for 0%

profile of v2, /device:TPU:80, one launch (start us, length us, event | category | flops | bytes accessed | tf_op | source)
XLA Modules:
  0.0 223.4 jit_solution(4216248384833868065)
XLA Ops:
  0.0 0.0 copy-start
  0.0 3.2 %reshape.63 = f32[2,4,2,2,8,2,3,2,128]{8,7,5,6,4,3,2,1,0:T(2,128)S(1)} reshape(f32[2,128,2,3,256]{4,2,3,1,0:T(2,128)} %param.5) | data formatting | bytes 3145728 | tf_op jit(solution)/shard_map/reshape | solution.py:130
  3.2 0.4 constant_dynamic-slice_fusion
  3.6 0.1 copy.23
  3.7 0.0 copy-start.3
  3.7 1.1 copy.20
  4.8 43.7 %all-to-all-start = ((f32[16,96,128]{2,1,0:T(8,128)}), f32[16,96,128]{2,1,0:T(8,128)S(1)}, u32[]{:S(2)}, u32[]{:S(2)}) async-start(f32[16,96,128]{2,1,0:T(8,128)} %copy.20), calls=%async_computation | async-start | bytes 1572864 | tf_op jit(solution)/shard_map/all_to_all | solution.py:134
  48.5 0.0 copy-done.3
  48.5 0.7 convert_reduce_fusion.index_ref
  49.2 38.2 %all-to-all-done = f32[16,96,128]{2,1,0:T(8,128)S(1)} async-done(((f32[16,96,128]{2,1,0:T(8,128)}), f32[16,96,128]{2,1,0:T(8,128)S(1)}, u32[]{:S(2)}, u32[]{:S(2)}) %all-to-all-start) | async-done | bytes 786464 | tf_op jit(solution)/shard_map/all_to_all | solution.py:134
  87.4 0.9 copy-done.1
  88.3 26.0 %pick_rows.1 = f32[32,48,128]{2,1,0:T(8,128)} custom-call(s32[32]{0:T(128)} %convert_reduce_fusion.index_ref, f32[32,48,128]{2,1,0:T(8,128)} %bitcast.24), custom_call_target="tpu_custom_call" | custom-call | tf_op jit(solution)/shard_map/pick_rows/pallas_call | solution.py:43
  114.3 7.7 %all-to-all-start.1 = ((f32[16,96,128]{2,1,0:T(8,128)}), f32[16,96,128]{2,1,0:T(8,128)}, u32[]{:S(2)}, u32[]{:S(2)}) async-start(f32[16,96,128]{2,1,0:T(8,128)} %bitcast.23), calls=%async_computation.1 | async-start | bytes 1572864 | tf_op jit(solution)/shard_map/all_to_all | solution.py:138
  122.1 0.0 copy-done.4
  122.1 0.1 select_reduce_fusion
  122.2 0.0 copy-done
  122.3 1.5 gather_fusion
  123.8 1.9 copy.21
  125.6 2.9 %reshape.49 = f32[2,2,128,768]{3,2,1,0:T(8,128)S(1)} reshape(f32[2,2,4,32,3,256]{5,4,3,2,1,0:T(4,128)} %copy.21) | data formatting | bytes 3145728 | tf_op jit(solution)/shard_map/reshape | solution.py:143
  128.5 2.0 collective-permute-start
  130.5 1.4 fusion
  131.9 2.0 collective-permute-done
  133.9 1.4 fusion.1
  135.2 25.8 %all-to-all-done.1 = f32[16,96,128]{2,1,0:T(8,128)} async-done(((f32[16,96,128]{2,1,0:T(8,128)}), f32[16,96,128]{2,1,0:T(8,128)}, u32[]{:S(2)}, u32[]{:S(2)}) %all-to-all-start.1) | async-done | bytes 786464 | tf_op jit(solution)/shard_map/all_to_all | solution.py:138
  161.1 4.5 %product.1 = f32[8,2,2,2,8,128]{5,4,3,2,1,0:T(8,128)} custom-call(s32[1]{0:T(128)} %bitcast.core_ref, f32[1536,128]{1,0:T(8,128)} %bitcast.7.v_ref, bf16[2,2,128,768]{3,2,1,0:T(8,128)(2,1)} %get-tuple-element.8.hh, bf16[2,2,128,768]{3,2,1,0:T(8,128)(2,1)} %get-tuple-element.7.hl, bf16[2,2,128,768]{3,2,1,0:T(8,128)(2,1)} %get-tuple-element.6.oh, ...), custom_call_target="tpu_custom_call" | custom-call | tf_op jit(solution)/shard_map/product/pallas_call | solution.py:154
  165.6 7.6 %all-to-all-start.2 = ((f32[16,32,128]{2,1,0:T(8,128)}), f32[16,32,128]{2,1,0:T(8,128)S(1)}, u32[]{:S(2)}, u32[]{:S(2)}) async-start(f32[16,32,128]{2,1,0:T(8,128)} %bitcast.27), calls=%async_computation.2 | async-start | bytes 524288 | tf_op jit(solution)/shard_map/all_to_all | solution.py:165
  173.2 0.0 copy-done.2
  173.3 0.1 select_reduce_fusion.1
  173.4 0.7 dynamic_slice.7.order_ref
  174.0 10.2 %all-to-all-done.2 = f32[16,32,128]{2,1,0:T(8,128)S(1)} async-done(((f32[16,32,128]{2,1,0:T(8,128)}), f32[16,32,128]{2,1,0:T(8,128)S(1)}, u32[]{:S(2)}, u32[]{:S(2)}) %all-to-all-start.2) | async-done | bytes 262176 | tf_op jit(solution)/shard_map/all_to_all | solution.py:165
  184.2 37.0 %all-gather = f32[1024,128]{1,0:T(8,128)} all-gather(f32[64,128]{1,0:T(8,128)S(1)} %bitcast_reduce_fusion), channel_id=2, replica_groups=mesh['job'=2,'ta'=16,'xyz'=8,'src'=2] {'ta'}, dimensions={0}, use_global_device_ids=true | all-gather | bytes 557056 | tf_op jit(solution)/shard_map/all_gather | solution.py:167
  221.2 2.2 final.1
  (7 shorter events, 0.0 us)
Async XLA Ops:
  0.0 122.2 %copy-start = (f32[32,2,2,4,3,256]{5,3,4,2,1,0:T(4,128)S(1)}, f32[32,2,2,4,3,256]{5,3,4,2,1,0:T(4,128)}, u32[]{:S(2)}) copy-start(f32[32,2,2,4,3,256]{5,3,4,2,1,0:T(4,128)} %param.4) | copy-start | bytes 4718596
  3.7 44.8 %copy-start.3 = (s32[32]{0:T(128)S(1)}, s32[32]{0:T(128)}, u32[]{:S(2)}) copy-start(s32[32]{0:T(128)} %param.6) | copy-start | bytes 388
  4.8 82.6 %all-to-all-start = ((f32[16,96,128]{2,1,0:T(8,128)}), f32[16,96,128]{2,1,0:T(8,128)S(1)}, u32[]{:S(2)}, u32[]{:S(2)}) async-start(f32[16,96,128]{2,1,0:T(8,128)} %copy.20), calls=%async_computation | async-start | bytes 1572864 | tf_op jit(solution)/shard_map/all_to_all | solution.py:134
  87.4 0.9 copy-start.1
  88.3 33.8 %copy-start.4 = (s32[32]{0:T(128)S(1)}, s32[32]{0:T(128)}, u32[]{:S(2)}) copy-start(s32[32]{0:T(128)} %param.7) | copy-start | bytes 388
  114.3 46.7 %all-to-all-start.1 = ((f32[16,96,128]{2,1,0:T(8,128)}), f32[16,96,128]{2,1,0:T(8,128)}, u32[]{:S(2)}, u32[]{:S(2)}) async-start(f32[16,96,128]{2,1,0:T(8,128)} %bitcast.23), calls=%async_computation.1 | async-start | bytes 1572864 | tf_op jit(solution)/shard_map/all_to_all | solution.py:138
  128.5 5.3 %collective-permute-start = (f32[2,2,128,768]{3,2,1,0:T(8,128)S(1)}, f32[2,2,128,768]{3,2,1,0:T(8,128)S(1)}, u32[]{:S(2)}, u32[]{:S(2)}) collective-permute-start(f32[2,2,128,768]{3,2,1,0:T(8,128)S(1)} %reshape.49), channel_id=1, source_target_pairs={{0,1},{1,0},{2,3},{3,2},{4,5},{5,4},{6,7},{7,6},{8,9},{9,8},{10,11... | collective-permute-start | bytes 4718600 | tf_op jit(solution)/shard_map/ppermute | solution.py:144
  161.1 12.2 %copy-start.2 = (s32[32]{0:T(128)S(1)}, s32[32]{0:T(128)}, u32[]{:S(2)}) copy-start(s32[32]{0:T(128)} %convert_reduce_fusion.index_ref) | copy-start | bytes 388
  165.6 18.6 %all-to-all-start.2 = ((f32[16,32,128]{2,1,0:T(8,128)}), f32[16,32,128]{2,1,0:T(8,128)S(1)}, u32[]{:S(2)}, u32[]{:S(2)}) async-start(f32[16,32,128]{2,1,0:T(8,128)} %bitcast.27), calls=%async_computation.2 | async-start | bytes 524288 | tf_op jit(solution)/shard_map/all_to_all | solution.py:165

commit v3 on v2

v3 whole, which is shorter than its diff:
```python
import jax
import jax.numpy as jnp
from jax import lax
from jax.experimental import pallas as pl
from jax.experimental.pallas import tpu as pltpu
from jax.sharding import Mesh
from jax.sharding import PartitionSpec as P


def rank_of(keys):
    extent = keys.shape[0]
    index = jnp.arange(extent, dtype=jnp.int32)
    before = (keys[None, :] < keys[:, None]) | (
        (keys[None, :] == keys[:, None]) & (index[None, :] < index[:, None])
    )
    return jnp.sum(before.astype(jnp.int32), axis=1)


def inverse_of(rank):
    extent = rank.shape[0]
    index = jnp.arange(extent, dtype=jnp.int32)
    hit = rank[None, :] == index[:, None]
    return jnp.sum(jnp.where(hit, index[None, :], 0), axis=1)


def small(mib):
    return pltpu.CompilerParams(vmem_limit_bytes=mib << 20)


def share_kernel(core_ref, in_ref, out_ref, sem):
    rows, parts = in_ref.shape[:2]
    core = core_ref[0]
    copies = [
        pltpu.make_async_copy(
            in_ref.at[r, i, :, core], out_ref.at[:, :, r, i], sem.at[r * parts + i]
        )
        for r in range(rows)
        for i in range(parts)
    ]
    for copy in copies:
        copy.start()
    for copy in copies:
        copy.wait()


def pick_rows_kernel(index_ref, table_ref, out_ref, sem):
    count = out_ref.shape[0]
    copies = [
        pltpu.make_async_copy(table_ref.at[index_ref[i]], out_ref.at[i], sem.at[i])
        for i in range(count)
    ]
    for copy in copies:
        copy.start()
    for copy in copies:
        copy.wait()


def pick_rows(table, index):
    count = index.shape[0]
    return pl.pallas_call(
        pick_rows_kernel,
        out_shape=jax.ShapeDtypeStruct((count, *table.shape[1:]), table.dtype),
        in_specs=[
            pl.BlockSpec(memory_space=pltpu.SMEM),
            pl.BlockSpec(memory_space=pltpu.VMEM),
        ],
        out_specs=pl.BlockSpec(memory_space=pl.ANY),
        scratch_shapes=[pltpu.SemaphoreType.DMA((count,))],
        compiler_params=small(4),
        name="pick_rows",
    )(index, table)


def halves(x):
    high = x.astype(jnp.bfloat16)
    low = (x - high.astype(jnp.float32)).astype(jnp.bfloat16)
    return high, low


def product_kernel(core_ref, v_ref, hh, hl, oh, ol, out_ref, a_hi, a_lo, b_hi, b_lo):
    nz, tl, parts, nc, _, sites = v_ref.shape
    half = parts * nz
    nq, nx, _, _, piece, _ = out_ref.shape
    core = core_ref[0]

    def dot(left, right):
        return lax.dot_general(
            left, right, (((1,), (1,)), ((), ())), preferred_element_type=jnp.float32
        )

    for t in range(tl):
        for i in range(parts):
            for c in range(nc):
                real_hi, real_lo = halves(v_ref[:, t, i, c, 0, :])
                imag_hi, imag_lo = halves(v_ref[:, t, i, c, 1, :])
                top = pl.ds(i * nz, nz)
                low = pl.ds(half + i * nz, nz)
                lane = pl.ds(c * sites, sites)
                a_hi[t, top, lane] = real_hi
                a_lo[t, top, lane] = real_lo
                a_hi[t, low, lane] = -imag_hi
                a_lo[t, low, lane] = -imag_lo
                b_hi[t, top, lane] = imag_hi
                b_lo[t, top, lane] = imag_lo
                b_hi[t, low, lane] = real_hi
                b_lo[t, low, lane] = real_lo
        ah, al, bh, bl = a_hi[t], a_lo[t], b_hi[t], b_lo[t]
        for slot, high, low in ((core, hh, hl), (1 - core, oh, ol)):
            total = dot(ah, high[t, 0]) + dot(bh, high[t, 1])
            total += dot(ah, low[t, 0]) + dot(bh, low[t, 1])
            total += dot(al, high[t, 0]) + dot(bl, high[t, 1])
            per = half // nx
            for q in range(nq):
                ri, part = divmod(q, nq // 2)
                for x in range(nx):
                    first = ri * half + x * per + part * piece
                    out_ref[q, x, slot, t] = total[first : first + piece]


def sum_kernel(index_ref, in_ref, out_ref, held):
    near, nx, nsrc, tl = in_ref.shape[:4]
    for z in range(near):
        total = in_ref[z, 0]
        for x in range(1, nx):
            total += in_ref[z, x]
        for t in range(tl):
            for core in range(nsrc):
                held[z * tl + t, core] = total[core, t]
    for row in range(out_ref.shape[0]):
        out_ref[row] = held[index_ref[row]]


def final_kernel(order_ref, in_ref, out_ref):
    nq, nsrc, piece = in_ref.shape[1], in_ref.shape[3], in_ref.shape[4]
    ns, n = out_ref.shape[2], out_ref.shape[4]
    parts = nq // 2
    for core in range(nsrc):
        for ri in range(2):
            for part in range(parts):
                value = in_ref[0, ri * parts + part, 0, core]
                first = (core * parts + part) * piece
                for s in range(ns):
                    out_ref[0, ri, s, first : first + piece, :] = value[:, s * n : (s + 1) * n]


TA = ("tq", "tp")
NEAR = 4


def local(spinors, eigvecs, group_of, source_ids):
    nta, nx, nsrc = lax.axis_size(TA), lax.axis_size("xyz"), lax.axis_size("src")
    near = lax.axis_size("tp")
    core = lax.axis_index("src").astype(jnp.int32)
    ta = lax.axis_index(TA).astype(jnp.int32)
    rows, k, _, nc, sites = eigvecs.shape
    n, tl, _, ns = spinors.shape[:4]
    mine = k // nsrc
    part = mine // nta
    per_x = mine // nx
    fold = nta // per_x

    rank = rank_of(group_of)
    ordering = inverse_of(rank)

    tail = (nc, 2, sites)
    share = pl.pallas_call(
        share_kernel,
        out_shape=jax.ShapeDtypeStruct((fold, per_x, rows, part, *tail), jnp.float32),
        in_specs=[
            pl.BlockSpec(memory_space=pltpu.SMEM),
            pl.BlockSpec(memory_space=pl.ANY),
        ],
        out_specs=pl.BlockSpec(memory_space=pltpu.VMEM),
        scratch_shapes=[pltpu.SemaphoreType.DMA((rows * part,))],
        compiler_params=small(4),
        name="share",
    )(
        core[None],
        eigvecs.transpose(0, 1, 3, 2, 4).reshape(rows, part, fold, nsrc, per_x, *tail),
    )
    share = share.reshape(nta, rows, part, *tail)
    spread = lax.all_to_all(share, TA, 0, 0, tiled=True)
    picked = pick_rows(spread.reshape(nta * rows, part, *tail), rank)
    sent = lax.all_to_all(picked.reshape(nta, tl, part, *tail), TA, 0, 0, tiled=True)

    inverse = inverse_of(source_ids - n * core)
    held = spinors.at[inverse].get(mode="promise_in_bounds")
    held = held.transpose(1, 2, 3, 0, 4, 5).reshape(tl, 2, ns * n, nc * sites)
    other = lax.ppermute(held, "src", [(i, nsrc - 1 - i) for i in range(nsrc)])

    def split(x):
        high = lax.reduce_precision(x, 8, 7)
        return high.astype(jnp.bfloat16), (x - high).astype(jnp.bfloat16)

    held_hi, held_lo = split(held)
    other_hi, other_lo = split(other)

    piece = 2 * per_x // near
    pair = pl.pallas_call(
        product_kernel,
        out_shape=jax.ShapeDtypeStruct((near, nx, nsrc, tl, piece, ns * n), jnp.float32),
        in_specs=[pl.BlockSpec(memory_space=pltpu.SMEM)]
        + [pl.BlockSpec(memory_space=pltpu.VMEM)] * 5,
        out_specs=pl.BlockSpec(memory_space=pltpu.VMEM),
        scratch_shapes=[pltpu.VMEM((tl, 2 * mine, nc * sites), jnp.bfloat16)] * 4,
        compiler_params=small(16),
        name="product",
    )(core[None], sent, held_hi, held_lo, other_hi, other_lo)

    pair = pair.reshape(near * nx * nsrc, tl, piece, ns * n)
    got = lax.all_to_all(pair, ("tp", "xyz", "src"), 0, 0, tiled=True)
    here = jnp.clip(ordering - (ta // near) * (near * tl), 0, near * tl - 1)
    back = pl.pallas_call(
        sum_kernel,
        out_shape=jax.ShapeDtypeStruct((nta * rows, nsrc, piece, ns * n), jnp.float32),
        in_specs=[
            pl.BlockSpec(memory_space=pltpu.SMEM),
            pl.BlockSpec(memory_space=pltpu.VMEM),
        ],
        out_specs=pl.BlockSpec(memory_space=pltpu.VMEM),
        scratch_shapes=[pltpu.VMEM((near * tl, nsrc, piece, ns * n), jnp.float32)],
        compiler_params=small(4),
        name="sum_over_xyz",
    )(here, got.reshape(near, nx, nsrc, tl, piece, ns * n))

    home = lax.all_to_all(back.reshape(nta, rows, nsrc, piece, ns * n), TA, 0, 0, tiled=True)
    home = home.reshape(nta // near, near, rows, nsrc, piece, ns * n)
    wanted = lax.dynamic_slice_in_dim(ordering, ta * rows, rows, 0)
    out = pl.pallas_call(
        final_kernel,
        out_shape=jax.ShapeDtypeStruct((rows, 2, ns, nsrc * per_x, n), jnp.float32),
        grid_spec=pltpu.PrefetchScalarGridSpec(
            num_scalar_prefetch=1,
            grid=(rows,),
            in_specs=[
                pl.BlockSpec(
                    (1, near, 1, nsrc, piece, ns * n),
                    lambda r, order: (order[r] // (near * tl), 0, r, 0, 0, 0),
                )
            ],
            out_specs=pl.BlockSpec((1, 2, ns, nsrc * per_x, n), lambda r, order: (r, 0, 0, 0, 0)),
        ),
        compiler_params=small(4),
        name="final",
    )(wanted, home)
    return out.transpose(0, 1, 2, 4, 3)


def solution(mesh):
    shape = dict(mesh.shape)
    cut = (shape["job"], shape["ta"] // NEAR, NEAR, shape["xyz"], shape["src"])
    mesh = Mesh(mesh.devices.reshape(cut), ("job", *TA, "xyz", "src"))
    in_specs = (
        P("src", TA, None, "job", None, "xyz"),
        P(TA, "job", None, None, "xyz"),
        P(),
        P("src"),
    )
    out_specs = P(TA, None, "job", "src", "xyz")
    return jax.shard_map(local, mesh=mesh, in_specs=in_specs, out_specs=out_specs, check_vma=False)
```

time: 224 us -> 191 us (0.85)
  blocking collectives: 37 us -> 0 us
  Pallas kernels: 32.8 us -> 10 us
  starting transfers between devices: 61 us -> 73.4 us
  waiting for transfers between devices: 76.2 us -> 87.6 us
    all_gather x1 -> x0, blocking collectives: 37 us -> none  [local(): everyone = lax.all_gather(summed, 'ta', axis=0, tiled=False)]
    pallas_call x1, Pallas kernels: 26 us -> 1.71 us  [pick_rows(): pl.pallas_call(pick_rows_kernel, out_shape=jax.ShapeDtypeStruct((count, *...]
    all_to_all x3 -> x4, starting transfers between devices: 59.1 us -> 71.4 us  [the longest x1 43.7 us: local(): spread = lax.all_to_all(share, TA, 0, 0, tiled=True)]
    all_to_all x3 -> x4, waiting for transfers between devices: 74.2 us -> 86.5 us  [the longest x1 38.7 us: local(): spread = lax.all_to_all(share, TA, 0, 0, tiled=True)]
    reshape x2 -> x0, local copies, waits for them, and re-layouts: 4.33 us -> none  [the longest x1 3.2 us: local(): share = eigvecs.reshape(rows, part, fold, nsrc, per_x, 2, nc, blocks, LANES)]
    unnamed x10 -> x14, local copies, waits for them, and re-layouts: 0.91 us -> 4.94 us
    pallas_call x1 -> x3, Pallas kernels: 4.53 us -> 6.85 us  [the longest x1 4.51 us: local(): pl.pallas_call(product_kernel, out_shape=jax.ShapeDtypeStruct((near, nx,...]
  transfers between devices with their start and end apart: 4 -> 5, of which waited for: 4 -> 5; matrix products, arithmetic and copies ran while one was open for 5% -> 7% of each run, Pallas kernels for 0% -> 0%
where the time goes in v3:
time: 191 us; the launch traced here: 190 us
  waiting for transfers between devices  87.6 us (46%)
  starting transfers between devices  73.4 us (38%)
  local copies, waits for them, and re-layouts  14.7 us (8%)
  Pallas kernels  10 us (5%)
  other arithmetic  4.32 us (2%)
    all_to_all x1, starting transfers between devices, local(): spread = lax.all_to_all(share, TA, 0, 0, tiled=True)  43.7 us
    all_to_all x1, waiting for transfers between devices, local(): spread = lax.all_to_all(share, TA, 0, 0, tiled=True)  38.7 us
    all_to_all x1, waiting for transfers between devices, local(): lax.all_to_all(picked.reshape(nta, tl, part, *tail), TA, 0, 0, tiled=True)  22.1 us
    all_to_all x1, waiting for transfers between devices, local(): lax.all_to_all(back.reshape(nta, rows, nsrc, piece, ns * n), TA, 0, 0, ti...  14.5 us
    all_to_all x1, starting transfers between devices, local(): got = lax.all_to_all(pair, ('tp', 'xyz', 'src'), 0, 0, tiled=True)  12.8 us
    all_to_all x1, waiting for transfers between devices, local(): got = lax.all_to_all(pair, ('tp', 'xyz', 'src'), 0, 0, tiled=True)  11.2 us
    all_to_all x1, starting transfers between devices, local(): lax.all_to_all(picked.reshape(nta, tl, part, *tail), TA, 0, 0, tiled=True)  7.83 us
    all_to_all x1, starting transfers between devices, local(): lax.all_to_all(back.reshape(nta, rows, nsrc, piece, ns * n), TA, 0, 0, ti...  7.05 us
  transfers between devices with their start and end apart: 5, of which 5 were waited for; matrix products, arithmetic and copies ran while one was open for 7% of the time, Pallas kernels for 0%

profile of v3, /device:TPU:80, one launch (start us, length us, event | category | flops | bytes accessed | tf_op | source)
XLA Modules:
  0.0 190.1 jit_solution(7186290525337981227)
XLA Ops:
  0.0 0.0 copy-start
  0.0 1.5 copy-done.4
  1.5 1.1 share.1
  2.6 43.7 %all-to-all-start = ((f32[16,2,4,3,2,256]{5,4,3,2,1,0:T(2,128)}), f32[16,2,4,3,2,256]{5,4,3,2,1,0:T(2,128)S(1)}, u32[]{:S(2)}, u32[]{:S(2)}) async-start(f32[16,2,4,3,2,256]{5,4,3,2,1,0:T(2,128)} %bitcast.3), calls=%async_computation | async-start | bytes 1572864 | tf_op jit(solution)/shard_map/all_to_all | solution.py:182
  46.3 0.0 copy-done.5
  46.3 0.2 convert_reduce_fusion.index_ref
  46.5 38.7 %all-to-all-done = f32[16,2,4,3,2,256]{5,4,3,2,1,0:T(2,128)S(1)} async-done(((f32[16,2,4,3,2,256]{5,4,3,2,1,0:T(2,128)}), f32[16,2,4,3,2,256]{5,4,3,2,1,0:T(2,128)S(1)}, u32[]{:S(2)}, u32[]{:S(2)}) %all-to-all-start) | async-done | bytes 786464 | tf_op jit(solution)/shard_map/all_to_all | solution.py:182
  85.2 1.7 pick_rows.1
  86.9 7.8 %all-to-all-start.1 = ((f32[16,2,4,3,2,256]{5,4,3,2,1,0:T(2,128)}), f32[16,2,4,3,2,256]{5,4,3,2,1,0:T(2,128)S(1)}, u32[]{:S(2)}, u32[]{:S(2)}) async-start(f32[16,2,4,3,2,256]{5,4,3,2,1,0:T(2,128)} %bitcast.5), calls=%async_computation.1 | async-start | bytes 1572864 | tf_op jit(solution)/shard_map/all_to_all | solution.py:184
  94.8 0.0 copy-done.6
  94.8 0.1 select_reduce_fusion
  94.9 0.0 copy-done
  94.9 2.5 %gather_fusion = f32[32,2,2,4,3,256]{5,3,4,2,1,0:T(4,128)} fusion(f32[32,2,2,4,3,256]{5,3,4,2,1,0:T(4,128)S(1)} %copy-done, s32[1024]{0:T(1024)S(1)} %pad_clamp_fusion), kind=kCustom, calls=%fused_computation | custom fusion | bytes 3145856 | tf_op jit(solution)/shard_map/gather | solution.py:187
  97.5 3.3 %copy.7 = f32[2,2,4,32,3,256]{5,4,3,2,1,0:T(4,128)} copy(f32[2,2,4,32,3,256]{5,2,4,1,0,3:T(4,128)} %bitcast.21) | data formatting | bytes 3145728 | tf_op jit(solution)/shard_map/transpose | solution.py:188
  100.8 3.9 %reshape.48 = f32[2,2,128,768]{3,2,1,0:T(8,128)} reshape(f32[2,2,4,32,3,256]{5,4,3,2,1,0:T(4,128)} %copy.7) | data formatting | bytes 3145728 | tf_op jit(solution)/shard_map/reshape | solution.py:188
  104.6 1.9 %collective-permute-start = (f32[2,2,128,768]{3,2,1,0:T(8,128)}, f32[2,2,128,768]{3,2,1,0:T(8,128)S(1)}, u32[]{:S(2)}, u32[]{:S(2)}) collective-permute-start(f32[2,2,128,768]{3,2,1,0:T(8,128)} %reshape.48), channel_id=1, source_target_pairs={{0,1},{1,0},{2,3},{3,2},{4,5},{5,4},{6,7},{7,6},{8,9},{9,8},{10,11... | collective-permute-start | bytes 4718600 | tf_op jit(solution)/shard_map/ppermute | solution.py:189
  106.6 2.5 %fusion = (bf16[2,2,128,768]{3,2,1,0:T(8,128)(2,1)S(1)}, bf16[2,2,128,768]{3,2,1,0:T(8,128)(2,1)}) fusion(f32[2,2,128,768]{3,2,1,0:T(8,128)} %reshape.48), kind=kLoop, calls=%fused_computation.5 | loop fusion | flops 1572864 | bytes 3145728 | tf_op jit(solution)/shard_map/convert_element_type | solution.py:193
  109.1 1.1 collective-permute-done
  110.2 1.4 fusion.1
  111.6 22.1 %all-to-all-done.1.v_ref = f32[16,2,4,3,2,256]{5,4,3,2,1,0:T(2,128)S(1)} async-done(((f32[16,2,4,3,2,256]{5,4,3,2,1,0:T(2,128)}), f32[16,2,4,3,2,256]{5,4,3,2,1,0:T(2,128)S(1)}, u32[]{:S(2)}, u32[]{:S(2)}) %all-to-all-start.1) | async-done | bytes 786464 | tf_op jit(solution)/shard_map/all_to_all | solution.py:184
  133.7 1.1 copy-done.1
  134.8 1.1 copy-done.2
  135.9 1.1 copy-done.3
  137.1 4.5 %product.1 = f32[4,8,2,2,4,128]{5,4,3,2,1,0:T(4,128)} custom-call(s32[1]{0:T(128)} %bitcast.core_ref, f32[16,2,4,3,2,256]{5,4,3,2,1,0:T(2,128)S(1)} %all-to-all-done.1.v_ref, bf16[2,2,128,768]{3,2,1,0:T(8,128)(2,1)S(1)} %copy-done.1, bf16[2,2,128,768]{3,2,1,0:T(8,128)(2,1)S(1)} %get-tuple-element.7.hl, bf16[2,2,128,768]{3,2,1,0:T(8,128)(2,1)S(1)} %copy-done.3, ...), custom_call_target="tpu_custom_call" | custom-call | tf_op jit(solution)/shard_map/product/pallas_call | solution.py:199
  141.6 12.8 %all-to-all-start.2 = ((f32[64,2,4,128]{3,2,1,0:T(4,128)}), f32[64,2,4,128]{3,2,1,0:T(4,128)S(1)}, u32[]{:S(2)}, u32[]{:S(2)}) async-start(f32[64,2,4,128]{3,2,1,0:T(4,128)} %bitcast.9), calls=%async_computation.2 | async-start | bytes 524288 | tf_op jit(solution)/shard_map/all_to_all | solution.py:211
  154.4 0.1 select_reduce_fusion.1
  154.6 11.2 %all-to-all-done.2 = f32[64,2,4,128]{3,2,1,0:T(4,128)S(1)} async-done(((f32[64,2,4,128]{3,2,1,0:T(4,128)}), f32[64,2,4,128]{3,2,1,0:T(4,128)S(1)}, u32[]{:S(2)}, u32[]{:S(2)}) %all-to-all-start.2) | async-done | bytes 262176 | tf_op jit(solution)/shard_map/all_to_all | solution.py:211
  165.8 1.2 sum_over_xyz.1
  167.0 7.1 %all-to-all-start.3 = ((f32[16,2,2,4,128]{4,3,2,1,0:T(4,128)}), f32[16,2,2,4,128]{4,3,2,1,0:T(4,128)S(1)}, u32[]{:S(2)}, u32[]{:S(2)}) async-start(f32[16,2,2,4,128]{4,3,2,1,0:T(4,128)} %bitcast.11), calls=%async_computation.3 | async-start | bytes 262144 | tf_op jit(solution)/shard_map/all_to_all | solution.py:226
  174.1 0.1 dynamic_slice.3.order_ref
  174.2 14.5 %all-to-all-done.3 = f32[16,2,2,4,128]{4,3,2,1,0:T(4,128)S(1)} async-done(((f32[16,2,2,4,128]{4,3,2,1,0:T(4,128)}), f32[16,2,2,4,128]{4,3,2,1,0:T(4,128)S(1)}, u32[]{:S(2)}, u32[]{:S(2)}) %all-to-all-start.3) | async-done | bytes 131104 | tf_op jit(solution)/shard_map/all_to_all | solution.py:226
  188.7 1.5 final.1
  (10 shorter events, 0.0 us)
Async XLA Ops:
  0.0 94.9 %copy-start = (f32[32,2,2,4,3,256]{5,3,4,2,1,0:T(4,128)S(1)}, f32[32,2,2,4,3,256]{5,3,4,2,1,0:T(4,128)}, u32[]{:S(2)}) copy-start(f32[32,2,2,4,3,256]{5,3,4,2,1,0:T(4,128)} %param.4) | copy-start | bytes 4718596
  0.0 1.5 copy-start.4
  1.5 44.8 %copy-start.5 = (s32[32]{0:T(128)S(1)}, s32[32]{0:T(128)}, u32[]{:S(2)}) copy-start(s32[32]{0:T(128)} %param.6) | copy-start | bytes 388
  2.6 82.6 %all-to-all-start = ((f32[16,2,4,3,2,256]{5,4,3,2,1,0:T(2,128)}), f32[16,2,4,3,2,256]{5,4,3,2,1,0:T(2,128)S(1)}, u32[]{:S(2)}, u32[]{:S(2)}) async-start(f32[16,2,4,3,2,256]{5,4,3,2,1,0:T(2,128)} %bitcast.3), calls=%async_computation | async-start | bytes 1572864 | tf_op jit(solution)/shard_map/all_to_all | solution.py:182
  85.2 9.6 %copy-start.6 = (s32[32]{0:T(128)S(1)}, s32[32]{0:T(128)}, u32[]{:S(2)}) copy-start(s32[32]{0:T(128)} %param.7) | copy-start | bytes 388
  86.9 46.7 %all-to-all-start.1 = ((f32[16,2,4,3,2,256]{5,4,3,2,1,0:T(2,128)}), f32[16,2,4,3,2,256]{5,4,3,2,1,0:T(2,128)S(1)}, u32[]{:S(2)}, u32[]{:S(2)}) async-start(f32[16,2,4,3,2,256]{5,4,3,2,1,0:T(2,128)} %bitcast.5), calls=%async_computation.1 | async-start | bytes 1572864 | tf_op jit(solution)/shard_map/all_to_all | solution.py:184
  104.6 5.5 %collective-permute-start = (f32[2,2,128,768]{3,2,1,0:T(8,128)}, f32[2,2,128,768]{3,2,1,0:T(8,128)S(1)}, u32[]{:S(2)}, u32[]{:S(2)}) collective-permute-start(f32[2,2,128,768]{3,2,1,0:T(8,128)} %reshape.48), channel_id=1, source_target_pairs={{0,1},{1,0},{2,3},{3,2},{4,5},{5,4},{6,7},{7,6},{8,9},{9,8},{10,11... | collective-permute-start | bytes 4718600 | tf_op jit(solution)/shard_map/ppermute | solution.py:189
  133.7 1.1 copy-start.1
  134.8 1.1 copy-start.2
  135.9 1.1 copy-start.3
  141.6 24.2 %all-to-all-start.2 = ((f32[64,2,4,128]{3,2,1,0:T(4,128)}), f32[64,2,4,128]{3,2,1,0:T(4,128)S(1)}, u32[]{:S(2)}, u32[]{:S(2)}) async-start(f32[64,2,4,128]{3,2,1,0:T(4,128)} %bitcast.9), calls=%async_computation.2 | async-start | bytes 524288 | tf_op jit(solution)/shard_map/all_to_all | solution.py:211
  167.0 21.6 %all-to-all-start.3 = ((f32[16,2,2,4,128]{4,3,2,1,0:T(4,128)}), f32[16,2,2,4,128]{4,3,2,1,0:T(4,128)S(1)}, u32[]{:S(2)}, u32[]{:S(2)}) async-start(f32[16,2,2,4,128]{4,3,2,1,0:T(4,128)} %bitcast.11), calls=%async_computation.3 | async-start | bytes 262144 | tf_op jit(solution)/shard_map/all_to_all | solution.py:226

commit v4 on v3

--- a/solution.py
+++ b/solution.py
@@ -1,3 +1,5 @@
+import functools
+
 import jax
 import jax.numpy as jnp
 from jax import lax
@@ -7,6 +9,9 @@
 from jax.sharding import PartitionSpec as P
 
 
+LANES = 128
+
+
 def rank_of(keys):
     extent = keys.shape[0]
     index = jnp.arange(extent, dtype=jnp.int32)
@@ -27,20 +32,27 @@
     return pltpu.CompilerParams(vmem_limit_bytes=mib << 20)
 
 
-def share_kernel(core_ref, in_ref, out_ref, sem):
-    rows, parts = in_ref.shape[:2]
+def share_kernel(core_ref, in_ref, out_ref, held, sem):
+    rows, parts, folds, _, per_x, nc, _, sites = in_ref.shape
     core = core_ref[0]
     copies = [
         pltpu.make_async_copy(
-            in_ref.at[r, i, :, core], out_ref.at[:, :, r, i], sem.at[r * parts + i]
+            in_ref.at[r, i, :, core], held.at[r * parts + i], sem.at[r * parts + i]
         )
         for r in range(rows)
         for i in range(parts)
     ]
     for copy in copies:
         copy.start()
-    for copy in copies:
+    for p, copy in enumerate(copies):
         copy.wait()
+        line = p * nc * 2 * (sites // LANES)
+        for c in range(nc):
+            for lane in range(0, sites, LANES):
+                for f in range(folds):
+                    value = held[p, f, :, c, :, lane : lane + LANES]
+                    out_ref[f * per_x : (f + 1) * per_x, line : line + 2, :] = value
+                line += 2
 
 
 def pick_rows_kernel(index_ref, table_ref, out_ref, sem):
@@ -77,44 +89,64 @@
     return high, low
 
 
-def product_kernel(core_ref, v_ref, hh, hl, oh, ol, out_ref, a_hi, a_lo, b_hi, b_lo):
-    nz, tl, parts, nc, _, sites = v_ref.shape
-    half = parts * nz
-    nq, nx, _, _, piece, _ = out_ref.shape
+def product_kernel(parts, core_ref, v_ref, hh, hl, oh, ol, out_ref, p_hi, p_lo, a_ref, b_ref, sem):
+    nq, nx, nsrc, tl, piece, width = out_ref.shape
+    wide = p_hi.shape[3]
+    cols = wide // LANES
+    half = a_ref.shape[1] // 4
+    nz = half // parts
     core = core_ref[0]
+
+    copies = []
+    for t in range(tl):
+        group = []
+        for i, (own, src, dst) in enumerate(
+            ((True, hh, p_hi), (False, oh, p_hi), (True, hl, p_lo), (False, ol, p_lo))
+        ):
+            first = (core if own else nsrc - 1 - core) * width
+            group.append(
+                pltpu.make_async_copy(
+                    src.at[t], dst.at[t, :, pl.ds(pl.multiple_of(first, width), width)], sem.at[t, i]
+                )
+            )
+            group[-1].start()
+        copies.append(group)
 
     def dot(left, right):
         return lax.dot_general(
             left, right, (((1,), (1,)), ((), ())), preferred_element_type=jnp.float32
         )
 
+    stride = tl * parts * cols * 2
     for t in range(tl):
         for i in range(parts):
-            for c in range(nc):
-                real_hi, real_lo = halves(v_ref[:, t, i, c, 0, :])
-                imag_hi, imag_lo = halves(v_ref[:, t, i, c, 1, :])
-                top = pl.ds(i * nz, nz)
-                low = pl.ds(half + i * nz, nz)
-                lane = pl.ds(c * sites, sites)
-                a_hi[t, top, lane] = real_hi
-                a_lo[t, top, lane] = real_lo
-                a_hi[t, low, lane] = -imag_hi
-                a_lo[t, low, lane] = -imag_lo
-                b_hi[t, top, lane] = imag_hi
-                b_lo[t, top, lane] = imag_lo
-                b_hi[t, low, lane] = real_hi
-                b_lo[t, low, lane] = real_lo
-        ah, al, bh, bl = a_hi[t], a_lo[t], b_hi[t], b_lo[t]
-        for slot, high, low in ((core, hh, hl), (1 - core, oh, ol)):
-            total = dot(ah, high[t, 0]) + dot(bh, high[t, 1])
-            total += dot(ah, low[t, 0]) + dot(bh, low[t, 1])
-            total += dot(al, high[t, 0]) + dot(bl, high[t, 1])
-            per = half // nx
-            for q in range(nq):
-                ri, part = divmod(q, nq // 2)
-                for x in range(nx):
-                    first = ri * half + x * per + part * piece
-                    out_ref[q, x, slot, t] = total[first : first + piece]
+            for b in range(cols):
+                start = ((t * parts + i) * cols + b) * 2
+                real_hi, real_lo = halves(v_ref[pl.ds(start, nz, stride=stride), :])
+                imag_hi, imag_lo = halves(v_ref[pl.ds(start + 1, nz, stride=stride), :])
+                lane = pl.ds(b * LANES, LANES)
+                for j, (real, imag) in enumerate(((real_hi, imag_hi), (real_lo, imag_lo))):
+                    top = pl.ds(2 * j * half + i * nz, nz)
+                    low = pl.ds((2 * j + 1) * half + i * nz, nz)
+                    a_ref[t, top, lane] = real
+                    a_ref[t, low, lane] = -imag
+                    b_ref[t, top, lane] = imag
+                    b_ref[t, low, lane] = real
+    per = half // nx
+    for t in range(tl):
+        for copy in copies[t]:
+            copy.wait()
+        both = dot(a_ref[t], p_hi[t, 0]) + dot(b_ref[t], p_hi[t, 1])
+        total = both[: 2 * half] + both[2 * half :]
+        total += dot(a_ref[t, : 2 * half], p_lo[t, 0]) + dot(b_ref[t, : 2 * half], p_lo[t, 1])
+        for q in range(nq):
+            ri, part = divmod(q, nq // 2)
+            for x in range(nx):
+                first = ri * half + x * per + part * piece
+                for slot in range(nsrc):
+                    out_ref[q, x, slot, t] = total[
+                        first : first + piece, slot * width : (slot + 1) * width
+                    ]
 
 
 def sum_kernel(index_ref, in_ref, out_ref, held):
@@ -163,25 +195,28 @@
     ordering = inverse_of(rank)
 
     tail = (nc, 2, sites)
+    lines = part * nc * 2 * sites // LANES
     share = pl.pallas_call(
         share_kernel,
-        out_shape=jax.ShapeDtypeStruct((fold, per_x, rows, part, *tail), jnp.float32),
-        in_specs=[
-            pl.BlockSpec(memory_space=pltpu.SMEM),
-            pl.BlockSpec(memory_space=pl.ANY),
+        out_shape=jax.ShapeDtypeStruct((nta, lines * rows, LANES), jnp.float32),
+        in_specs=[
+            pl.BlockSpec(memory_space=pltpu.SMEM),
+            pl.BlockSpec(memory_space=pltpu.HBM),
         ],
         out_specs=pl.BlockSpec(memory_space=pltpu.VMEM),
-        scratch_shapes=[pltpu.SemaphoreType.DMA((rows * part,))],
-        compiler_params=small(4),
+        scratch_shapes=[
+            pltpu.VMEM((rows * part, fold, per_x, *tail), jnp.float32),
+            pltpu.SemaphoreType.DMA((rows * part,)),
+        ],
         name="share",
     )(
         core[None],
         eigvecs.transpose(0, 1, 3, 2, 4).reshape(rows, part, fold, nsrc, per_x, *tail),
     )
-    share = share.reshape(nta, rows, part, *tail)
     spread = lax.all_to_all(share, TA, 0, 0, tiled=True)
-    picked = pick_rows(spread.reshape(nta * rows, part, *tail), rank)
-    sent = lax.all_to_all(picked.reshape(nta, tl, part, *tail), TA, 0, 0, tiled=True)
+    picked = pick_rows(spread.reshape(nta * rows, lines, LANES), rank)
+    sent = lax.all_to_all(picked.reshape(nta, tl * lines, LANES), TA, 0, 0, tiled=True)
+    sent = sent.reshape(nta * tl * lines, LANES)
 
     inverse = inverse_of(source_ids - n * core)
     held = spinors.at[inverse].get(mode="promise_in_bounds")
@@ -197,13 +232,17 @@
 
     piece = 2 * per_x // near
     pair = pl.pallas_call(
-        product_kernel,
+        functools.partial(product_kernel, part),
         out_shape=jax.ShapeDtypeStruct((near, nx, nsrc, tl, piece, ns * n), jnp.float32),
-        in_specs=[pl.BlockSpec(memory_space=pltpu.SMEM)]
-        + [pl.BlockSpec(memory_space=pltpu.VMEM)] * 5,
+        in_specs=[
+            pl.BlockSpec(memory_space=pltpu.SMEM),
+            pl.BlockSpec(memory_space=pltpu.VMEM),
+        ]
+        + [pl.BlockSpec(memory_space=pltpu.HBM)] * 4,
         out_specs=pl.BlockSpec(memory_space=pltpu.VMEM),
-        scratch_shapes=[pltpu.VMEM((tl, 2 * mine, nc * sites), jnp.bfloat16)] * 4,
-        compiler_params=small(16),
+        scratch_shapes=[pltpu.VMEM((tl, 2, nsrc * ns * n, nc * sites), jnp.bfloat16)] * 2
+        + [pltpu.VMEM((tl, 4 * mine, nc * sites), jnp.bfloat16)] * 2
+        + [pltpu.SemaphoreType.DMA((tl, 4))],
         name="product",
     )(core[None], sent, held_hi, held_lo, other_hi, other_lo)
 

time: 191 us -> 188 us (0.984)
  local copies, waits for them, and re-layouts: 14.7 us -> 6.37 us
  waiting for transfers between devices: 87.6 us -> 92.2 us
    unnamed x14 -> x6, local copies, waits for them, and re-layouts: 4.94 us -> 0.01 us
    all_to_all x1, waiting for transfers between devices: 22.1 us -> 25.8 us  [local(): lax.all_to_all(picked.reshape(nta, tl * lines, LANES), TA, 0, 0, tiled=True)]
    pallas_call x2, Pallas kernels: 5.6 us -> 7.52 us  [the longest x1 5.2 us: local(): pl.pallas_call(functools.partial(product_kernel, part), out_shape=jax.Sha...]
  transfers between devices with their start and end apart: 5 -> 5, of which waited for: 5 -> 5; matrix products, arithmetic and copies ran while one was open for 7% -> 5% of each run, Pallas kernels for 0% -> 0%
where the time goes in v4:
time: 188 us; the launch traced here: 187 us
  waiting for transfers between devices  92.2 us (49%)
  starting transfers between devices  73.4 us (39%)
  Pallas kernels  11.9 us (6%)
  local copies, waits for them, and re-layouts  6.37 us (3%)
  other arithmetic  3.19 us (2%)
    all_to_all x1, starting transfers between devices, local(): spread = lax.all_to_all(share, TA, 0, 0, tiled=True)  43.7 us
    all_to_all x1, waiting for transfers between devices, local(): spread = lax.all_to_all(share, TA, 0, 0, tiled=True)  38.7 us
    all_to_all x1, waiting for transfers between devices, local(): lax.all_to_all(picked.reshape(nta, tl * lines, LANES), TA, 0, 0, tiled=True)  25.8 us
    all_to_all x1, waiting for transfers between devices, local(): lax.all_to_all(back.reshape(nta, rows, nsrc, piece, ns * n), TA, 0, 0, ti...  14.5 us
    all_to_all x1, starting transfers between devices, local(): got = lax.all_to_all(pair, ('tp', 'xyz', 'src'), 0, 0, tiled=True)  12.9 us
    all_to_all x1, waiting for transfers between devices, local(): got = lax.all_to_all(pair, ('tp', 'xyz', 'src'), 0, 0, tiled=True)  11.2 us
    all_to_all x1, starting transfers between devices, local(): lax.all_to_all(picked.reshape(nta, tl * lines, LANES), TA, 0, 0, tiled=True)  7.83 us
    all_to_all x1, starting transfers between devices, local(): lax.all_to_all(back.reshape(nta, rows, nsrc, piece, ns * n), TA, 0, 0, ti...  7.05 us
  transfers between devices with their start and end apart: 5, of which 5 were waited for; matrix products, arithmetic and copies ran while one was open for 5% of the time, Pallas kernels for 0%

profile of v4, /device:TPU:80, one launch (start us, length us, event | category | flops | bytes accessed | tf_op | source)
XLA Modules:
  0.0 187.2 jit_solution(8559228961028098954)
XLA Ops:
  0.0 0.0 copy-start
  0.0 0.0 copy-start.1
  0.0 2.3 %share.1 = f32[16,96,128]{2,1,0:T(8,128)} custom-call(s32[1]{0:T(128)} %bitcast.core_ref, f32[2,4,2,2,8,3,2,256]{7,6,5,4,3,2,1,0:T(2,128)} %bitcast.21), custom_call_target="tpu_custom_call" | custom-call | tf_op jit(solution)/shard_map/share/pallas_call | solution.py:199
  2.3 43.7 %all-to-all-start = ((f32[16,96,128]{2,1,0:T(8,128)}), f32[16,96,128]{2,1,0:T(8,128)S(1)}, u32[]{:S(2)}, u32[]{:S(2)}) async-start(f32[16,96,128]{2,1,0:T(8,128)} %share.1), calls=%async_computation | async-start | bytes 1572864 | tf_op jit(solution)/shard_map/all_to_all | solution.py:216
  46.0 0.0 copy-done.1
  46.0 0.2 convert_reduce_fusion.index_ref
  46.2 38.7 %all-to-all-done = f32[16,96,128]{2,1,0:T(8,128)S(1)} async-done(((f32[16,96,128]{2,1,0:T(8,128)}), f32[16,96,128]{2,1,0:T(8,128)S(1)}, u32[]{:S(2)}, u32[]{:S(2)}) %all-to-all-start) | async-done | bytes 786464 | tf_op jit(solution)/shard_map/all_to_all | solution.py:216
  84.9 0.0 copy-start.2
  84.9 1.7 pick_rows.1
  86.7 7.8 %all-to-all-start.1 = ((f32[16,96,128]{2,1,0:T(8,128)}), f32[16,96,128]{2,1,0:T(8,128)}, u32[]{:S(2)}, u32[]{:S(2)}) async-start(f32[16,96,128]{2,1,0:T(8,128)} %bitcast.4), calls=%async_computation.1 | async-start | bytes 1572864 | tf_op jit(solution)/shard_map/all_to_all | solution.py:218
  94.5 0.0 copy-done.2
  94.5 0.1 select_reduce_fusion
  94.7 0.0 copy-done
  94.7 1.5 gather_fusion
  96.2 1.9 %copy.7 = f32[2,2,4,32,3,256]{5,4,3,2,1,0:T(4,128)} copy(f32[2,2,4,32,3,256]{5,2,4,1,0,3:T(4,128)S(1)} %bitcast.20) | data formatting | bytes 3145728 | tf_op jit(solution)/shard_map/transpose | solution.py:223
  98.1 2.9 %reshape.48 = f32[2,2,128,768]{3,2,1,0:T(8,128)S(1)} reshape(f32[2,2,4,32,3,256]{5,4,3,2,1,0:T(4,128)} %copy.7) | data formatting | bytes 3145728 | tf_op jit(solution)/shard_map/reshape | solution.py:223
  101.0 2.0 %collective-permute-start = (f32[2,2,128,768]{3,2,1,0:T(8,128)S(1)}, f32[2,2,128,768]{3,2,1,0:T(8,128)S(1)}, u32[]{:S(2)}, u32[]{:S(2)}) collective-permute-start(f32[2,2,128,768]{3,2,1,0:T(8,128)S(1)} %reshape.48), channel_id=1, source_target_pairs={{0,1},{1,0},{2,3},{3,2},{4,5},{5,4},{6,7},{7,6},{8,9},{9,8},{10,11... | collective-permute-start | bytes 4718600 | tf_op jit(solution)/shard_map/ppermute | solution.py:224
  102.9 1.4 fusion
  104.3 2.0 %collective-permute-done = f32[2,2,128,768]{3,2,1,0:T(8,128)S(1)} collective-permute-done((f32[2,2,128,768]{3,2,1,0:T(8,128)S(1)}, f32[2,2,128,768]{3,2,1,0:T(8,128)S(1)}, u32[]{:S(2)}, u32[]{:S(2)}) %collective-permute-start) | collective-permute-done | bytes 1572896 | tf_op jit(solution)/shard_map/ppermute | solution.py:224
  106.3 1.4 fusion.1
  107.7 25.8 %all-to-all-done.1 = f32[16,96,128]{2,1,0:T(8,128)} async-done(((f32[16,96,128]{2,1,0:T(8,128)}), f32[16,96,128]{2,1,0:T(8,128)}, u32[]{:S(2)}, u32[]{:S(2)}) %all-to-all-start.1) | async-done | bytes 786464 | tf_op jit(solution)/shard_map/all_to_all | solution.py:218
  133.5 5.2 %product.1 = f32[4,8,2,2,4,128]{5,4,3,2,1,0:T(4,128)} custom-call(s32[1]{0:T(128)} %bitcast.core_ref, f32[1536,128]{1,0:T(8,128)} %bitcast.5.v_ref, bf16[2,2,128,768]{3,2,1,0:T(8,128)(2,1)} %get-tuple-element.8.hh, bf16[2,2,128,768]{3,2,1,0:T(8,128)(2,1)} %get-tuple-element.7.hl, bf16[2,2,128,768]{3,2,1,0:T(8,128)(2,1)} %get-tuple-element.6.oh, ...), custom_call_target="tpu_custom_call" | custom-call | tf_op jit(solution)/shard_map/product/pallas_call | solution.py:234
  138.7 12.9 %all-to-all-start.2 = ((f32[64,2,4,128]{3,2,1,0:T(4,128)}), f32[64,2,4,128]{3,2,1,0:T(4,128)S(1)}, u32[]{:S(2)}, u32[]{:S(2)}) async-start(f32[64,2,4,128]{3,2,1,0:T(4,128)} %bitcast.22), calls=%async_computation.2 | async-start | bytes 524288 | tf_op jit(solution)/shard_map/all_to_all | solution.py:250
  151.6 0.1 select_reduce_fusion.1
  151.7 11.2 %all-to-all-done.2 = f32[64,2,4,128]{3,2,1,0:T(4,128)S(1)} async-done(((f32[64,2,4,128]{3,2,1,0:T(4,128)}), f32[64,2,4,128]{3,2,1,0:T(4,128)S(1)}, u32[]{:S(2)}, u32[]{:S(2)}) %all-to-all-start.2) | async-done | bytes 262176 | tf_op jit(solution)/shard_map/all_to_all | solution.py:250
  162.9 1.2 sum_over_xyz.1
  164.1 7.1 %all-to-all-start.3 = ((f32[16,2,2,4,128]{4,3,2,1,0:T(4,128)}), f32[16,2,2,4,128]{4,3,2,1,0:T(4,128)S(1)}, u32[]{:S(2)}, u32[]{:S(2)}) async-start(f32[16,2,2,4,128]{4,3,2,1,0:T(4,128)} %bitcast.11), calls=%async_computation.3 | async-start | bytes 262144 | tf_op jit(solution)/shard_map/all_to_all | solution.py:265
  171.2 0.1 dynamic_slice.3.order_ref
  171.3 14.5 %all-to-all-done.3 = f32[16,2,2,4,128]{4,3,2,1,0:T(4,128)S(1)} async-done(((f32[16,2,2,4,128]{4,3,2,1,0:T(4,128)}), f32[16,2,2,4,128]{4,3,2,1,0:T(4,128)S(1)}, u32[]{:S(2)}, u32[]{:S(2)}) %all-to-all-start.3) | async-done | bytes 131104 | tf_op jit(solution)/shard_map/all_to_all | solution.py:265
  185.8 1.5 final.1
  (4 shorter events, 0.0 us)
Async XLA Ops:
  0.0 94.7 %copy-start = (f32[32,2,2,4,3,256]{5,3,4,2,1,0:T(4,128)S(1)}, f32[32,2,2,4,3,256]{5,3,4,2,1,0:T(4,128)}, u32[]{:S(2)}) copy-start(f32[32,2,2,4,3,256]{5,3,4,2,1,0:T(4,128)} %param.4) | copy-start | bytes 4718596
  0.0 46.0 %copy-start.1 = (s32[32]{0:T(128)S(1)}, s32[32]{0:T(128)}, u32[]{:S(2)}) copy-start(s32[32]{0:T(128)} %param.6) | copy-start | bytes 388
  2.3 82.6 %all-to-all-start = ((f32[16,96,128]{2,1,0:T(8,128)}), f32[16,96,128]{2,1,0:T(8,128)S(1)}, u32[]{:S(2)}, u32[]{:S(2)}) async-start(f32[16,96,128]{2,1,0:T(8,128)} %share.1), calls=%async_computation | async-start | bytes 1572864 | tf_op jit(solution)/shard_map/all_to_all | solution.py:216
  84.9 9.6 %copy-start.2 = (s32[32]{0:T(128)S(1)}, s32[32]{0:T(128)}, u32[]{:S(2)}) copy-start(s32[32]{0:T(128)} %param.7) | copy-start | bytes 388
  86.7 46.8 %all-to-all-start.1 = ((f32[16,96,128]{2,1,0:T(8,128)}), f32[16,96,128]{2,1,0:T(8,128)}, u32[]{:S(2)}, u32[]{:S(2)}) async-start(f32[16,96,128]{2,1,0:T(8,128)} %bitcast.4), calls=%async_computation.1 | async-start | bytes 1572864 | tf_op jit(solution)/shard_map/all_to_all | solution.py:218
  101.0 5.3 %collective-permute-start = (f32[2,2,128,768]{3,2,1,0:T(8,128)S(1)}, f32[2,2,128,768]{3,2,1,0:T(8,128)S(1)}, u32[]{:S(2)}, u32[]{:S(2)}) collective-permute-start(f32[2,2,128,768]{3,2,1,0:T(8,128)S(1)} %reshape.48), channel_id=1, source_target_pairs={{0,1},{1,0},{2,3},{3,2},{4,5},{5,4},{6,7},{7,6},{8,9},{9,8},{10,11... | collective-permute-start | bytes 4718600 | tf_op jit(solution)/shard_map/ppermute | solution.py:224
  138.7 24.2 %all-to-all-start.2 = ((f32[64,2,4,128]{3,2,1,0:T(4,128)}), f32[64,2,4,128]{3,2,1,0:T(4,128)S(1)}, u32[]{:S(2)}, u32[]{:S(2)}) async-start(f32[64,2,4,128]{3,2,1,0:T(4,128)} %bitcast.22), calls=%async_computation.2 | async-start | bytes 524288 | tf_op jit(solution)/shard_map/all_to_all | solution.py:250
  164.1 21.6 %all-to-all-start.3 = ((f32[16,2,2,4,128]{4,3,2,1,0:T(4,128)}), f32[16,2,2,4,128]{4,3,2,1,0:T(4,128)S(1)}, u32[]{:S(2)}, u32[]{:S(2)}) async-start(f32[16,2,2,4,128]{4,3,2,1,0:T(4,128)} %bitcast.11), calls=%async_computation.3 | async-start | bytes 262144 | tf_op jit(solution)/shard_map/all_to_all | solution.py:265

commit v5 on v4

--- a/solution.py
+++ b/solution.py
@@ -32,7 +32,7 @@
     return pltpu.CompilerParams(vmem_limit_bytes=mib << 20)
 
 
-def share_kernel(core_ref, in_ref, out_ref, held, sem):
+def share_kernel(core_ref, in_ref, out_ref, held, packed, sem, out_sem):
     rows, parts, folds, _, per_x, nc, _, sites = in_ref.shape
     core = core_ref[0]
     copies = [
@@ -44,15 +44,26 @@
     ]
     for copy in copies:
         copy.start()
-    for p, copy in enumerate(copies):
-        copy.wait()
-        line = p * nc * 2 * (sites // LANES)
-        for c in range(nc):
-            for lane in range(0, sites, LANES):
-                for f in range(folds):
-                    value = held[p, f, :, c, :, lane : lane + LANES]
-                    out_ref[f * per_x : (f + 1) * per_x, line : line + 2, :] = value
-                line += 2
+    lines = out_ref.shape[1] // rows
+    sends = []
+    for r in range(rows):
+        line = r * lines
+        for i in range(parts):
+            p = r * parts + i
+            copies[p].wait()
+            for c in range(nc):
+                for lane in range(0, sites, LANES):
+                    for f in range(folds):
+                        value = held[p, f, :, c, :, lane : lane + LANES]
+                        packed[f * per_x : (f + 1) * per_x, line : line + 2, :] = value
+                    line += 2
+        span = pl.ds(r * lines, lines)
+        sends.append(
+            pltpu.make_async_copy(packed.at[:, span], out_ref.at[:, span], out_sem.at[r])
+        )
+        sends[-1].start()
+    for send in sends:
+        send.wait()
 
 
 def pick_rows_kernel(index_ref, table_ref, out_ref, sem):
@@ -89,7 +100,9 @@
     return high, low
 
 
-def product_kernel(parts, core_ref, v_ref, hh, hl, oh, ol, out_ref, p_hi, p_lo, a_ref, b_ref, sem):
+def product_kernel(
+    parts, core_ref, v_in, hh, hl, oh, ol, out_ref, v_ref, p_hi, p_lo, a_ref, b_ref, sem, v_sem
+):
     nq, nx, nsrc, tl, piece, width = out_ref.shape
     wide = p_hi.shape[3]
     cols = wide // LANES
@@ -97,6 +110,8 @@
     nz = half // parts
     core = core_ref[0]
 
+    v_copy = pltpu.make_async_copy(v_in, v_ref, v_sem)
+    v_copy.start()
     copies = []
     for t in range(tl):
         group = []
@@ -118,6 +133,7 @@
         )
 
     stride = tl * parts * cols * 2
+    v_copy.wait()
     for t in range(tl):
         for i in range(parts):
             for b in range(cols):
@@ -151,6 +167,7 @@
 
 def sum_kernel(index_ref, in_ref, out_ref, held):
     near, nx, nsrc, tl = in_ref.shape[:4]
+    nta, _, rows = out_ref.shape[:3]
     for z in range(near):
         total = in_ref[z, 0]
         for x in range(1, nx):
@@ -158,21 +175,28 @@
         for t in range(tl):
             for core in range(nsrc):
                 held[z * tl + t, core] = total[core, t]
-    for row in range(out_ref.shape[0]):
-        out_ref[row] = held[index_ref[row]]
-
-
-def final_kernel(order_ref, in_ref, out_ref):
-    nq, nsrc, piece = in_ref.shape[1], in_ref.shape[3], in_ref.shape[4]
+    for ta in range(nta):
+        for row in range(rows):
+            value = held[index_ref[ta * rows + row]]
+            for core in range(nsrc):
+                out_ref[ta, core, row] = value[core]
+
+
+def final_kernel(per_group, order_ref, in_ref, out_ref):
+    _, nq, nsrc, rows, piece, _ = in_ref.shape
     ns, n = out_ref.shape[2], out_ref.shape[4]
     parts = nq // 2
-    for core in range(nsrc):
-        for ri in range(2):
-            for part in range(parts):
-                value = in_ref[0, ri * parts + part, 0, core]
-                first = (core * parts + part) * piece
-                for s in range(ns):
-                    out_ref[0, ri, s, first : first + piece, :] = value[:, s * n : (s + 1) * n]
+    for row in range(rows):
+        group = order_ref[row] // per_group
+        for core in range(nsrc):
+            for ri in range(2):
+                for part in range(parts):
+                    value = in_ref[group, ri * parts + part, core, row]
+                    first = (core * parts + part) * piece
+                    for s in range(ns):
+                        out_ref[row, ri, s, first : first + piece, :] = value[
+                            :, s * n : (s + 1) * n
+                        ]
 
 
 TA = ("tq", "tp")
@@ -203,10 +227,12 @@
             pl.BlockSpec(memory_space=pltpu.SMEM),
             pl.BlockSpec(memory_space=pltpu.HBM),
         ],
-        out_specs=pl.BlockSpec(memory_space=pltpu.VMEM),
+        out_specs=pl.BlockSpec(memory_space=pltpu.HBM),
         scratch_shapes=[
             pltpu.VMEM((rows * part, fold, per_x, *tail), jnp.float32),
+            pltpu.VMEM((nta, lines * rows, LANES), jnp.float32),
             pltpu.SemaphoreType.DMA((rows * part,)),
+            pltpu.SemaphoreType.DMA((rows,)),
         ],
         name="share",
     )(
@@ -234,24 +260,22 @@
     pair = pl.pallas_call(
         functools.partial(product_kernel, part),
         out_shape=jax.ShapeDtypeStruct((near, nx, nsrc, tl, piece, ns * n), jnp.float32),
-        in_specs=[
-            pl.BlockSpec(memory_space=pltpu.SMEM),
-            pl.BlockSpec(memory_space=pltpu.VMEM),
-        ]
-        + [pl.BlockSpec(memory_space=pltpu.HBM)] * 4,
+        in_specs=[pl.BlockSpec(memory_space=pltpu.SMEM)]
+        + [pl.BlockSpec(memory_space=pltpu.HBM)] * 5,
         out_specs=pl.BlockSpec(memory_space=pltpu.VMEM),
-        scratch_shapes=[pltpu.VMEM((tl, 2, nsrc * ns * n, nc * sites), jnp.bfloat16)] * 2
+        scratch_shapes=[pltpu.VMEM(sent.shape, jnp.float32)]
+        + [pltpu.VMEM((tl, 2, nsrc * ns * n, nc * sites), jnp.bfloat16)] * 2
         + [pltpu.VMEM((tl, 4 * mine, nc * sites), jnp.bfloat16)] * 2
-        + [pltpu.SemaphoreType.DMA((tl, 4))],
+        + [pltpu.SemaphoreType.DMA((tl, 4)), pltpu.SemaphoreType.DMA],
         name="product",
     )(core[None], sent, held_hi, held_lo, other_hi, other_lo)
 
-    pair = pair.reshape(near * nx * nsrc, tl, piece, ns * n)
-    got = lax.all_to_all(pair, ("tp", "xyz", "src"), 0, 0, tiled=True)
+    pair = pair.reshape(near * nx, nsrc, tl, piece, ns * n)
+    got = lax.all_to_all(pair, ("tp", "xyz"), 0, 0, tiled=True)
     here = jnp.clip(ordering - (ta // near) * (near * tl), 0, near * tl - 1)
     back = pl.pallas_call(
         sum_kernel,
-        out_shape=jax.ShapeDtypeStruct((nta * rows, nsrc, piece, ns * n), jnp.float32),
+        out_shape=jax.ShapeDtypeStruct((nta, nsrc, rows, piece, ns * n), jnp.float32),
         in_specs=[
             pl.BlockSpec(memory_space=pltpu.SMEM),
             pl.BlockSpec(memory_space=pltpu.VMEM),
@@ -262,23 +286,18 @@
         name="sum_over_xyz",
     )(here, got.reshape(near, nx, nsrc, tl, piece, ns * n))
 
-    home = lax.all_to_all(back.reshape(nta, rows, nsrc, piece, ns * n), TA, 0, 0, tiled=True)
-    home = home.reshape(nta // near, near, rows, nsrc, piece, ns * n)
+    back = back.reshape(nta * nsrc, rows, piece, ns * n)
+    home = lax.all_to_all(back, (*TA, "src"), 0, 0, tiled=True)
+    home = home.reshape(nta // near, near, nsrc, rows, piece, ns * n)
     wanted = lax.dynamic_slice_in_dim(ordering, ta * rows, rows, 0)
     out = pl.pallas_call(
-        final_kernel,
+        functools.partial(final_kernel, near * tl),
         out_shape=jax.ShapeDtypeStruct((rows, 2, ns, nsrc * per_x, n), jnp.float32),
-        grid_spec=pltpu.PrefetchScalarGridSpec(
-            num_scalar_prefetch=1,
-            grid=(rows,),
-            in_specs=[
-                pl.BlockSpec(
-                    (1, near, 1, nsrc, piece, ns * n),
-                    lambda r, order: (order[r] // (near * tl), 0, r, 0, 0, 0),
-                )
-            ],
-            out_specs=pl.BlockSpec((1, 2, ns, nsrc * per_x, n), lambda r, order: (r, 0, 0, 0, 0)),
-        ),
+        in_specs=[
+            pl.BlockSpec(memory_space=pltpu.SMEM),
+            pl.BlockSpec(memory_space=pltpu.VMEM),
+        ],
+        out_specs=pl.BlockSpec(memory_space=pltpu.VMEM),
         compiler_params=small(4),
         name="final",
     )(wanted, home)

time: 188 us -> 189 us (level)
  no operation moved by 1% of the time
where the time goes in v5:
time: 189 us; the launch traced here: 188 us
  waiting for transfers between devices  93.5 us (49%)
  starting transfers between devices  73.1 us (39%)
  Pallas kernels  11.9 us (6%)
  local copies, waits for them, and re-layouts  6.37 us (3%)
  other arithmetic  3.19 us (2%)
    all_to_all x1, starting transfers between devices, local(): spread = lax.all_to_all(share, TA, 0, 0, tiled=True)  43.7 us
    all_to_all x1, waiting for transfers between devices, local(): spread = lax.all_to_all(share, TA, 0, 0, tiled=True)  38.7 us
    all_to_all x1, waiting for transfers between devices, local(): lax.all_to_all(picked.reshape(nta, tl * lines, LANES), TA, 0, 0, tiled=True)  25.8 us
    all_to_all x1, waiting for transfers between devices, local(): home = lax.all_to_all(back, (*TA, 'src'), 0, 0, tiled=True)  16.4 us
    all_to_all x1, starting transfers between devices, local(): got = lax.all_to_all(pair, ('tp', 'xyz'), 0, 0, tiled=True)  11.3 us
    all_to_all x1, waiting for transfers between devices, local(): got = lax.all_to_all(pair, ('tp', 'xyz'), 0, 0, tiled=True)  10.5 us
    all_to_all x1, starting transfers between devices, local(): home = lax.all_to_all(back, (*TA, 'src'), 0, 0, tiled=True)  8.37 us
    all_to_all x1, starting transfers between devices, local(): lax.all_to_all(picked.reshape(nta, tl * lines, LANES), TA, 0, 0, tiled=True)  7.83 us
  transfers between devices with their start and end apart: 5, of which 5 were waited for; matrix products, arithmetic and copies ran while one was open for 5% of the time, Pallas kernels for 0%

profile of v5, /device:TPU:80, one launch (start us, length us, event | category | flops | bytes accessed | tf_op | source)
XLA Modules:
  0.0 188.2 jit_solution(845564853393914219)
XLA Ops:
  0.0 0.0 copy-start
  0.0 0.0 copy-start.1
  0.0 2.3 %share.1 = f32[16,96,128]{2,1,0:T(8,128)} custom-call(s32[1]{0:T(128)} %bitcast.core_ref, f32[2,4,2,2,8,3,2,256]{7,6,5,4,3,2,1,0:T(2,128)} %bitcast.21), custom_call_target="tpu_custom_call" | custom-call | tf_op jit(solution)/shard_map/share/pallas_call | solution.py:223
  2.3 43.7 %all-to-all-start = ((f32[16,96,128]{2,1,0:T(8,128)}), f32[16,96,128]{2,1,0:T(8,128)S(1)}, u32[]{:S(2)}, u32[]{:S(2)}) async-start(f32[16,96,128]{2,1,0:T(8,128)} %share.1), calls=%async_computation | async-start | bytes 1572864 | tf_op jit(solution)/shard_map/all_to_all | solution.py:242
  46.0 0.0 copy-done.1
  46.0 0.2 convert_reduce_fusion.index_ref
  46.2 38.7 %all-to-all-done = f32[16,96,128]{2,1,0:T(8,128)S(1)} async-done(((f32[16,96,128]{2,1,0:T(8,128)}), f32[16,96,128]{2,1,0:T(8,128)S(1)}, u32[]{:S(2)}, u32[]{:S(2)}) %all-to-all-start) | async-done | bytes 786464 | tf_op jit(solution)/shard_map/all_to_all | solution.py:242
  84.9 0.0 copy-start.2
  84.9 1.7 pick_rows.1
  86.6 7.8 %all-to-all-start.1 = ((f32[16,96,128]{2,1,0:T(8,128)}), f32[16,96,128]{2,1,0:T(8,128)}, u32[]{:S(2)}, u32[]{:S(2)}) async-start(f32[16,96,128]{2,1,0:T(8,128)} %bitcast.4), calls=%async_computation.1 | async-start | bytes 1572864 | tf_op jit(solution)/shard_map/all_to_all | solution.py:244
  94.4 0.0 copy-done.2
  94.5 0.1 select_reduce_fusion
  94.6 0.0 copy-done
  94.6 1.5 gather_fusion
  96.1 1.9 %copy.7 = f32[2,2,4,32,3,256]{5,4,3,2,1,0:T(4,128)} copy(f32[2,2,4,32,3,256]{5,2,4,1,0,3:T(4,128)S(1)} %bitcast.20) | data formatting | bytes 3145728 | tf_op jit(solution)/shard_map/transpose | solution.py:249
  98.0 2.9 %reshape.48 = f32[2,2,128,768]{3,2,1,0:T(8,128)S(1)} reshape(f32[2,2,4,32,3,256]{5,4,3,2,1,0:T(4,128)} %copy.7) | data formatting | bytes 3145728 | tf_op jit(solution)/shard_map/reshape | solution.py:249
  100.9 2.0 %collective-permute-start = (f32[2,2,128,768]{3,2,1,0:T(8,128)S(1)}, f32[2,2,128,768]{3,2,1,0:T(8,128)S(1)}, u32[]{:S(2)}, u32[]{:S(2)}) collective-permute-start(f32[2,2,128,768]{3,2,1,0:T(8,128)S(1)} %reshape.48), channel_id=1, source_target_pairs={{0,1},{1,0},{2,3},{3,2},{4,5},{5,4},{6,7},{7,6},{8,9},{9,8},{10,11... | collective-permute-start | bytes 4718600 | tf_op jit(solution)/shard_map/ppermute | solution.py:250
  102.9 1.4 fusion
  104.2 2.0 %collective-permute-done = f32[2,2,128,768]{3,2,1,0:T(8,128)S(1)} collective-permute-done((f32[2,2,128,768]{3,2,1,0:T(8,128)S(1)}, f32[2,2,128,768]{3,2,1,0:T(8,128)S(1)}, u32[]{:S(2)}, u32[]{:S(2)}) %collective-permute-start) | collective-permute-done | bytes 1572896 | tf_op jit(solution)/shard_map/ppermute | solution.py:250
  106.2 1.4 fusion.1
  107.6 25.8 %all-to-all-done.1 = f32[16,96,128]{2,1,0:T(8,128)} async-done(((f32[16,96,128]{2,1,0:T(8,128)}), f32[16,96,128]{2,1,0:T(8,128)}, u32[]{:S(2)}, u32[]{:S(2)}) %all-to-all-start.1) | async-done | bytes 786464 | tf_op jit(solution)/shard_map/all_to_all | solution.py:244
  133.4 5.3 %product.1 = f32[4,8,2,2,4,128]{5,4,3,2,1,0:T(4,128)} custom-call(s32[1]{0:T(128)} %bitcast.core_ref, f32[1536,128]{1,0:T(8,128)} %bitcast.5.v_in, bf16[2,2,128,768]{3,2,1,0:T(8,128)(2,1)} %get-tuple-element.8.hh, bf16[2,2,128,768]{3,2,1,0:T(8,128)(2,1)} %get-tuple-element.7.hl, bf16[2,2,128,768]{3,2,1,0:T(8,128)(2,1)} %get-tuple-element.6.oh, ...), custom_call_target="tpu_custom_call" | custom-call | tf_op jit(solution)/shard_map/product/pallas_call | solution.py:260
  138.7 11.3 %all-to-all-start.2 = ((f32[32,2,2,4,128]{4,3,2,1,0:T(4,128)}), f32[32,2,2,4,128]{4,3,2,1,0:T(4,128)S(1)}, u32[]{:S(2)}, u32[]{:S(2)}) async-start(f32[32,2,2,4,128]{4,3,2,1,0:T(4,128)} %bitcast.22), calls=%async_computation.2 | async-start | bytes 524288 | tf_op jit(solution)/shard_map/all_to_all | solution.py:274
  150.0 0.1 select_reduce_fusion.1
  150.2 10.5 %all-to-all-done.2 = f32[32,2,2,4,128]{4,3,2,1,0:T(4,128)S(1)} async-done(((f32[32,2,2,4,128]{4,3,2,1,0:T(4,128)}), f32[32,2,2,4,128]{4,3,2,1,0:T(4,128)S(1)}, u32[]{:S(2)}, u32[]{:S(2)}) %all-to-all-start.2) | async-done | bytes 262176 | tf_op jit(solution)/shard_map/all_to_all | solution.py:274
  160.7 1.3 sum_over_xyz.1
  162.0 8.4 %all-to-all-start.3 = ((f32[32,2,4,128]{3,2,1,0:T(4,128)}), f32[32,2,4,128]{3,2,1,0:T(4,128)S(1)}, u32[]{:S(2)}, u32[]{:S(2)}) async-start(f32[32,2,4,128]{3,2,1,0:T(4,128)} %bitcast.11), calls=%async_computation.3 | async-start | bytes 262144 | tf_op jit(solution)/shard_map/all_to_all | solution.py:290
  170.3 0.1 dynamic_slice.3.order_ref
  170.4 16.4 %all-to-all-done.3 = f32[32,2,4,128]{3,2,1,0:T(4,128)S(1)} async-done(((f32[32,2,4,128]{3,2,1,0:T(4,128)}), f32[32,2,4,128]{3,2,1,0:T(4,128)S(1)}, u32[]{:S(2)}, u32[]{:S(2)}) %all-to-all-start.3) | async-done | bytes 131104 | tf_op jit(solution)/shard_map/all_to_all | solution.py:290
  186.8 1.3 final.1
  (4 shorter events, 0.0 us)
Async XLA Ops:
  0.0 94.6 %copy-start = (f32[32,2,2,4,3,256]{5,3,4,2,1,0:T(4,128)S(1)}, f32[32,2,2,4,3,256]{5,3,4,2,1,0:T(4,128)}, u32[]{:S(2)}) copy-start(f32[32,2,2,4,3,256]{5,3,4,2,1,0:T(4,128)} %param.4) | copy-start | bytes 4718596
  0.0 46.0 %copy-start.1 = (s32[32]{0:T(128)S(1)}, s32[32]{0:T(128)}, u32[]{:S(2)}) copy-start(s32[32]{0:T(128)} %param.6) | copy-start | bytes 388
  2.3 82.6 %all-to-all-start = ((f32[16,96,128]{2,1,0:T(8,128)}), f32[16,96,128]{2,1,0:T(8,128)S(1)}, u32[]{:S(2)}, u32[]{:S(2)}) async-start(f32[16,96,128]{2,1,0:T(8,128)} %share.1), calls=%async_computation | async-start | bytes 1572864 | tf_op jit(solution)/shard_map/all_to_all | solution.py:242
  84.9 9.6 %copy-start.2 = (s32[32]{0:T(128)S(1)}, s32[32]{0:T(128)}, u32[]{:S(2)}) copy-start(s32[32]{0:T(128)} %param.7) | copy-start | bytes 388
  86.6 46.8 %all-to-all-start.1 = ((f32[16,96,128]{2,1,0:T(8,128)}), f32[16,96,128]{2,1,0:T(8,128)}, u32[]{:S(2)}, u32[]{:S(2)}) async-start(f32[16,96,128]{2,1,0:T(8,128)} %bitcast.4), calls=%async_computation.1 | async-start | bytes 1572864 | tf_op jit(solution)/shard_map/all_to_all | solution.py:244
  100.9 5.3 %collective-permute-start = (f32[2,2,128,768]{3,2,1,0:T(8,128)S(1)}, f32[2,2,128,768]{3,2,1,0:T(8,128)S(1)}, u32[]{:S(2)}, u32[]{:S(2)}) collective-permute-start(f32[2,2,128,768]{3,2,1,0:T(8,128)S(1)} %reshape.48), channel_id=1, source_target_pairs={{0,1},{1,0},{2,3},{3,2},{4,5},{5,4},{6,7},{7,6},{8,9},{9,8},{10,11... | collective-permute-start | bytes 4718600 | tf_op jit(solution)/shard_map/ppermute | solution.py:250
  138.7 22.0 %all-to-all-start.2 = ((f32[32,2,2,4,128]{4,3,2,1,0:T(4,128)}), f32[32,2,2,4,128]{4,3,2,1,0:T(4,128)S(1)}, u32[]{:S(2)}, u32[]{:S(2)}) async-start(f32[32,2,2,4,128]{4,3,2,1,0:T(4,128)} %bitcast.22), calls=%async_computation.2 | async-start | bytes 524288 | tf_op jit(solution)/shard_map/all_to_all | solution.py:274
  162.0 24.9 %all-to-all-start.3 = ((f32[32,2,4,128]{3,2,1,0:T(4,128)}), f32[32,2,4,128]{3,2,1,0:T(4,128)S(1)}, u32[]{:S(2)}, u32[]{:S(2)}) async-start(f32[32,2,4,128]{3,2,1,0:T(4,128)} %bitcast.11), calls=%async_computation.3 | async-start | bytes 262144 | tf_op jit(solution)/shard_map/all_to_all | solution.py:290

commit v6 on v5

--- a/solution.py
+++ b/solution.py
@@ -101,11 +101,11 @@
 
 
 def product_kernel(
-    parts, core_ref, v_in, hh, hl, oh, ol, out_ref, v_ref, p_hi, p_lo, a_ref, b_ref, sem, v_sem
+    parts, core_ref, v_in, hh, hl, oh, ol, out_hbm,
+    v_ref, p_hi, p_lo, a_ref, b_ref, out_ref, sem, v_sem, out_sem,
 ):
-    nq, nx, nsrc, tl, piece, width = out_ref.shape
-    wide = p_hi.shape[3]
-    cols = wide // LANES
+    tl, nq, nx, nsrc, piece, width = out_ref.shape
+    cols = p_hi.shape[3] // LANES
     half = a_ref.shape[1] // 4
     nz = half // parts
     core = core_ref[0]
@@ -114,18 +114,15 @@
     v_copy.start()
     copies = []
     for t in range(tl):
-        group = []
-        for i, (own, src, dst) in enumerate(
-            ((True, hh, p_hi), (False, oh, p_hi), (True, hl, p_lo), (False, ol, p_lo))
-        ):
-            first = (core if own else nsrc - 1 - core) * width
-            group.append(
-                pltpu.make_async_copy(
-                    src.at[t], dst.at[t, :, pl.ds(pl.multiple_of(first, width), width)], sem.at[t, i]
+        for own, other, dst in ((hh, oh, p_hi), (hl, ol, p_lo)):
+            pair = []
+            for i, (src, slot) in enumerate(((own, core), (other, nsrc - 1 - core))):
+                span = pl.ds(pl.multiple_of(slot * width, width), width)
+                pair.append(
+                    pltpu.make_async_copy(src.at[t], dst.at[t, :, span], sem.at[len(copies), i])
                 )
-            )
-            group[-1].start()
-        copies.append(group)
+                pair[-1].start()
+            copies.append(pair)
 
     def dot(left, right):
         return lax.dot_general(
@@ -133,6 +130,8 @@
         )
 
     stride = tl * parts * cols * 2
+    per = half // nx
+    sends = []
     v_copy.wait()
     for t in range(tl):
         for i in range(parts):
@@ -148,11 +147,12 @@
                     a_ref[t, low, lane] = -imag
                     b_ref[t, top, lane] = imag
                     b_ref[t, low, lane] = real
-    per = half // nx
     for t in range(tl):
-        for copy in copies[t]:
+        for copy in copies[2 * t]:
             copy.wait()
         both = dot(a_ref[t], p_hi[t, 0]) + dot(b_ref[t], p_hi[t, 1])
+        for copy in copies[2 * t + 1]:
+            copy.wait()
         total = both[: 2 * half] + both[2 * half :]
         total += dot(a_ref[t, : 2 * half], p_lo[t, 0]) + dot(b_ref[t, : 2 * half], p_lo[t, 1])
         for q in range(nq):
@@ -160,14 +160,17 @@
             for x in range(nx):
                 first = ri * half + x * per + part * piece
                 for slot in range(nsrc):
-                    out_ref[q, x, slot, t] = total[
+                    out_ref[t, q, x, slot] = total[
                         first : first + piece, slot * width : (slot + 1) * width
                     ]
+        sends.append(pltpu.make_async_copy(out_ref.at[t], out_hbm.at[:, :, :, t], out_sem.at[t]))
+        sends[-1].start()
+    for send in sends:
+        send.wait()
 
 
 def sum_kernel(index_ref, in_ref, out_ref, held):
     near, nx, nsrc, tl = in_ref.shape[:4]
-    nta, _, rows = out_ref.shape[:3]
     for z in range(near):
         total = in_ref[z, 0]
         for x in range(1, nx):
@@ -175,15 +178,12 @@
         for t in range(tl):
             for core in range(nsrc):
                 held[z * tl + t, core] = total[core, t]
-    for ta in range(nta):
-        for row in range(rows):
-            value = held[index_ref[ta * rows + row]]
-            for core in range(nsrc):
-                out_ref[ta, core, row] = value[core]
+    for row in range(out_ref.shape[0]):
+        out_ref[row] = held[index_ref[row]]
 
 
 def final_kernel(per_group, order_ref, in_ref, out_ref):
-    _, nq, nsrc, rows, piece, _ = in_ref.shape
+    _, nq, rows, nsrc, piece, _ = in_ref.shape
     ns, n = out_ref.shape[2], out_ref.shape[4]
     parts = nq // 2
     for row in range(rows):
@@ -191,7 +191,7 @@
         for core in range(nsrc):
             for ri in range(2):
                 for part in range(parts):
-                    value = in_ref[group, ri * parts + part, core, row]
+                    value = in_ref[group, ri * parts + part, row, core]
                     first = (core * parts + part) * piece
                     for s in range(ns):
                         out_ref[row, ri, s, first : first + piece, :] = value[
@@ -200,7 +200,7 @@
 
 
 TA = ("tq", "tp")
-NEAR = 4
+NEAR = 2
 
 
 def local(spinors, eigvecs, group_of, source_ids):
@@ -249,46 +249,48 @@
     held = held.transpose(1, 2, 3, 0, 4, 5).reshape(tl, 2, ns * n, nc * sites)
     other = lax.ppermute(held, "src", [(i, nsrc - 1 - i) for i in range(nsrc)])
 
+    vmem = pl.BlockSpec(memory_space=pltpu.VMEM)
+    smem = pl.BlockSpec(memory_space=pltpu.SMEM)
+    wide = nc * sites
+
     def split(x):
         high = lax.reduce_precision(x, 8, 7)
         return high.astype(jnp.bfloat16), (x - high).astype(jnp.bfloat16)
 
-    held_hi, held_lo = split(held)
-    other_hi, other_lo = split(other)
-
     piece = 2 * per_x // near
+    hbm = pl.BlockSpec(memory_space=pltpu.HBM)
     pair = pl.pallas_call(
         functools.partial(product_kernel, part),
         out_shape=jax.ShapeDtypeStruct((near, nx, nsrc, tl, piece, ns * n), jnp.float32),
-        in_specs=[pl.BlockSpec(memory_space=pltpu.SMEM)]
-        + [pl.BlockSpec(memory_space=pltpu.HBM)] * 5,
-        out_specs=pl.BlockSpec(memory_space=pltpu.VMEM),
+        in_specs=[smem] + [hbm] * 5,
+        out_specs=hbm,
         scratch_shapes=[pltpu.VMEM(sent.shape, jnp.float32)]
-        + [pltpu.VMEM((tl, 2, nsrc * ns * n, nc * sites), jnp.bfloat16)] * 2
-        + [pltpu.VMEM((tl, 4 * mine, nc * sites), jnp.bfloat16)] * 2
-        + [pltpu.SemaphoreType.DMA((tl, 4)), pltpu.SemaphoreType.DMA],
+        + [pltpu.VMEM((tl, 2, nsrc * ns * n, wide), jnp.bfloat16)] * 2
+        + [pltpu.VMEM((tl, 4 * mine, wide), jnp.bfloat16)] * 2
+        + [
+            pltpu.VMEM((tl, near, nx, nsrc, piece, ns * n), jnp.float32),
+            pltpu.SemaphoreType.DMA((2 * tl, 2)),
+            pltpu.SemaphoreType.DMA,
+            pltpu.SemaphoreType.DMA((tl,)),
+        ],
         name="product",
-    )(core[None], sent, held_hi, held_lo, other_hi, other_lo)
-
-    pair = pair.reshape(near * nx, nsrc, tl, piece, ns * n)
-    got = lax.all_to_all(pair, ("tp", "xyz"), 0, 0, tiled=True)
+    )(core[None], sent, *split(held), *split(other))
+
+    pair = pair.reshape(near * nx * nsrc, tl, piece, ns * n)
+    got = lax.all_to_all(pair, ("tp", "xyz", "src"), 0, 0, tiled=True)
     here = jnp.clip(ordering - (ta // near) * (near * tl), 0, near * tl - 1)
     back = pl.pallas_call(
         sum_kernel,
-        out_shape=jax.ShapeDtypeStruct((nta, nsrc, rows, piece, ns * n), jnp.float32),
-        in_specs=[
-            pl.BlockSpec(memory_space=pltpu.SMEM),
-            pl.BlockSpec(memory_space=pltpu.VMEM),
-        ],
-        out_specs=pl.BlockSpec(memory_space=pltpu.VMEM),
+        out_shape=jax.ShapeDtypeStruct((nta * rows, nsrc, piece, ns * n), jnp.float32),
+        in_specs=[smem, vmem],
+        out_specs=vmem,
         scratch_shapes=[pltpu.VMEM((near * tl, nsrc, piece, ns * n), jnp.float32)],
         compiler_params=small(4),
         name="sum_over_xyz",
     )(here, got.reshape(near, nx, nsrc, tl, piece, ns * n))
 
-    back = back.reshape(nta * nsrc, rows, piece, ns * n)
-    home = lax.all_to_all(back, (*TA, "src"), 0, 0, tiled=True)
-    home = home.reshape(nta // near, near, nsrc, rows, piece, ns * n)
+    home = lax.all_to_all(back.reshape(nta, rows, nsrc, piece, ns * n), TA, 0, 0, tiled=True)
+    home = home.reshape(nta // near, near, rows, nsrc, piece, ns * n)
     wanted = lax.dynamic_slice_in_dim(ordering, ta * rows, rows, 0)
     out = pl.pallas_call(
         functools.partial(final_kernel, near * tl),

time: 189 us -> 188 us (level)
  no operation moved by 1% of the time
where the time goes in v6:
time: 188 us; the launch traced here: 187 us
  waiting for transfers between devices  94.2 us (50%)
  starting transfers between devices  71.6 us (38%)
  Pallas kernels  12 us (6%)
  local copies, waits for them, and re-layouts  6.37 us (3%)
  other arithmetic  3.19 us (2%)
    all_to_all x1, starting transfers between devices, local(): spread = lax.all_to_all(share, TA, 0, 0, tiled=True)  43.7 us
    all_to_all x1, waiting for transfers between devices, local(): spread = lax.all_to_all(share, TA, 0, 0, tiled=True)  38.7 us
    all_to_all x1, waiting for transfers between devices, local(): lax.all_to_all(picked.reshape(nta, tl * lines, LANES), TA, 0, 0, tiled=True)  25.8 us
    all_to_all x1, waiting for transfers between devices, local(): lax.all_to_all(back.reshape(nta, rows, nsrc, piece, ns * n), TA, 0, 0, ti...  17.9 us
    all_to_all x1, starting transfers between devices, local(): got = lax.all_to_all(pair, ('tp', 'xyz', 'src'), 0, 0, tiled=True)  10.4 us
    all_to_all x1, waiting for transfers between devices, local(): got = lax.all_to_all(pair, ('tp', 'xyz', 'src'), 0, 0, tiled=True)  9.79 us
    all_to_all x1, starting transfers between devices, local(): lax.all_to_all(picked.reshape(nta, tl * lines, LANES), TA, 0, 0, tiled=True)  7.83 us
    all_to_all x1, starting transfers between devices, local(): lax.all_to_all(back.reshape(nta, rows, nsrc, piece, ns * n), TA, 0, 0, ti...  7.65 us
  transfers between devices with their start and end apart: 5, of which 5 were waited for; matrix products, arithmetic and copies ran while one was open for 5% of the time, Pallas kernels for 0%

profile of v6, /device:TPU:80, one launch (start us, length us, event | category | flops | bytes accessed | tf_op | source)
XLA Modules:
  0.0 187.5 jit_solution(3197755625858371082)
XLA Ops:
  0.0 0.0 copy-start
  0.0 0.0 copy-start.1
  0.0 2.3 %share.1 = f32[16,96,128]{2,1,0:T(8,128)} custom-call(s32[1]{0:T(128)} %bitcast.core_ref, f32[2,4,2,2,8,3,2,256]{7,6,5,4,3,2,1,0:T(2,128)} %bitcast.21), custom_call_target="tpu_custom_call" | custom-call | tf_op jit(solution)/shard_map/share/pallas_call | solution.py:223
  2.3 43.7 %all-to-all-start = ((f32[16,96,128]{2,1,0:T(8,128)}), f32[16,96,128]{2,1,0:T(8,128)S(1)}, u32[]{:S(2)}, u32[]{:S(2)}) async-start(f32[16,96,128]{2,1,0:T(8,128)} %share.1), calls=%async_computation | async-start | bytes 1572864 | tf_op jit(solution)/shard_map/all_to_all | solution.py:242
  46.0 0.0 copy-done.1
  46.0 0.2 convert_reduce_fusion.index_ref
  46.2 38.7 %all-to-all-done = f32[16,96,128]{2,1,0:T(8,128)S(1)} async-done(((f32[16,96,128]{2,1,0:T(8,128)}), f32[16,96,128]{2,1,0:T(8,128)S(1)}, u32[]{:S(2)}, u32[]{:S(2)}) %all-to-all-start) | async-done | bytes 786464 | tf_op jit(solution)/shard_map/all_to_all | solution.py:242
  84.9 0.0 copy-start.2
  84.9 1.7 pick_rows.1
  86.6 7.8 %all-to-all-start.1 = ((f32[16,96,128]{2,1,0:T(8,128)}), f32[16,96,128]{2,1,0:T(8,128)}, u32[]{:S(2)}, u32[]{:S(2)}) async-start(f32[16,96,128]{2,1,0:T(8,128)} %bitcast.4), calls=%async_computation.1 | async-start | bytes 1572864 | tf_op jit(solution)/shard_map/all_to_all | solution.py:244
  94.4 0.0 copy-done.2
  94.5 0.1 select_reduce_fusion
  94.6 0.0 copy-done
  94.6 1.5 gather_fusion
  96.1 1.9 %copy.7 = f32[2,2,4,32,3,256]{5,4,3,2,1,0:T(4,128)} copy(f32[2,2,4,32,3,256]{5,2,4,1,0,3:T(4,128)S(1)} %bitcast.20) | data formatting | bytes 3145728 | tf_op jit(solution)/shard_map/transpose | solution.py:249
  98.0 2.9 %reshape.48 = f32[2,2,128,768]{3,2,1,0:T(8,128)S(1)} reshape(f32[2,2,4,32,3,256]{5,4,3,2,1,0:T(4,128)} %copy.7) | data formatting | bytes 3145728 | tf_op jit(solution)/shard_map/reshape | solution.py:249
  100.9 2.0 %collective-permute-start = (f32[2,2,128,768]{3,2,1,0:T(8,128)S(1)}, f32[2,2,128,768]{3,2,1,0:T(8,128)S(1)}, u32[]{:S(2)}, u32[]{:S(2)}) collective-permute-start(f32[2,2,128,768]{3,2,1,0:T(8,128)S(1)} %reshape.48), channel_id=1, source_target_pairs={{0,1},{1,0},{2,3},{3,2},{4,5},{5,4},{6,7},{7,6},{8,9},{9,8},{10,11... | collective-permute-start | bytes 4718600 | tf_op jit(solution)/shard_map/ppermute | solution.py:250
  102.9 1.4 fusion
  104.2 2.0 %collective-permute-done = f32[2,2,128,768]{3,2,1,0:T(8,128)S(1)} collective-permute-done((f32[2,2,128,768]{3,2,1,0:T(8,128)S(1)}, f32[2,2,128,768]{3,2,1,0:T(8,128)S(1)}, u32[]{:S(2)}, u32[]{:S(2)}) %collective-permute-start) | collective-permute-done | bytes 1572896 | tf_op jit(solution)/shard_map/ppermute | solution.py:250
  106.2 1.4 fusion.1
  107.6 25.8 %all-to-all-done.1 = f32[16,96,128]{2,1,0:T(8,128)} async-done(((f32[16,96,128]{2,1,0:T(8,128)}), f32[16,96,128]{2,1,0:T(8,128)}, u32[]{:S(2)}, u32[]{:S(2)}) %all-to-all-start.1) | async-done | bytes 786464 | tf_op jit(solution)/shard_map/all_to_all | solution.py:244
  133.4 5.4 %product.1 = f32[2,8,2,2,8,128]{5,4,3,2,1,0:T(8,128)} custom-call(s32[1]{0:T(128)} %bitcast.core_ref, f32[1536,128]{1,0:T(8,128)} %bitcast.5.v_in, bf16[2,2,128,768]{3,2,1,0:T(8,128)(2,1)} %get-tuple-element.8.hh, bf16[2,2,128,768]{3,2,1,0:T(8,128)(2,1)} %get-tuple-element.7.hl, bf16[2,2,128,768]{3,2,1,0:T(8,128)(2,1)} %get-tuple-element.6.oh, ...), custom_call_target="tpu_custom_call" | custom-call | tf_op jit(solution)/shard_map/product/pallas_call | solution.py:262
  138.8 10.4 %all-to-all-start.2 = ((f32[32,2,8,128]{3,2,1,0:T(8,128)}), f32[32,2,8,128]{3,2,1,0:T(8,128)S(1)}, u32[]{:S(2)}, u32[]{:S(2)}) async-start(f32[32,2,8,128]{3,2,1,0:T(8,128)} %bitcast.22), calls=%async_computation.2 | async-start | bytes 524288 | tf_op jit(solution)/shard_map/all_to_all | solution.py:280
  149.3 0.1 select_reduce_fusion.1
  149.4 9.8 %all-to-all-done.2 = f32[32,2,8,128]{3,2,1,0:T(8,128)S(1)} async-done(((f32[32,2,8,128]{3,2,1,0:T(8,128)}), f32[32,2,8,128]{3,2,1,0:T(8,128)S(1)}, u32[]{:S(2)}, u32[]{:S(2)}) %all-to-all-start.2) | async-done | bytes 262176 | tf_op jit(solution)/shard_map/all_to_all | solution.py:280
  159.2 1.3 sum_over_xyz.1
  160.5 7.7 %all-to-all-start.3 = ((f32[16,2,2,8,128]{4,3,2,1,0:T(8,128)}), f32[16,2,2,8,128]{4,3,2,1,0:T(8,128)S(1)}, u32[]{:S(2)}, u32[]{:S(2)}) async-start(f32[16,2,2,8,128]{4,3,2,1,0:T(8,128)} %bitcast.11), calls=%async_computation.3 | async-start | bytes 524288 | tf_op jit(solution)/shard_map/all_to_all | solution.py:292
  168.1 0.1 dynamic_slice.3.order_ref
  168.2 17.9 %all-to-all-done.3 = f32[16,2,2,8,128]{4,3,2,1,0:T(8,128)S(1)} async-done(((f32[16,2,2,8,128]{4,3,2,1,0:T(8,128)}), f32[16,2,2,8,128]{4,3,2,1,0:T(8,128)S(1)}, u32[]{:S(2)}, u32[]{:S(2)}) %all-to-all-start.3) | async-done | bytes 262176 | tf_op jit(solution)/shard_map/all_to_all | solution.py:292
  186.2 1.3 final.1
  (4 shorter events, 0.0 us)
Async XLA Ops:
  0.0 94.6 %copy-start = (f32[32,2,2,4,3,256]{5,3,4,2,1,0:T(4,128)S(1)}, f32[32,2,2,4,3,256]{5,3,4,2,1,0:T(4,128)}, u32[]{:S(2)}) copy-start(f32[32,2,2,4,3,256]{5,3,4,2,1,0:T(4,128)} %param.4) | copy-start | bytes 4718596
  0.0 46.0 %copy-start.1 = (s32[32]{0:T(128)S(1)}, s32[32]{0:T(128)}, u32[]{:S(2)}) copy-start(s32[32]{0:T(128)} %param.6) | copy-start | bytes 388
  2.3 82.6 %all-to-all-start = ((f32[16,96,128]{2,1,0:T(8,128)}), f32[16,96,128]{2,1,0:T(8,128)S(1)}, u32[]{:S(2)}, u32[]{:S(2)}) async-start(f32[16,96,128]{2,1,0:T(8,128)} %share.1), calls=%async_computation | async-start | bytes 1572864 | tf_op jit(solution)/shard_map/all_to_all | solution.py:242
  84.9 9.6 %copy-start.2 = (s32[32]{0:T(128)S(1)}, s32[32]{0:T(128)}, u32[]{:S(2)}) copy-start(s32[32]{0:T(128)} %param.7) | copy-start | bytes 388
  86.6 46.8 %all-to-all-start.1 = ((f32[16,96,128]{2,1,0:T(8,128)}), f32[16,96,128]{2,1,0:T(8,128)}, u32[]{:S(2)}, u32[]{:S(2)}) async-start(f32[16,96,128]{2,1,0:T(8,128)} %bitcast.4), calls=%async_computation.1 | async-start | bytes 1572864 | tf_op jit(solution)/shard_map/all_to_all | solution.py:244
  100.9 5.3 %collective-permute-start = (f32[2,2,128,768]{3,2,1,0:T(8,128)S(1)}, f32[2,2,128,768]{3,2,1,0:T(8,128)S(1)}, u32[]{:S(2)}, u32[]{:S(2)}) collective-permute-start(f32[2,2,128,768]{3,2,1,0:T(8,128)S(1)} %reshape.48), channel_id=1, source_target_pairs={{0,1},{1,0},{2,3},{3,2},{4,5},{5,4},{6,7},{7,6},{8,9},{9,8},{10,11... | collective-permute-start | bytes 4718600 | tf_op jit(solution)/shard_map/ppermute | solution.py:250
  138.8 20.4 %all-to-all-start.2 = ((f32[32,2,8,128]{3,2,1,0:T(8,128)}), f32[32,2,8,128]{3,2,1,0:T(8,128)S(1)}, u32[]{:S(2)}, u32[]{:S(2)}) async-start(f32[32,2,8,128]{3,2,1,0:T(8,128)} %bitcast.22), calls=%async_computation.2 | async-start | bytes 524288 | tf_op jit(solution)/shard_map/all_to_all | solution.py:280
  160.5 25.7 %all-to-all-start.3 = ((f32[16,2,2,8,128]{4,3,2,1,0:T(8,128)}), f32[16,2,2,8,128]{4,3,2,1,0:T(8,128)S(1)}, u32[]{:S(2)}, u32[]{:S(2)}) async-start(f32[16,2,2,8,128]{4,3,2,1,0:T(8,128)} %bitcast.11), calls=%async_computation.3 | async-start | bytes 524288 | tf_op jit(solution)/shard_map/all_to_all | solution.py:292

commit v7 on v6

--- a/solution.py
+++ b/solution.py
@@ -100,29 +100,25 @@
     return high, low
 
 
-def product_kernel(
-    parts, core_ref, v_in, hh, hl, oh, ol, out_hbm,
-    v_ref, p_hi, p_lo, a_ref, b_ref, out_ref, sem, v_sem, out_sem,
-):
-    tl, nq, nx, nsrc, piece, width = out_ref.shape
-    cols = p_hi.shape[3] // LANES
+def split_kernel(core_ref, own_ref, other_ref, *outs):
+    tl, _, width, _ = own_ref.shape
+    core = core_ref[0]
+    for slot, ref in ((core, own_ref), (1 - core, other_ref)):
+        span = pl.ds(pl.multiple_of(slot * width, width), width)
+        for t in range(tl):
+            for ri in range(2):
+                high, low = halves(ref[t, ri])
+                outs[t][ri, span, :] = high
+                outs[tl + t][ri, span, :] = low
+
+
+def product_kernel(parts, tl, v_ref, *refs):
+    p_hi, p_lo = refs[:tl], refs[tl : 2 * tl]
+    out_hbm, a_ref, b_ref, out_ref, out_sem = refs[2 * tl :]
+    _, nq, nx, nsrc, piece, width = out_ref.shape
+    cols = p_hi[0].shape[2] // LANES
     half = a_ref.shape[1] // 4
     nz = half // parts
-    core = core_ref[0]
-
-    v_copy = pltpu.make_async_copy(v_in, v_ref, v_sem)
-    v_copy.start()
-    copies = []
-    for t in range(tl):
-        for own, other, dst in ((hh, oh, p_hi), (hl, ol, p_lo)):
-            pair = []
-            for i, (src, slot) in enumerate(((own, core), (other, nsrc - 1 - core))):
-                span = pl.ds(pl.multiple_of(slot * width, width), width)
-                pair.append(
-                    pltpu.make_async_copy(src.at[t], dst.at[t, :, span], sem.at[len(copies), i])
-                )
-                pair[-1].start()
-            copies.append(pair)
 
     def dot(left, right):
         return lax.dot_general(
@@ -132,7 +128,6 @@
     stride = tl * parts * cols * 2
     per = half // nx
     sends = []
-    v_copy.wait()
     for t in range(tl):
         for i in range(parts):
             for b in range(cols):
@@ -147,14 +142,9 @@
                     a_ref[t, low, lane] = -imag
                     b_ref[t, top, lane] = imag
                     b_ref[t, low, lane] = real
-    for t in range(tl):
-        for copy in copies[2 * t]:
-            copy.wait()
-        both = dot(a_ref[t], p_hi[t, 0]) + dot(b_ref[t], p_hi[t, 1])
-        for copy in copies[2 * t + 1]:
-            copy.wait()
+        both = dot(a_ref[t], p_hi[t][0]) + dot(b_ref[t], p_hi[t][1])
         total = both[: 2 * half] + both[2 * half :]
-        total += dot(a_ref[t, : 2 * half], p_lo[t, 0]) + dot(b_ref[t, : 2 * half], p_lo[t, 1])
+        total += dot(a_ref[t, : 2 * half], p_lo[t][0]) + dot(b_ref[t, : 2 * half], p_lo[t][1])
         for q in range(nq):
             ri, part = divmod(q, nq // 2)
             for x in range(nx):
@@ -200,7 +190,7 @@
 
 
 TA = ("tq", "tp")
-NEAR = 2
+NEAR = 4
 
 
 def local(spinors, eigvecs, group_of, source_ids):
@@ -252,29 +242,29 @@
     vmem = pl.BlockSpec(memory_space=pltpu.VMEM)
     smem = pl.BlockSpec(memory_space=pltpu.SMEM)
     wide = nc * sites
-
-    def split(x):
-        high = lax.reduce_precision(x, 8, 7)
-        return high.astype(jnp.bfloat16), (x - high).astype(jnp.bfloat16)
+    cut = pl.pallas_call(
+        split_kernel,
+        out_shape=[pltpu.VMEM((2, nsrc * ns * n, wide), jnp.bfloat16)] * (2 * tl),
+        in_specs=[smem, vmem, vmem],
+        out_specs=[vmem] * (2 * tl),
+        compiler_params=small(60),
+        name="split",
+    )(core[None], held, other)
 
     piece = 2 * per_x // near
-    hbm = pl.BlockSpec(memory_space=pltpu.HBM)
     pair = pl.pallas_call(
-        functools.partial(product_kernel, part),
+        functools.partial(product_kernel, part, tl),
         out_shape=jax.ShapeDtypeStruct((near, nx, nsrc, tl, piece, ns * n), jnp.float32),
-        in_specs=[smem] + [hbm] * 5,
-        out_specs=hbm,
-        scratch_shapes=[pltpu.VMEM(sent.shape, jnp.float32)]
-        + [pltpu.VMEM((tl, 2, nsrc * ns * n, wide), jnp.bfloat16)] * 2
-        + [pltpu.VMEM((tl, 4 * mine, wide), jnp.bfloat16)] * 2
+        in_specs=[vmem] * (1 + 2 * tl),
+        out_specs=pl.BlockSpec(memory_space=pltpu.HBM),
+        scratch_shapes=[pltpu.VMEM((tl, 4 * mine, wide), jnp.bfloat16)] * 2
         + [
             pltpu.VMEM((tl, near, nx, nsrc, piece, ns * n), jnp.float32),
-            pltpu.SemaphoreType.DMA((2 * tl, 2)),
-            pltpu.SemaphoreType.DMA,
             pltpu.SemaphoreType.DMA((tl,)),
         ],
+        compiler_params=small(12),
         name="product",
-    )(core[None], sent, *split(held), *split(other))
+    )(sent, *cut)
 
     pair = pair.reshape(near * nx * nsrc, tl, piece, ns * n)
     got = lax.all_to_all(pair, ("tp", "xyz", "src"), 0, 0, tiled=True)

time: 188 us -> 186 us (0.989)
  waiting for transfers between devices: 94.2 us -> 90.1 us
  local copies, waits for them, and re-layouts: 6.37 us -> 9.83 us
  other arithmetic: 3.19 us -> 0.43 us
    all_to_all x1, waiting for transfers between devices: 25.8 us -> 22.2 us  [local(): lax.all_to_all(picked.reshape(nta, tl * lines, LANES), TA, 0, 0, tiled=True)]
    all_to_all x1, waiting for transfers between devices: 17.9 us -> 14.5 us  [local(): lax.all_to_all(back.reshape(nta, rows, nsrc, piece, ns * n), TA, 0, 0, ti...]
    convert_element_type x2 -> x0, other arithmetic: 2.76 us -> none  [split(): return (high.astype(jnp.bfloat16), (x - high).astype(jnp.bfloat16))]
    all_to_all x1, starting transfers between devices: 10.4 us -> 12.8 us  [local(): got = lax.all_to_all(pair, ('tp', 'xyz', 'src'), 0, 0, tiled=True)]
    unnamed x6 -> x10, local copies, waits for them, and re-layouts: 0.01 us -> 2.03 us
    pallas_call x1 -> x2, Pallas kernels: 5.41 us -> 4.63 us  [the longest x1 2.42 us: local(): pl.pallas_call(split_kernel, out_shape=[pltpu.VMEM((2, nsrc * ns * n, wid...]
  transfers between devices with their start and end apart: 5 -> 5, of which waited for: 5 -> 5; matrix products, arithmetic and copies ran while one was open for 5% -> 4% of each run, Pallas kernels for 0% -> 1%
where the time goes in v7:
time: 186 us; the launch traced here: 185 us
  waiting for transfers between devices  90.1 us (48%)
  starting transfers between devices  73.4 us (39%)
  Pallas kernels  11 us (6%)
  local copies, waits for them, and re-layouts  9.83 us (5%)
    all_to_all x1, starting transfers between devices, local(): spread = lax.all_to_all(share, TA, 0, 0, tiled=True)  43.7 us
    all_to_all x1, waiting for transfers between devices, local(): spread = lax.all_to_all(share, TA, 0, 0, tiled=True)  38.7 us
    all_to_all x1, waiting for transfers between devices, local(): lax.all_to_all(picked.reshape(nta, tl * lines, LANES), TA, 0, 0, tiled=True)  22.2 us
    all_to_all x1, waiting for transfers between devices, local(): lax.all_to_all(back.reshape(nta, rows, nsrc, piece, ns * n), TA, 0, 0, ti...  14.5 us
    all_to_all x1, starting transfers between devices, local(): got = lax.all_to_all(pair, ('tp', 'xyz', 'src'), 0, 0, tiled=True)  12.8 us
    all_to_all x1, waiting for transfers between devices, local(): got = lax.all_to_all(pair, ('tp', 'xyz', 'src'), 0, 0, tiled=True)  11.2 us
    all_to_all x1, starting transfers between devices, local(): lax.all_to_all(picked.reshape(nta, tl * lines, LANES), TA, 0, 0, tiled=True)  7.83 us
    all_to_all x1, starting transfers between devices, local(): lax.all_to_all(back.reshape(nta, rows, nsrc, piece, ns * n), TA, 0, 0, ti...  7.05 us
  transfers between devices with their start and end apart: 5, of which 5 were waited for; matrix products, arithmetic and copies ran while one was open for 4% of the time, Pallas kernels for 1%

profile of v7, /device:TPU:80, one launch (start us, length us, event | category | flops | bytes accessed | tf_op | source)
XLA Modules:
  0.0 184.9 jit_solution(18124313922488047015)
XLA Ops:
  0.0 0.0 copy-start.3
  0.0 2.1 %share.1 = f32[16,96,128]{2,1,0:T(8,128)} custom-call(s32[1]{0:T(128)} %bitcast.core_ref, f32[2,4,2,2,8,3,2,256]{7,6,5,4,3,2,1,0:T(2,128)} %bitcast.22), custom_call_target="tpu_custom_call" | custom-call | tf_op jit(solution)/shard_map/share/pallas_call | solution.py:213
  2.1 43.7 %all-to-all-start = ((f32[16,96,128]{2,1,0:T(8,128)}), f32[16,96,128]{2,1,0:T(8,128)S(1)}, u32[]{:S(2)}, u32[]{:S(2)}) async-start(f32[16,96,128]{2,1,0:T(8,128)} %share.1), calls=%async_computation | async-start | bytes 1572864 | tf_op jit(solution)/shard_map/all_to_all | solution.py:232
  45.8 0.0 copy-done.3
  45.8 0.2 convert_reduce_fusion.index_ref
  46.0 38.7 %all-to-all-done = f32[16,96,128]{2,1,0:T(8,128)S(1)} async-done(((f32[16,96,128]{2,1,0:T(8,128)}), f32[16,96,128]{2,1,0:T(8,128)S(1)}, u32[]{:S(2)}, u32[]{:S(2)}) %all-to-all-start) | async-done | bytes 786464 | tf_op jit(solution)/shard_map/all_to_all | solution.py:232
  84.7 0.0 copy-start.4
  84.7 1.7 pick_rows.1
  86.4 7.8 %all-to-all-start.1 = ((f32[16,96,128]{2,1,0:T(8,128)}), f32[16,96,128]{2,1,0:T(8,128)S(1)}, u32[]{:S(2)}, u32[]{:S(2)}) async-start(f32[16,96,128]{2,1,0:T(8,128)} %bitcast.4), calls=%async_computation.1 | async-start | bytes 1572864 | tf_op jit(solution)/shard_map/all_to_all | solution.py:234
  94.3 0.0 copy-done.4
  94.3 0.1 select_reduce_fusion
  94.4 2.9 %gather_fusion = f32[32,2,2,4,3,256]{5,3,4,2,1,0:T(4,128)S(1)} fusion(f32[32,2,2,4,3,256]{5,3,4,2,1,0:T(4,128)} %param.4, s32[1024]{0:T(1024)S(1)} %pad_clamp_fusion), kind=kCustom, calls=%fused_computation | custom fusion | bytes 3145856 | tf_op jit(solution)/shard_map/gather | solution.py:238
  97.3 1.9 %copy.7 = f32[2,2,4,32,3,256]{5,4,3,2,1,0:T(4,128)} copy(f32[2,2,4,32,3,256]{5,2,4,1,0,3:T(4,128)S(1)} %bitcast.21) | data formatting | bytes 3145728 | tf_op jit(solution)/shard_map/transpose | solution.py:239
  99.3 2.9 %reshape.48.own_ref = f32[2,2,128,768]{3,2,1,0:T(8,128)S(1)} reshape(f32[2,2,4,32,3,256]{5,4,3,2,1,0:T(4,128)} %copy.7) | data formatting | bytes 3145728 | tf_op jit(solution)/shard_map/reshape | solution.py:239
  102.2 0.0 copy-start.2
  102.2 2.0 %collective-permute-start = (f32[2,2,128,768]{3,2,1,0:T(8,128)S(1)}, f32[2,2,128,768]{3,2,1,0:T(8,128)}, u32[]{:S(2)}, u32[]{:S(2)}) collective-permute-start(f32[2,2,128,768]{3,2,1,0:T(8,128)S(1)} %reshape.48.own_ref), channel_id=1, source_target_pairs={{0,1},{1,0},{2,3},{3,2},{4,5},{5,4},{6,7},{7,6},{8,9},{9,8},{10,11... | collective-permute-start | bytes 4718600 | tf_op jit(solution)/shard_map/ppermute | solution.py:240
  104.1 0.0 copy-done.2
  104.1 3.5 %collective-permute-done.other_ref = f32[2,2,128,768]{3,2,1,0:T(8,128)} collective-permute-done((f32[2,2,128,768]{3,2,1,0:T(8,128)S(1)}, f32[2,2,128,768]{3,2,1,0:T(8,128)}, u32[]{:S(2)}, u32[]{:S(2)}) %collective-permute-start) | collective-permute-done | bytes 1572896 | tf_op jit(solution)/shard_map/ppermute | solution.py:240
  107.6 2.4 %split.1 = (bf16[2,256,768]{2,1,0:T(8,128)(2,1)S(1)}, bf16[2,256,768]{2,1,0:T(8,128)(2,1)S(1)}, bf16[2,256,768]{2,1,0:T(8,128)(2,1)S(1)}, bf16[2,256,768]{2,1,0:T(8,128)(2,1)S(1)}) custom-call(s32[1]{0:T(128)} %bitcast.core_ref, f32[2,2,128,768]{3,2,1,0:T(8,128)} %copy-done.2, f32[2,2,128,768]{3,2,1,0:T(8,128)} %collective-permute-done.other_ref), custom_call_target="tpu_custom_call" | custom-call | tf_op jit(solution)/shard_map/split/pallas_call | solution.py:245
  110.1 0.0 copy-start
  110.1 0.9 copy-done
  111.0 22.2 %all-to-all-done.1 = f32[16,96,128]{2,1,0:T(8,128)S(1)} async-done(((f32[16,96,128]{2,1,0:T(8,128)}), f32[16,96,128]{2,1,0:T(8,128)S(1)}, u32[]{:S(2)}, u32[]{:S(2)}) %all-to-all-start.1) | async-done | bytes 786464 | tf_op jit(solution)/shard_map/all_to_all | solution.py:234
  133.2 1.1 copy-done.1
  134.3 2.2 %product.1 = f32[4,8,2,2,4,128]{5,4,3,2,1,0:T(4,128)} custom-call(f32[1536,128]{1,0:T(8,128)S(1)} %bitcast.17, bf16[2,256,768]{2,1,0:T(8,128)(2,1)S(1)} %copy-done.1, bf16[2,256,768]{2,1,0:T(8,128)(2,1)S(1)} %get-tuple-element.10.refs_1_, bf16[2,256,768]{2,1,0:T(8,128)(2,1)S(1)} %get-tuple-element.11.refs_2_, bf16[2,256,768]{2,1,0:T(8,128)(2,1)S(1)} %get-tuple-element.12.refs_3_), custom_call_target="tpu_custom_call" | custom-call | tf_op jit(solution)/shard_map/product/pallas_call | solution.py:255
  136.5 12.8 %all-to-all-start.2 = ((f32[64,2,4,128]{3,2,1,0:T(4,128)}), f32[64,2,4,128]{3,2,1,0:T(4,128)S(1)}, u32[]{:S(2)}, u32[]{:S(2)}) async-start(f32[64,2,4,128]{3,2,1,0:T(4,128)} %bitcast.9), calls=%async_computation.2 | async-start | bytes 524288 | tf_op jit(solution)/shard_map/all_to_all | solution.py:270
  149.4 0.1 select_reduce_fusion.1
  149.5 11.2 %all-to-all-done.2 = f32[64,2,4,128]{3,2,1,0:T(4,128)S(1)} async-done(((f32[64,2,4,128]{3,2,1,0:T(4,128)}), f32[64,2,4,128]{3,2,1,0:T(4,128)S(1)}, u32[]{:S(2)}, u32[]{:S(2)}) %all-to-all-start.2) | async-done | bytes 262176 | tf_op jit(solution)/shard_map/all_to_all | solution.py:270
  160.7 1.2 sum_over_xyz.1
  162.0 7.1 %all-to-all-start.3 = ((f32[16,2,2,4,128]{4,3,2,1,0:T(4,128)}), f32[16,2,2,4,128]{4,3,2,1,0:T(4,128)S(1)}, u32[]{:S(2)}, u32[]{:S(2)}) async-start(f32[16,2,2,4,128]{4,3,2,1,0:T(4,128)} %bitcast.11), calls=%async_computation.3 | async-start | bytes 262144 | tf_op jit(solution)/shard_map/all_to_all | solution.py:282
  169.0 0.1 dynamic_slice.3.order_ref
  169.1 14.5 %all-to-all-done.3 = f32[16,2,2,4,128]{4,3,2,1,0:T(4,128)S(1)} async-done(((f32[16,2,2,4,128]{4,3,2,1,0:T(4,128)}), f32[16,2,2,4,128]{4,3,2,1,0:T(4,128)S(1)}, u32[]{:S(2)}, u32[]{:S(2)}) %all-to-all-start.3) | async-done | bytes 131104 | tf_op jit(solution)/shard_map/all_to_all | solution.py:282
  183.6 1.3 final.1
  (5 shorter events, 0.0 us)
Async XLA Ops:
  0.0 45.8 %copy-start.3 = (s32[32]{0:T(128)S(1)}, s32[32]{0:T(128)}, u32[]{:S(2)}) copy-start(s32[32]{0:T(128)} %param.6) | copy-start | bytes 388
  2.1 82.6 %all-to-all-start = ((f32[16,96,128]{2,1,0:T(8,128)}), f32[16,96,128]{2,1,0:T(8,128)S(1)}, u32[]{:S(2)}, u32[]{:S(2)}) async-start(f32[16,96,128]{2,1,0:T(8,128)} %share.1), calls=%async_computation | async-start | bytes 1572864 | tf_op jit(solution)/shard_map/all_to_all | solution.py:232
  84.7 9.6 %copy-start.4 = (s32[32]{0:T(128)S(1)}, s32[32]{0:T(128)}, u32[]{:S(2)}) copy-start(s32[32]{0:T(128)} %param.7) | copy-start | bytes 388
  86.4 46.7 %all-to-all-start.1 = ((f32[16,96,128]{2,1,0:T(8,128)}), f32[16,96,128]{2,1,0:T(8,128)S(1)}, u32[]{:S(2)}, u32[]{:S(2)}) async-start(f32[16,96,128]{2,1,0:T(8,128)} %bitcast.4), calls=%async_computation.1 | async-start | bytes 1572864 | tf_op jit(solution)/shard_map/all_to_all | solution.py:234
  102.2 2.0 %copy-start.2 = (f32[2,2,128,768]{3,2,1,0:T(8,128)}, f32[2,2,128,768]{3,2,1,0:T(8,128)S(1)}, u32[]{:S(2)}) copy-start(f32[2,2,128,768]{3,2,1,0:T(8,128)S(1)} %reshape.48.own_ref) | copy-start | bytes 4718596
  102.2 5.5 %collective-permute-start = (f32[2,2,128,768]{3,2,1,0:T(8,128)S(1)}, f32[2,2,128,768]{3,2,1,0:T(8,128)}, u32[]{:S(2)}, u32[]{:S(2)}) collective-permute-start(f32[2,2,128,768]{3,2,1,0:T(8,128)S(1)} %reshape.48.own_ref), channel_id=1, source_target_pairs={{0,1},{1,0},{2,3},{3,2},{4,5},{5,4},{6,7},{7,6},{8,9},{9,8},{10,11... | collective-permute-start | bytes 4718600 | tf_op jit(solution)/shard_map/ppermute | solution.py:240
  110.1 0.9 copy-start
  133.2 1.1 copy-start.1
  136.5 24.2 %all-to-all-start.2 = ((f32[64,2,4,128]{3,2,1,0:T(4,128)}), f32[64,2,4,128]{3,2,1,0:T(4,128)S(1)}, u32[]{:S(2)}, u32[]{:S(2)}) async-start(f32[64,2,4,128]{3,2,1,0:T(4,128)} %bitcast.9), calls=%async_computation.2 | async-start | bytes 524288 | tf_op jit(solution)/shard_map/all_to_all | solution.py:270
  162.0 21.6 %all-to-all-start.3 = ((f32[16,2,2,4,128]{4,3,2,1,0:T(4,128)}), f32[16,2,2,4,128]{4,3,2,1,0:T(4,128)S(1)}, u32[]{:S(2)}, u32[]{:S(2)}) async-start(f32[16,2,2,4,128]{4,3,2,1,0:T(4,128)} %bitcast.11), calls=%async_computation.3 | async-start | bytes 262144 | tf_op jit(solution)/shard_map/all_to_all | solution.py:282

commit v8 on v7

--- a/solution.py
+++ b/solution.py
@@ -100,25 +100,21 @@
     return high, low
 
 
-def split_kernel(core_ref, own_ref, other_ref, *outs):
-    tl, _, width, _ = own_ref.shape
-    core = core_ref[0]
-    for slot, ref in ((core, own_ref), (1 - core, other_ref)):
-        span = pl.ds(pl.multiple_of(slot * width, width), width)
-        for t in range(tl):
-            for ri in range(2):
-                high, low = halves(ref[t, ri])
-                outs[t][ri, span, :] = high
-                outs[tl + t][ri, span, :] = low
-
-
-def product_kernel(parts, tl, v_ref, *refs):
+def split_kernel(in_ref, *outs):
+    tl = in_ref.shape[0]
+    for t in range(tl):
+        for ri in range(2):
+            outs[t][ri], outs[tl + t][ri] = halves(in_ref[t, ri])
+
+
+def product_kernel(parts, tl, slot_ref, v_ref, *refs):
     p_hi, p_lo = refs[:tl], refs[tl : 2 * tl]
-    out_hbm, a_ref, b_ref, out_ref, out_sem = refs[2 * tl :]
-    _, nq, nx, nsrc, piece, width = out_ref.shape
+    out_hbm, a_ref, b_ref, out_ref, out_sem = refs[-5:]
+    _, nq, nx, piece, _ = out_ref.shape
     cols = p_hi[0].shape[2] // LANES
     half = a_ref.shape[1] // 4
     nz = half // parts
+    slot = slot_ref[0]
 
     def dot(left, right):
         return lax.dot_general(
@@ -149,11 +145,10 @@
             ri, part = divmod(q, nq // 2)
             for x in range(nx):
                 first = ri * half + x * per + part * piece
-                for slot in range(nsrc):
-                    out_ref[t, q, x, slot] = total[
-                        first : first + piece, slot * width : (slot + 1) * width
-                    ]
-        sends.append(pltpu.make_async_copy(out_ref.at[t], out_hbm.at[:, :, :, t], out_sem.at[t]))
+                out_ref[t, q, x] = total[first : first + piece]
+        sends.append(
+            pltpu.make_async_copy(out_ref.at[t], out_hbm.at[:, :, slot, t], out_sem.at[t])
+        )
         sends[-1].start()
     for send in sends:
         send.wait()
@@ -237,37 +232,45 @@
     inverse = inverse_of(source_ids - n * core)
     held = spinors.at[inverse].get(mode="promise_in_bounds")
     held = held.transpose(1, 2, 3, 0, 4, 5).reshape(tl, 2, ns * n, nc * sites)
-    other = lax.ppermute(held, "src", [(i, nsrc - 1 - i) for i in range(nsrc)])
-
     vmem = pl.BlockSpec(memory_space=pltpu.VMEM)
     smem = pl.BlockSpec(memory_space=pltpu.SMEM)
+    hbm = pl.BlockSpec(memory_space=pltpu.HBM)
     wide = nc * sites
     cut = pl.pallas_call(
         split_kernel,
-        out_shape=[pltpu.VMEM((2, nsrc * ns * n, wide), jnp.bfloat16)] * (2 * tl),
-        in_specs=[smem, vmem, vmem],
+        out_shape=[pltpu.VMEM((2, ns * n, wide), jnp.bfloat16)] * (2 * tl),
+        in_specs=[vmem],
         out_specs=[vmem] * (2 * tl),
-        compiler_params=small(60),
+        compiler_params=small(61),
         name="split",
-    )(core[None], held, other)
-
+    )(held)
+
+    sent, *cut = lax.optimization_barrier((sent, *cut))
+
+    other = lax.ppermute(sent, "src", [(i, nsrc - 1 - i) for i in range(nsrc)])
     piece = 2 * per_x // near
-    pair = pl.pallas_call(
-        functools.partial(product_kernel, part, tl),
-        out_shape=jax.ShapeDtypeStruct((near, nx, nsrc, tl, piece, ns * n), jnp.float32),
-        in_specs=[vmem] * (1 + 2 * tl),
-        out_specs=pl.BlockSpec(memory_space=pltpu.HBM),
-        scratch_shapes=[pltpu.VMEM((tl, 4 * mine, wide), jnp.bfloat16)] * 2
-        + [
-            pltpu.VMEM((tl, near, nx, nsrc, piece, ns * n), jnp.float32),
-            pltpu.SemaphoreType.DMA((tl,)),
-        ],
-        compiler_params=small(12),
-        name="product",
-    )(sent, *cut)
-
-    pair = pair.reshape(near * nx * nsrc, tl, piece, ns * n)
-    got = lax.all_to_all(pair, ("tp", "xyz", "src"), 0, 0, tiled=True)
+
+    def product(slot, vectors, *into):
+        return pl.pallas_call(
+            functools.partial(product_kernel, part, tl),
+            out_shape=jax.ShapeDtypeStruct((near, nx, nsrc, tl, piece, ns * n), jnp.float32),
+            in_specs=[smem] + [vmem] * (1 + 2 * tl) + [hbm] * len(into),
+            out_specs=hbm,
+            scratch_shapes=[pltpu.VMEM((tl, 4 * mine, wide), jnp.bfloat16)] * 2
+            + [
+                pltpu.VMEM((tl, near, nx, piece, ns * n), jnp.float32),
+                pltpu.SemaphoreType.DMA((tl,)),
+            ],
+            input_output_aliases={2 + 2 * tl: 0} if into else {},
+            compiler_params=small(12),
+            name="product",
+        )(slot[None], vectors, *cut, *into)
+
+    pair = product(core, sent)
+    pair = product(nsrc - 1 - core, other, pair)
+
+    pair = pair.reshape(near * nx, nsrc, tl, piece, ns * n)
+    got = lax.all_to_all(pair, ("tp", "xyz"), 0, 0, tiled=True)
     here = jnp.clip(ordering - (ta // near) * (near * tl), 0, near * tl - 1)
     back = pl.pallas_call(
         sum_kernel,

time: 186 us -> 188 us (1.011)
  waiting for transfers between devices: 90.1 us -> 92.9 us
  Pallas kernels: 11 us -> 13 us
    all_to_all x1, waiting for transfers between devices: 22.2 us -> 28.4 us  [local(): lax.all_to_all(picked.reshape(nta, tl * lines, LANES), TA, 0, 0, tiled=True)]
    ppermute x1, waiting for transfers between devices: 3.5 us -> 0.46 us  [local(): other = lax.ppermute(sent, 'src', [(i, nsrc - 1 - i) for i in range(nsrc)])]
    unnamed x10 -> x4, local copies, waits for them, and re-layouts: 2.03 us -> 0.01 us
    pallas_call x2 -> x3, Pallas kernels: 4.63 us -> 6.63 us  [the longest x2 4.95 us: product(): pl.pallas_call(functools.partial(product_kernel, part, tl), out_shape=jax...]
  transfers between devices with their start and end apart: 5 -> 5, of which waited for: 5 -> 5; matrix products, arithmetic and copies ran while one was open for 4% -> 5% of each run, Pallas kernels for 1% -> 2%
where the time goes in v8:
time: 188 us; the launch traced here: 187 us
  waiting for transfers between devices  92.9 us (49%)
  starting transfers between devices  71.8 us (38%)
  Pallas kernels  13 us (7%)
  local copies, waits for them, and re-layouts  8.74 us (5%)
    all_to_all x1, starting transfers between devices, local(): spread = lax.all_to_all(share, TA, 0, 0, tiled=True)  43.7 us
    all_to_all x1, waiting for transfers between devices, local(): spread = lax.all_to_all(share, TA, 0, 0, tiled=True)  38.7 us
    all_to_all x1, waiting for transfers between devices, local(): lax.all_to_all(picked.reshape(nta, tl * lines, LANES), TA, 0, 0, tiled=True)  28.4 us
    all_to_all x1, waiting for transfers between devices, local(): lax.all_to_all(back.reshape(nta, rows, nsrc, piece, ns * n), TA, 0, 0, ti...  13.8 us
    all_to_all x1, waiting for transfers between devices, local(): got = lax.all_to_all(pair, ('tp', 'xyz'), 0, 0, tiled=True)  11.6 us
    all_to_all x1, starting transfers between devices, local(): got = lax.all_to_all(pair, ('tp', 'xyz'), 0, 0, tiled=True)  11.3 us
    all_to_all x1, starting transfers between devices, local(): lax.all_to_all(picked.reshape(nta, tl * lines, LANES), TA, 0, 0, tiled=True)  7.83 us
    all_to_all x1, starting transfers between devices, local(): lax.all_to_all(back.reshape(nta, rows, nsrc, piece, ns * n), TA, 0, 0, ti...  7.05 us
  transfers between devices with their start and end apart: 5, of which 5 were waited for; matrix products, arithmetic and copies ran while one was open for 5% of the time, Pallas kernels for 2%

profile of v8, /device:TPU:80, one launch (start us, length us, event | category | flops | bytes accessed | tf_op | source)
XLA Modules:
  0.0 187.0 jit_solution(1912449782277483930)
XLA Ops:
  0.0 0.0 copy-start
  0.0 2.1 %share.1 = f32[16,96,128]{2,1,0:T(8,128)} custom-call(s32[1]{0:T(128)} %bitcast.1.core_ref.slot_ref, f32[2,4,2,2,8,3,2,256]{7,6,5,4,3,2,1,0:T(2,128)} %bitcast.24), custom_call_target="tpu_custom_call" | custom-call | tf_op jit(solution)/shard_map/share/pallas_call | solution.py:208
  2.1 43.7 %all-to-all-start = ((f32[16,96,128]{2,1,0:T(8,128)}), f32[16,96,128]{2,1,0:T(8,128)S(1)}, u32[]{:S(2)}, u32[]{:S(2)}) async-start(f32[16,96,128]{2,1,0:T(8,128)} %share.1), calls=%async_computation | async-start | bytes 1572864 | tf_op jit(solution)/shard_map/all_to_all | solution.py:227
  45.8 0.0 copy-done
  45.8 0.2 convert_reduce_fusion.index_ref
  46.0 38.7 %all-to-all-done = f32[16,96,128]{2,1,0:T(8,128)S(1)} async-done(((f32[16,96,128]{2,1,0:T(8,128)}), f32[16,96,128]{2,1,0:T(8,128)S(1)}, u32[]{:S(2)}, u32[]{:S(2)}) %all-to-all-start) | async-done | bytes 786464 | tf_op jit(solution)/shard_map/all_to_all | solution.py:227
  84.7 0.0 copy-start.1
  84.7 1.7 pick_rows.1
  86.4 7.8 %all-to-all-start.1 = ((f32[16,96,128]{2,1,0:T(8,128)}), f32[16,96,128]{2,1,0:T(8,128)S(1)}, u32[]{:S(2)}, u32[]{:S(2)}) async-start(f32[16,96,128]{2,1,0:T(8,128)} %bitcast.5), calls=%async_computation.1 | async-start | bytes 1572864 | tf_op jit(solution)/shard_map/all_to_all | solution.py:229
  94.3 0.0 copy-done.1
  94.3 0.1 select_reduce_fusion
  94.4 2.9 %gather_fusion = f32[32,2,2,4,3,256]{5,3,4,2,1,0:T(4,128)S(1)} fusion(f32[32,2,2,4,3,256]{5,3,4,2,1,0:T(4,128)} %param.4, s32[1024]{0:T(1024)S(1)} %pad_clamp_fusion), kind=kCustom, calls=%fused_computation | custom fusion | bytes 3145856 | tf_op jit(solution)/shard_map/gather | solution.py:233
  97.3 1.9 %copy.8 = f32[2,2,4,32,3,256]{5,4,3,2,1,0:T(4,128)} copy(f32[2,2,4,32,3,256]{5,2,4,1,0,3:T(4,128)S(1)} %bitcast.23) | data formatting | bytes 3145728 | tf_op jit(solution)/shard_map/transpose | solution.py:234
  99.2 3.8 %reshape.48.in_ref = f32[2,2,128,768]{3,2,1,0:T(8,128)} reshape(f32[2,2,4,32,3,256]{5,4,3,2,1,0:T(4,128)} %copy.8) | data formatting | bytes 3145728 | tf_op jit(solution)/shard_map/reshape | solution.py:234
  103.1 1.7 split.1
  104.8 28.4 %all-to-all-done.1 = f32[16,96,128]{2,1,0:T(8,128)S(1)} async-done(((f32[16,96,128]{2,1,0:T(8,128)}), f32[16,96,128]{2,1,0:T(8,128)S(1)}, u32[]{:S(2)}, u32[]{:S(2)}) %all-to-all-start.1) | async-done | bytes 786464 | tf_op jit(solution)/shard_map/all_to_all | solution.py:229
  133.1 1.9 %collective-permute-start = (f32[1536,128]{1,0:T(8,128)S(1)}, f32[1536,128]{1,0:T(8,128)}, u32[]{:S(2)}, u32[]{:S(2)}) collective-permute-start(f32[1536,128]{1,0:T(8,128)S(1)} %bitcast.19), channel_id=1, source_target_pairs={{0,1},{1,0},{2,3},{3,2},{4,5},{5,4},{6,7},{7,6},{8,9},{9,8},{10,11... | collective-permute-start | bytes 2359304 | tf_op jit(solution)/shard_map/ppermute | solution.py:250
  135.1 1.9 %product.2.refs_4_ = f32[4,8,2,2,4,128]{5,4,3,2,1,0:T(4,128)} custom-call(s32[1]{0:T(128)} %bitcast.1.core_ref.slot_ref, f32[1536,128]{1,0:T(8,128)S(1)} %bitcast.20, bf16[2,128,768]{2,1,0:T(8,128)(2,1)S(1)} %get-tuple-element.19.refs_0_, bf16[2,128,768]{2,1,0:T(8,128)(2,1)S(1)} %get-tuple-element.20.refs_1_, ...), custom_call_target="tpu_custom_call" | custom-call | tf_op jit(solution)/shard_map/product/pallas_call | solution.py:254
  137.0 0.5 collective-permute-done.v_ref
  137.5 3.0 %product.3 = f32[4,8,2,2,4,128]{5,4,3,2,1,0:T(4,128)} custom-call(s32[1]{0:T(128)} %bitcast.slot_ref, f32[1536,128]{1,0:T(8,128)} %collective-permute-done.v_ref, bf16[2,128,768]{2,1,0:T(8,128)(2,1)S(1)} %get-tuple-element.19.refs_0_, bf16[2,128,768]{2,1,0:T(8,128)(2,1)S(1)} %get-tuple-element.20.refs_1_, ...), custom_call_target="tpu_custom_call", output_to_operand_aliasing={{}: (6, {})} | custom-call | tf_op jit(solution)/shard_map/product/pallas_call | solution.py:254
  140.5 11.3 %all-to-all-start.2 = ((f32[32,2,2,4,128]{4,3,2,1,0:T(4,128)}), f32[32,2,2,4,128]{4,3,2,1,0:T(4,128)S(1)}, u32[]{:S(2)}, u32[]{:S(2)}) async-start(f32[32,2,2,4,128]{4,3,2,1,0:T(4,128)} %bitcast.10), calls=%async_computation.2 | async-start | bytes 524288 | tf_op jit(solution)/shard_map/all_to_all | solution.py:273
  151.8 0.1 select_reduce_fusion.1
  152.0 11.6 %all-to-all-done.2 = f32[32,2,2,4,128]{4,3,2,1,0:T(4,128)S(1)} async-done(((f32[32,2,2,4,128]{4,3,2,1,0:T(4,128)}), f32[32,2,2,4,128]{4,3,2,1,0:T(4,128)S(1)}, u32[]{:S(2)}, u32[]{:S(2)}) %all-to-all-start.2) | async-done | bytes 262176 | tf_op jit(solution)/shard_map/all_to_all | solution.py:273
  163.6 1.2 sum_over_xyz.1
  164.8 7.0 %all-to-all-start.3 = ((f32[16,2,2,4,128]{4,3,2,1,0:T(4,128)}), f32[16,2,2,4,128]{4,3,2,1,0:T(4,128)S(1)}, u32[]{:S(2)}, u32[]{:S(2)}) async-start(f32[16,2,2,4,128]{4,3,2,1,0:T(4,128)} %bitcast.12), calls=%async_computation.3 | async-start | bytes 262144 | tf_op jit(solution)/shard_map/all_to_all | solution.py:285
  171.9 0.1 dynamic_slice.3.order_ref
  171.9 13.8 %all-to-all-done.3 = f32[16,2,2,4,128]{4,3,2,1,0:T(4,128)S(1)} async-done(((f32[16,2,2,4,128]{4,3,2,1,0:T(4,128)}), f32[16,2,2,4,128]{4,3,2,1,0:T(4,128)S(1)}, u32[]{:S(2)}, u32[]{:S(2)}) %all-to-all-start.3) | async-done | bytes 131104 | tf_op jit(solution)/shard_map/all_to_all | solution.py:285
  185.7 1.3 final.1
  (4 shorter events, 0.0 us)
Async XLA Ops:
  0.0 45.8 %copy-start = (s32[32]{0:T(128)S(1)}, s32[32]{0:T(128)}, u32[]{:S(2)}) copy-start(s32[32]{0:T(128)} %param.6) | copy-start | bytes 388
  2.1 82.6 %all-to-all-start = ((f32[16,96,128]{2,1,0:T(8,128)}), f32[16,96,128]{2,1,0:T(8,128)S(1)}, u32[]{:S(2)}, u32[]{:S(2)}) async-start(f32[16,96,128]{2,1,0:T(8,128)} %share.1), calls=%async_computation | async-start | bytes 1572864 | tf_op jit(solution)/shard_map/all_to_all | solution.py:227
  84.7 9.6 %copy-start.1 = (s32[32]{0:T(128)S(1)}, s32[32]{0:T(128)}, u32[]{:S(2)}) copy-start(s32[32]{0:T(128)} %param.7) | copy-start | bytes 388
  86.4 46.7 %all-to-all-start.1 = ((f32[16,96,128]{2,1,0:T(8,128)}), f32[16,96,128]{2,1,0:T(8,128)S(1)}, u32[]{:S(2)}, u32[]{:S(2)}) async-start(f32[16,96,128]{2,1,0:T(8,128)} %bitcast.5), calls=%async_computation.1 | async-start | bytes 1572864 | tf_op jit(solution)/shard_map/all_to_all | solution.py:229
  133.1 4.3 %collective-permute-start = (f32[1536,128]{1,0:T(8,128)S(1)}, f32[1536,128]{1,0:T(8,128)}, u32[]{:S(2)}, u32[]{:S(2)}) collective-permute-start(f32[1536,128]{1,0:T(8,128)S(1)} %bitcast.19), channel_id=1, source_target_pairs={{0,1},{1,0},{2,3},{3,2},{4,5},{5,4},{6,7},{7,6},{8,9},{9,8},{10,11... | collective-permute-start | bytes 2359304 | tf_op jit(solution)/shard_map/ppermute | solution.py:250
  140.5 23.0 %all-to-all-start.2 = ((f32[32,2,2,4,128]{4,3,2,1,0:T(4,128)}), f32[32,2,2,4,128]{4,3,2,1,0:T(4,128)S(1)}, u32[]{:S(2)}, u32[]{:S(2)}) async-start(f32[32,2,2,4,128]{4,3,2,1,0:T(4,128)} %bitcast.10), calls=%async_computation.2 | async-start | bytes 524288 | tf_op jit(solution)/shard_map/all_to_all | solution.py:273
  164.8 20.9 %all-to-all-start.3 = ((f32[16,2,2,4,128]{4,3,2,1,0:T(4,128)}), f32[16,2,2,4,128]{4,3,2,1,0:T(4,128)S(1)}, u32[]{:S(2)}, u32[]{:S(2)}) async-start(f32[16,2,2,4,128]{4,3,2,1,0:T(4,128)} %bitcast.12), calls=%async_computation.3 | async-start | bytes 262144 | tf_op jit(solution)/shard_map/all_to_all | solution.py:285

commit v9 on v7

--- a/solution.py
+++ b/solution.py
@@ -114,8 +114,8 @@
 
 def product_kernel(parts, tl, v_ref, *refs):
     p_hi, p_lo = refs[:tl], refs[tl : 2 * tl]
-    out_hbm, a_ref, b_ref, out_ref, out_sem = refs[2 * tl :]
-    _, nq, nx, nsrc, piece, width = out_ref.shape
+    out_ref, a_ref, b_ref = refs[2 * tl :]
+    nq, nx, nsrc, _, piece, width = out_ref.shape
     cols = p_hi[0].shape[2] // LANES
     half = a_ref.shape[1] // 4
     nz = half // parts
@@ -127,7 +127,6 @@
 
     stride = tl * parts * cols * 2
     per = half // nx
-    sends = []
     for t in range(tl):
         for i in range(parts):
             for b in range(cols):
@@ -150,13 +149,9 @@
             for x in range(nx):
                 first = ri * half + x * per + part * piece
                 for slot in range(nsrc):
-                    out_ref[t, q, x, slot] = total[
+                    out_ref[q, x, slot, t] = total[
                         first : first + piece, slot * width : (slot + 1) * width
                     ]
-        sends.append(pltpu.make_async_copy(out_ref.at[t], out_hbm.at[:, :, :, t], out_sem.at[t]))
-        sends[-1].start()
-    for send in sends:
-        send.wait()
 
 
 def sum_kernel(index_ref, in_ref, out_ref, held):
@@ -230,10 +225,6 @@
         eigvecs.transpose(0, 1, 3, 2, 4).reshape(rows, part, fold, nsrc, per_x, *tail),
     )
     spread = lax.all_to_all(share, TA, 0, 0, tiled=True)
-    picked = pick_rows(spread.reshape(nta * rows, lines, LANES), rank)
-    sent = lax.all_to_all(picked.reshape(nta, tl * lines, LANES), TA, 0, 0, tiled=True)
-    sent = sent.reshape(nta * tl * lines, LANES)
-
     inverse = inverse_of(source_ids - n * core)
     held = spinors.at[inverse].get(mode="promise_in_bounds")
     held = held.transpose(1, 2, 3, 0, 4, 5).reshape(tl, 2, ns * n, nc * sites)
@@ -251,24 +242,29 @@
         name="split",
     )(core[None], held, other)
 
+    here = jnp.clip(ordering - (ta // near) * (near * tl), 0, near * tl - 1)
+    wanted = lax.dynamic_slice_in_dim(ordering, ta * rows, rows, 0)
+    spread, rank, here, wanted, *cut = lax.optimization_barrier(
+        (spread, rank, here, wanted, *cut)
+    )
+
+    picked = pick_rows(spread.reshape(nta * rows, lines, LANES), rank)
+    sent = lax.all_to_all(picked.reshape(nta, tl * lines, LANES), TA, 0, 0, tiled=True)
+    sent = sent.reshape(nta * tl * lines, LANES)
+
     piece = 2 * per_x // near
     pair = pl.pallas_call(
         functools.partial(product_kernel, part, tl),
         out_shape=jax.ShapeDtypeStruct((near, nx, nsrc, tl, piece, ns * n), jnp.float32),
         in_specs=[vmem] * (1 + 2 * tl),
-        out_specs=pl.BlockSpec(memory_space=pltpu.HBM),
-        scratch_shapes=[pltpu.VMEM((tl, 4 * mine, wide), jnp.bfloat16)] * 2
-        + [
-            pltpu.VMEM((tl, near, nx, nsrc, piece, ns * n), jnp.float32),
-            pltpu.SemaphoreType.DMA((tl,)),
-        ],
+        out_specs=vmem,
+        scratch_shapes=[pltpu.VMEM((tl, 4 * mine, wide), jnp.bfloat16)] * 2,
         compiler_params=small(12),
         name="product",
     )(sent, *cut)
 
     pair = pair.reshape(near * nx * nsrc, tl, piece, ns * n)
     got = lax.all_to_all(pair, ("tp", "xyz", "src"), 0, 0, tiled=True)
-    here = jnp.clip(ordering - (ta // near) * (near * tl), 0, near * tl - 1)
     back = pl.pallas_call(
         sum_kernel,
         out_shape=jax.ShapeDtypeStruct((nta * rows, nsrc, piece, ns * n), jnp.float32),
@@ -281,7 +277,6 @@
 
     home = lax.all_to_all(back.reshape(nta, rows, nsrc, piece, ns * n), TA, 0, 0, tiled=True)
     home = home.reshape(nta // near, near, rows, nsrc, piece, ns * n)
-    wanted = lax.dynamic_slice_in_dim(ordering, ta * rows, rows, 0)
     out = pl.pallas_call(
         functools.partial(final_kernel, near * tl),
         out_shape=jax.ShapeDtypeStruct((rows, 2, ns, nsrc * per_x, n), jnp.float32),

time: 186 us -> 182 us (0.978)
  blocking collectives: 0 us -> 91.8 us
  waiting for transfers between devices: 90.1 us -> 25.3 us
  starting transfers between devices: 73.4 us -> 45.6 us
    all_to_all x0 -> x3, blocking collectives: none -> 91.8 us  [the longest x1 48.7 us: local(): lax.all_to_all(picked.reshape(nta, tl * lines, LANES), TA, 0, 0, tiled=True)]
    all_to_all x3 -> x0, waiting for transfers between devices: 47.9 us -> none  [the longest x1 22.2 us: local(): lax.all_to_all(picked.reshape(nta, tl * lines, LANES), TA, 0, 0, tiled=True)]
    all_to_all x3 -> x0, starting transfers between devices: 27.7 us -> none  [the longest x1 12.8 us: local(): got = lax.all_to_all(pair, ('tp', 'xyz', 'src'), 0, 0, tiled=True)]
    all_to_all x1, waiting for transfers between devices: 38.7 us -> 22.2 us  [local(): spread = lax.all_to_all(share, TA, 0, 0, tiled=True)]
  transfers between devices with their start and end apart: 5 -> 2, of which waited for: 5 -> 2; matrix products, arithmetic and copies ran while one was open for 4% -> 5% of each run, Pallas kernels for 1% -> 1%
where the time goes in v9:
time: 182 us
  blocking collectives  91.8 us (50%)
  starting transfers between devices  45.6 us (25%)
  waiting for transfers between devices  25.3 us (14%)
  Pallas kernels  9.9 us (5%)
  local copies, waits for them, and re-layouts  8.7 us (5%)
    all_to_all x1, blocking collectives, local(): lax.all_to_all(picked.reshape(nta, tl * lines, LANES), TA, 0, 0, tiled=True)  48.7 us
    all_to_all x1, starting transfers between devices, local(): spread = lax.all_to_all(share, TA, 0, 0, tiled=True)  43.7 us
    all_to_all x1, blocking collectives, local(): got = lax.all_to_all(pair, ('tp', 'xyz', 'src'), 0, 0, tiled=True)  23.9 us
    all_to_all x1, waiting for transfers between devices, local(): spread = lax.all_to_all(share, TA, 0, 0, tiled=True)  22.2 us
    all_to_all x1, blocking collectives, local(): lax.all_to_all(back.reshape(nta, rows, nsrc, piece, ns * n), TA, 0, 0, ti...  19.2 us
  transfers between devices with their start and end apart: 2, of which 2 were waited for; matrix products, arithmetic and copies ran while one was open for 5% of the time, Pallas kernels for 1%

profile of v9, /device:TPU:80, one launch (start us, length us, event | category | flops | bytes accessed | tf_op | source)
XLA Modules:
  0.0 181.9 jit_solution(12625525796915653156)
XLA Ops:
  0.0 0.0 copy-start.3
  0.0 2.1 %share.1 = f32[16,96,128]{2,1,0:T(8,128)} custom-call(s32[1]{0:T(128)} %bitcast.core_ref, f32[2,4,2,2,8,3,2,256]{7,6,5,4,3,2,1,0:T(2,128)} %bitcast.25), custom_call_target="tpu_custom_call" | custom-call | tf_op jit(solution)/shard_map/share/pallas_call | solution.py:208
  2.1 43.7 %all-to-all-start = ((f32[16,96,128]{2,1,0:T(8,128)}), f32[16,96,128]{2,1,0:T(8,128)S(1)}, u32[]{:S(2)}, u32[]{:S(2)}) async-start(f32[16,96,128]{2,1,0:T(8,128)} %share.1), calls=%async_computation | async-start | bytes 1572864 | tf_op jit(solution)/shard_map/all_to_all | solution.py:227
  45.8 0.0 copy-done.3
  45.8 0.1 select_reduce_fusion
  46.0 2.9 %gather_fusion = f32[32,2,2,4,3,256]{5,3,4,2,1,0:T(4,128)S(1)} fusion(f32[32,2,2,4,3,256]{5,3,4,2,1,0:T(4,128)} %param.4, s32[1024]{0:T(1024)S(1)} %pad_clamp_fusion), kind=kCustom, calls=%fused_computation | custom fusion | bytes 3145856 | tf_op jit(solution)/shard_map/gather | solution.py:229
  48.9 1.9 %copy.7 = f32[2,2,4,32,3,256]{5,4,3,2,1,0:T(4,128)} copy(f32[2,2,4,32,3,256]{5,2,4,1,0,3:T(4,128)S(1)} %bitcast.24) | data formatting | bytes 3145728 | tf_op jit(solution)/shard_map/transpose | solution.py:230
  50.8 0.0 copy-start.4
  50.8 2.9 %reshape.45.own_ref = f32[2,2,128,768]{3,2,1,0:T(8,128)S(1)} reshape(f32[2,2,4,32,3,256]{5,4,3,2,1,0:T(4,128)} %copy.7) | data formatting | bytes 3145728 | tf_op jit(solution)/shard_map/reshape | solution.py:230
  53.7 0.0 copy-start.2
  53.7 2.0 %collective-permute-start = (f32[2,2,128,768]{3,2,1,0:T(8,128)S(1)}, f32[2,2,128,768]{3,2,1,0:T(8,128)}, u32[]{:S(2)}, u32[]{:S(2)}) collective-permute-start(f32[2,2,128,768]{3,2,1,0:T(8,128)S(1)} %reshape.45.own_ref), channel_id=1, source_target_pairs={{0,1},{1,0},{2,3},{3,2},{4,5},{5,4},{6,7},{7,6},{8,9},{9,8},{10,11... | collective-permute-start | bytes 4718600 | tf_op jit(solution)/shard_map/ppermute | solution.py:231
  55.7 0.0 copy-done.4
  55.7 0.2 convert_reduce_fusion.index_ref
  55.9 0.1 select_reduce_fusion.1
  56.0 0.1 dynamic_slice.3.order_ref
  56.1 0.0 copy-done.2
  56.1 3.1 %collective-permute-done.other_ref = f32[2,2,128,768]{3,2,1,0:T(8,128)} collective-permute-done((f32[2,2,128,768]{3,2,1,0:T(8,128)S(1)}, f32[2,2,128,768]{3,2,1,0:T(8,128)}, u32[]{:S(2)}, u32[]{:S(2)}) %collective-permute-start) | collective-permute-done | bytes 1572896 | tf_op jit(solution)/shard_map/ppermute | solution.py:231
  59.2 2.4 %split.1 = (bf16[2,256,768]{2,1,0:T(8,128)(2,1)S(1)}, bf16[2,256,768]{2,1,0:T(8,128)(2,1)S(1)}, bf16[2,256,768]{2,1,0:T(8,128)(2,1)S(1)}, bf16[2,256,768]{2,1,0:T(8,128)(2,1)S(1)}) custom-call(s32[1]{0:T(128)} %bitcast.core_ref, f32[2,2,128,768]{3,2,1,0:T(8,128)} %copy-done.2, f32[2,2,128,768]{3,2,1,0:T(8,128)} %collective-permute-done.other_ref), custom_call_target="tpu_custom_call" | custom-call | tf_op jit(solution)/shard_map/split/pallas_call | solution.py:236
  61.6 0.0 copy-start
  61.6 0.9 copy-done
  62.5 22.2 %all-to-all-done = f32[16,96,128]{2,1,0:T(8,128)S(1)} async-done(((f32[16,96,128]{2,1,0:T(8,128)}), f32[16,96,128]{2,1,0:T(8,128)S(1)}, u32[]{:S(2)}, u32[]{:S(2)}) %all-to-all-start) | async-done | bytes 786464 | tf_op jit(solution)/shard_map/all_to_all | solution.py:227
  84.7 0.0 copy-start.1
  84.7 2.0 %pick_rows.1 = f32[32,48,128]{2,1,0:T(8,128)S(1)} custom-call(s32[32]{0:T(128)S(1)} %convert_reduce_fusion.index_ref, f32[32,48,128]{2,1,0:T(8,128)S(1)} %bitcast.18), custom_call_target="tpu_custom_call" | custom-call | tf_op jit(solution)/shard_map/pick_rows/pallas_call | solution.py:83
  86.7 48.7 %all_to_all.20 = f32[16,96,128]{2,1,0:T(8,128)S(1)} all-to-all(f32[16,96,128]{2,1,0:T(8,128)S(1)} %bitcast.19), channel_id=1, replica_groups=mesh['job'=2,'tq'=4,'tp'=4,'xyz'=8,'src'=2] {'tq','tp'}, dimensions={0} | all-to-all | bytes 1572864 | tf_op jit(solution)/shard_map/all_to_all | solution.py:252
  135.4 0.0 copy-done.1
  135.5 1.5 product.1
  136.9 23.9 %all_to_all.21 = f32[64,2,4,128]{3,2,1,0:T(4,128)S(1)} all-to-all(f32[64,2,4,128]{3,2,1,0:T(4,128)S(1)} %bitcast.20), channel_id=1, replica_groups=mesh['job'=2,'tq'=4,'tp'=4,'xyz'=8,'src'=2] {'tp','xyz','src'}, dimensions={0} | all-to-all | bytes 524288 | tf_op jit(solution)/shard_map/all_to_all | solution.py:267
  160.8 0.6 sum_over_xyz.1
  161.4 19.2 %all_to_all.22 = f32[16,2,2,4,128]{4,3,2,1,0:T(4,128)S(1)} all-to-all(f32[16,2,2,4,128]{4,3,2,1,0:T(4,128)S(1)} %bitcast.22), channel_id=1, replica_groups=mesh['job'=2,'tq'=4,'tp'=4,'xyz'=8,'src'=2] {'tq','tp'}, dimensions={0} | all-to-all | bytes 262144 | tf_op jit(solution)/shard_map/all_to_all | solution.py:278
  180.6 1.3 final.1
  (4 shorter events, 0.0 us)
Async XLA Ops:
  0.0 45.8 %copy-start.3 = (s32[32]{0:T(128)S(1)}, s32[32]{0:T(128)}, u32[]{:S(2)}) copy-start(s32[32]{0:T(128)} %param.7) | copy-start | bytes 388
  2.1 82.6 %all-to-all-start = ((f32[16,96,128]{2,1,0:T(8,128)}), f32[16,96,128]{2,1,0:T(8,128)S(1)}, u32[]{:S(2)}, u32[]{:S(2)}) async-start(f32[16,96,128]{2,1,0:T(8,128)} %share.1), calls=%async_computation | async-start | bytes 1572864 | tf_op jit(solution)/shard_map/all_to_all | solution.py:227
  50.8 4.9 %copy-start.4 = (s32[32]{0:T(128)S(1)}, s32[32]{0:T(128)}, u32[]{:S(2)}) copy-start(s32[32]{0:T(128)} %param.6) | copy-start | bytes 388
  53.7 2.4 %copy-start.2 = (f32[2,2,128,768]{3,2,1,0:T(8,128)}, f32[2,2,128,768]{3,2,1,0:T(8,128)S(1)}, u32[]{:S(2)}) copy-start(f32[2,2,128,768]{3,2,1,0:T(8,128)S(1)} %reshape.45.own_ref) | copy-start | bytes 4718596
  53.7 5.5 %collective-permute-start = (f32[2,2,128,768]{3,2,1,0:T(8,128)S(1)}, f32[2,2,128,768]{3,2,1,0:T(8,128)}, u32[]{:S(2)}, u32[]{:S(2)}) collective-permute-start(f32[2,2,128,768]{3,2,1,0:T(8,128)S(1)} %reshape.45.own_ref), channel_id=1, source_target_pairs={{0,1},{1,0},{2,3},{3,2},{4,5},{5,4},{6,7},{7,6},{8,9},{9,8},{10,11... | collective-permute-start | bytes 4718600 | tf_op jit(solution)/shard_map/ppermute | solution.py:231
  61.6 0.9 copy-start
  84.7 50.8 %copy-start.1 = (bf16[2,256,768]{2,1,0:T(8,128)(2,1)S(1)}, bf16[2,256,768]{2,1,0:T(8,128)(2,1)}, u32[]{:S(2)}) copy-start(bf16[2,256,768]{2,1,0:T(8,128)(2,1)} %copy-done) | copy-start | bytes 2359300

commit v10 on v9

--- a/solution.py
+++ b/solution.py
@@ -66,16 +66,9 @@
         send.wait()
 
 
-def pick_rows_kernel(index_ref, table_ref, out_ref, sem):
-    count = out_ref.shape[0]
-    copies = [
-        pltpu.make_async_copy(table_ref.at[index_ref[i]], out_ref.at[i], sem.at[i])
-        for i in range(count)
-    ]
-    for copy in copies:
-        copy.start()
-    for copy in copies:
-        copy.wait()
+def pick_rows_kernel(index_ref, table_ref, out_ref):
+    for i in range(out_ref.shape[0]):
+        out_ref[i] = table_ref[index_ref[i]]
 
 
 def pick_rows(table, index):
@@ -87,8 +80,7 @@
             pl.BlockSpec(memory_space=pltpu.SMEM),
             pl.BlockSpec(memory_space=pltpu.VMEM),
         ],
-        out_specs=pl.BlockSpec(memory_space=pl.ANY),
-        scratch_shapes=[pltpu.SemaphoreType.DMA((count,))],
+        out_specs=pl.BlockSpec(memory_space=pltpu.VMEM),
         compiler_params=small(4),
         name="pick_rows",
     )(index, table)

time: 182 us -> 181 us (level)
  no operation moved by 1% of the time
where the time goes in v10:
time: 181 us
  blocking collectives  91.8 us (51%)
  starting transfers between devices  45.6 us (25%)
  waiting for transfers between devices  25.3 us (14%)
  local copies, waits for them, and re-layouts  8.7 us (5%)
  Pallas kernels  8.5 us (5%)
    all_to_all x1, blocking collectives, local(): lax.all_to_all(picked.reshape(nta, tl * lines, LANES), TA, 0, 0, tiled=True)  48.7 us
    all_to_all x1, starting transfers between devices, local(): spread = lax.all_to_all(share, TA, 0, 0, tiled=True)  43.7 us
    all_to_all x1, blocking collectives, local(): got = lax.all_to_all(pair, ('tp', 'xyz', 'src'), 0, 0, tiled=True)  23.9 us
    all_to_all x1, waiting for transfers between devices, local(): spread = lax.all_to_all(share, TA, 0, 0, tiled=True)  22.2 us
    all_to_all x1, blocking collectives, local(): lax.all_to_all(back.reshape(nta, rows, nsrc, piece, ns * n), TA, 0, 0, ti...  19.2 us
  transfers between devices with their start and end apart: 2, of which 2 were waited for; matrix products, arithmetic and copies ran while one was open for 5% of the time, Pallas kernels for 1%

profile of v10, /device:TPU:80, one launch (start us, length us, event | category | flops | bytes accessed | tf_op | source)
XLA Modules:
  0.0 180.5 jit_solution(12532133770853333148)
XLA Ops:
  0.0 0.0 copy-start.3
  0.0 2.1 %share.1 = f32[16,96,128]{2,1,0:T(8,128)} custom-call(s32[1]{0:T(128)} %bitcast.core_ref, f32[2,4,2,2,8,3,2,256]{7,6,5,4,3,2,1,0:T(2,128)} %bitcast.25), custom_call_target="tpu_custom_call" | custom-call | tf_op jit(solution)/shard_map/share/pallas_call | solution.py:200
  2.1 43.7 %all-to-all-start = ((f32[16,96,128]{2,1,0:T(8,128)}), f32[16,96,128]{2,1,0:T(8,128)S(1)}, u32[]{:S(2)}, u32[]{:S(2)}) async-start(f32[16,96,128]{2,1,0:T(8,128)} %share.1), calls=%async_computation | async-start | bytes 1572864 | tf_op jit(solution)/shard_map/all_to_all | solution.py:219
  45.8 0.0 copy-done.3
  45.8 0.1 select_reduce_fusion
  46.0 2.9 %gather_fusion = f32[32,2,2,4,3,256]{5,3,4,2,1,0:T(4,128)S(1)} fusion(f32[32,2,2,4,3,256]{5,3,4,2,1,0:T(4,128)} %param.4, s32[1024]{0:T(1024)S(1)} %pad_clamp_fusion), kind=kCustom, calls=%fused_computation | custom fusion | bytes 3145856 | tf_op jit(solution)/shard_map/gather | solution.py:221
  48.9 1.9 %copy.7 = f32[2,2,4,32,3,256]{5,4,3,2,1,0:T(4,128)} copy(f32[2,2,4,32,3,256]{5,2,4,1,0,3:T(4,128)S(1)} %bitcast.24) | data formatting | bytes 3145728 | tf_op jit(solution)/shard_map/transpose | solution.py:222
  50.8 0.0 copy-start.4
  50.8 2.9 %reshape.45.own_ref = f32[2,2,128,768]{3,2,1,0:T(8,128)S(1)} reshape(f32[2,2,4,32,3,256]{5,4,3,2,1,0:T(4,128)} %copy.7) | data formatting | bytes 3145728 | tf_op jit(solution)/shard_map/reshape | solution.py:222
  53.7 0.0 copy-start.2
  53.7 2.0 %collective-permute-start = (f32[2,2,128,768]{3,2,1,0:T(8,128)S(1)}, f32[2,2,128,768]{3,2,1,0:T(8,128)}, u32[]{:S(2)}, u32[]{:S(2)}) collective-permute-start(f32[2,2,128,768]{3,2,1,0:T(8,128)S(1)} %reshape.45.own_ref), channel_id=1, source_target_pairs={{0,1},{1,0},{2,3},{3,2},{4,5},{5,4},{6,7},{7,6},{8,9},{9,8},{10,11... | collective-permute-start | bytes 4718600 | tf_op jit(solution)/shard_map/ppermute | solution.py:223
  55.7 0.0 copy-done.4
  55.7 0.2 convert_reduce_fusion.index_ref
  55.9 0.1 select_reduce_fusion.1
  56.0 0.1 dynamic_slice.3.order_ref
  56.1 0.0 copy-done.2
  56.1 3.1 %collective-permute-done.other_ref = f32[2,2,128,768]{3,2,1,0:T(8,128)} collective-permute-done((f32[2,2,128,768]{3,2,1,0:T(8,128)S(1)}, f32[2,2,128,768]{3,2,1,0:T(8,128)}, u32[]{:S(2)}, u32[]{:S(2)}) %collective-permute-start) | collective-permute-done | bytes 1572896 | tf_op jit(solution)/shard_map/ppermute | solution.py:223
  59.2 2.4 %split.1 = (bf16[2,256,768]{2,1,0:T(8,128)(2,1)S(1)}, bf16[2,256,768]{2,1,0:T(8,128)(2,1)S(1)}, bf16[2,256,768]{2,1,0:T(8,128)(2,1)S(1)}, bf16[2,256,768]{2,1,0:T(8,128)(2,1)S(1)}) custom-call(s32[1]{0:T(128)} %bitcast.core_ref, f32[2,2,128,768]{3,2,1,0:T(8,128)} %copy-done.2, f32[2,2,128,768]{3,2,1,0:T(8,128)} %collective-permute-done.other_ref), custom_call_target="tpu_custom_call" | custom-call | tf_op jit(solution)/shard_map/split/pallas_call | solution.py:228
  61.6 0.0 copy-start
  61.6 0.9 copy-done
  62.5 22.2 %all-to-all-done = f32[16,96,128]{2,1,0:T(8,128)S(1)} async-done(((f32[16,96,128]{2,1,0:T(8,128)}), f32[16,96,128]{2,1,0:T(8,128)S(1)}, u32[]{:S(2)}, u32[]{:S(2)}) %all-to-all-start) | async-done | bytes 786464 | tf_op jit(solution)/shard_map/all_to_all | solution.py:219
  84.7 0.0 copy-start.1
  84.7 0.6 pick_rows.1
  85.3 48.7 %all_to_all.20 = f32[16,96,128]{2,1,0:T(8,128)S(1)} all-to-all(f32[16,96,128]{2,1,0:T(8,128)S(1)} %bitcast.19), channel_id=1, replica_groups=mesh['job'=2,'tq'=4,'tp'=4,'xyz'=8,'src'=2] {'tq','tp'}, dimensions={0} | all-to-all | bytes 1572864 | tf_op jit(solution)/shard_map/all_to_all | solution.py:244
  134.1 0.0 copy-done.1
  134.1 1.5 product.1
  135.5 23.9 %all_to_all.21 = f32[64,2,4,128]{3,2,1,0:T(4,128)S(1)} all-to-all(f32[64,2,4,128]{3,2,1,0:T(4,128)S(1)} %bitcast.20), channel_id=1, replica_groups=mesh['job'=2,'tq'=4,'tp'=4,'xyz'=8,'src'=2] {'tp','xyz','src'}, dimensions={0} | all-to-all | bytes 524288 | tf_op jit(solution)/shard_map/all_to_all | solution.py:259
  159.4 0.6 sum_over_xyz.1
  160.0 19.2 %all_to_all.22 = f32[16,2,2,4,128]{4,3,2,1,0:T(4,128)S(1)} all-to-all(f32[16,2,2,4,128]{4,3,2,1,0:T(4,128)S(1)} %bitcast.22), channel_id=1, replica_groups=mesh['job'=2,'tq'=4,'tp'=4,'xyz'=8,'src'=2] {'tq','tp'}, dimensions={0} | all-to-all | bytes 262144 | tf_op jit(solution)/shard_map/all_to_all | solution.py:270
  179.2 1.3 final.1
  (4 shorter events, 0.0 us)
Async XLA Ops:
  0.0 45.8 %copy-start.3 = (s32[32]{0:T(128)S(1)}, s32[32]{0:T(128)}, u32[]{:S(2)}) copy-start(s32[32]{0:T(128)} %param.7) | copy-start | bytes 388
  2.1 82.6 %all-to-all-start = ((f32[16,96,128]{2,1,0:T(8,128)}), f32[16,96,128]{2,1,0:T(8,128)S(1)}, u32[]{:S(2)}, u32[]{:S(2)}) async-start(f32[16,96,128]{2,1,0:T(8,128)} %share.1), calls=%async_computation | async-start | bytes 1572864 | tf_op jit(solution)/shard_map/all_to_all | solution.py:219
  50.8 4.9 %copy-start.4 = (s32[32]{0:T(128)S(1)}, s32[32]{0:T(128)}, u32[]{:S(2)}) copy-start(s32[32]{0:T(128)} %param.6) | copy-start | bytes 388
  53.7 2.4 %copy-start.2 = (f32[2,2,128,768]{3,2,1,0:T(8,128)}, f32[2,2,128,768]{3,2,1,0:T(8,128)S(1)}, u32[]{:S(2)}) copy-start(f32[2,2,128,768]{3,2,1,0:T(8,128)S(1)} %reshape.45.own_ref) | copy-start | bytes 4718596
  53.7 5.5 %collective-permute-start = (f32[2,2,128,768]{3,2,1,0:T(8,128)S(1)}, f32[2,2,128,768]{3,2,1,0:T(8,128)}, u32[]{:S(2)}, u32[]{:S(2)}) collective-permute-start(f32[2,2,128,768]{3,2,1,0:T(8,128)S(1)} %reshape.45.own_ref), channel_id=1, source_target_pairs={{0,1},{1,0},{2,3},{3,2},{4,5},{5,4},{6,7},{7,6},{8,9},{9,8},{10,11... | collective-permute-start | bytes 4718600 | tf_op jit(solution)/shard_map/ppermute | solution.py:223
  61.6 0.9 copy-start
  84.7 49.4 %copy-start.1 = (bf16[2,256,768]{2,1,0:T(8,128)(2,1)S(1)}, bf16[2,256,768]{2,1,0:T(8,128)(2,1)}, u32[]{:S(2)}) copy-start(bf16[2,256,768]{2,1,0:T(8,128)(2,1)} %copy-done) | copy-start | bytes 2359300

commit v11 on v10

--- a/solution.py
+++ b/solution.py
@@ -177,7 +177,7 @@
 
 
 TA = ("tq", "tp")
-NEAR = 4
+NEAR = 2
 
 
 def local(spinors, eigvecs, group_of, source_ids):

time: 181 us -> 181 us (level)
    all_to_all x1, blocking collectives: 19.2 us -> 23.8 us  [local(): lax.all_to_all(back.reshape(nta, rows, nsrc, piece, ns * n), TA, 0, 0, ti...]
    all_to_all x1, blocking collectives: 23.9 us -> 19.8 us  [local(): got = lax.all_to_all(pair, ('tp', 'xyz', 'src'), 0, 0, tiled=True)]
where the time goes in v11:
time: 181 us
  blocking collectives  92.3 us (51%)
  starting transfers between devices  45.6 us (25%)
  waiting for transfers between devices  25.3 us (14%)
  local copies, waits for them, and re-layouts  8.7 us (5%)
  Pallas kernels  8.46 us (5%)
    all_to_all x1, blocking collectives, local(): lax.all_to_all(picked.reshape(nta, tl * lines, LANES), TA, 0, 0, tiled=True)  48.7 us
    all_to_all x1, starting transfers between devices, local(): spread = lax.all_to_all(share, TA, 0, 0, tiled=True)  43.7 us
    all_to_all x1, blocking collectives, local(): lax.all_to_all(back.reshape(nta, rows, nsrc, piece, ns * n), TA, 0, 0, ti...  23.8 us
    all_to_all x1, waiting for transfers between devices, local(): spread = lax.all_to_all(share, TA, 0, 0, tiled=True)  22.2 us
    all_to_all x1, blocking collectives, local(): got = lax.all_to_all(pair, ('tp', 'xyz', 'src'), 0, 0, tiled=True)  19.8 us
  transfers between devices with their start and end apart: 2, of which 2 were waited for; matrix products, arithmetic and copies ran while one was open for 5% of the time, Pallas kernels for 1%

profile of v11, /device:TPU:80, one launch (start us, length us, event | category | flops | bytes accessed | tf_op | source)
XLA Modules:
  0.0 181.0 jit_solution(7033451821131044864)
XLA Ops:
  0.0 0.0 copy-start.3
  0.0 2.1 %share.1 = f32[16,96,128]{2,1,0:T(8,128)} custom-call(s32[1]{0:T(128)} %bitcast.core_ref, f32[2,4,2,2,8,3,2,256]{7,6,5,4,3,2,1,0:T(2,128)} %bitcast.25), custom_call_target="tpu_custom_call" | custom-call | tf_op jit(solution)/shard_map/share/pallas_call | solution.py:200
  2.1 43.7 %all-to-all-start = ((f32[16,96,128]{2,1,0:T(8,128)}), f32[16,96,128]{2,1,0:T(8,128)S(1)}, u32[]{:S(2)}, u32[]{:S(2)}) async-start(f32[16,96,128]{2,1,0:T(8,128)} %share.1), calls=%async_computation | async-start | bytes 1572864 | tf_op jit(solution)/shard_map/all_to_all | solution.py:219
  45.8 0.0 copy-done.3
  45.8 0.1 select_reduce_fusion
  46.0 2.9 %gather_fusion = f32[32,2,2,4,3,256]{5,3,4,2,1,0:T(4,128)S(1)} fusion(f32[32,2,2,4,3,256]{5,3,4,2,1,0:T(4,128)} %param.4, s32[1024]{0:T(1024)S(1)} %pad_clamp_fusion), kind=kCustom, calls=%fused_computation | custom fusion | bytes 3145856 | tf_op jit(solution)/shard_map/gather | solution.py:221
  48.9 1.9 %copy.7 = f32[2,2,4,32,3,256]{5,4,3,2,1,0:T(4,128)} copy(f32[2,2,4,32,3,256]{5,2,4,1,0,3:T(4,128)S(1)} %bitcast.24) | data formatting | bytes 3145728 | tf_op jit(solution)/shard_map/transpose | solution.py:222
  50.8 0.0 copy-start.4
  50.8 2.9 %reshape.45.own_ref = f32[2,2,128,768]{3,2,1,0:T(8,128)S(1)} reshape(f32[2,2,4,32,3,256]{5,4,3,2,1,0:T(4,128)} %copy.7) | data formatting | bytes 3145728 | tf_op jit(solution)/shard_map/reshape | solution.py:222
  53.7 0.0 copy-start.2
  53.7 2.0 %collective-permute-start = (f32[2,2,128,768]{3,2,1,0:T(8,128)S(1)}, f32[2,2,128,768]{3,2,1,0:T(8,128)}, u32[]{:S(2)}, u32[]{:S(2)}) collective-permute-start(f32[2,2,128,768]{3,2,1,0:T(8,128)S(1)} %reshape.45.own_ref), channel_id=1, source_target_pairs={{0,1},{1,0},{2,3},{3,2},{4,5},{5,4},{6,7},{7,6},{8,9},{9,8},{10,11... | collective-permute-start | bytes 4718600 | tf_op jit(solution)/shard_map/ppermute | solution.py:223
  55.7 0.0 copy-done.4
  55.7 0.2 convert_reduce_fusion.index_ref
  55.9 0.1 select_reduce_fusion.1
  56.0 0.1 dynamic_slice.3.order_ref
  56.1 0.0 copy-done.2
  56.1 3.1 %collective-permute-done.other_ref = f32[2,2,128,768]{3,2,1,0:T(8,128)} collective-permute-done((f32[2,2,128,768]{3,2,1,0:T(8,128)S(1)}, f32[2,2,128,768]{3,2,1,0:T(8,128)}, u32[]{:S(2)}, u32[]{:S(2)}) %collective-permute-start) | collective-permute-done | bytes 1572896 | tf_op jit(solution)/shard_map/ppermute | solution.py:223
  59.2 2.4 %split.1 = (bf16[2,256,768]{2,1,0:T(8,128)(2,1)S(1)}, bf16[2,256,768]{2,1,0:T(8,128)(2,1)S(1)}, bf16[2,256,768]{2,1,0:T(8,128)(2,1)S(1)}, bf16[2,256,768]{2,1,0:T(8,128)(2,1)S(1)}) custom-call(s32[1]{0:T(128)} %bitcast.core_ref, f32[2,2,128,768]{3,2,1,0:T(8,128)} %copy-done.2, f32[2,2,128,768]{3,2,1,0:T(8,128)} %collective-permute-done.other_ref), custom_call_target="tpu_custom_call" | custom-call | tf_op jit(solution)/shard_map/split/pallas_call | solution.py:228
  61.6 0.0 copy-start
  61.6 0.9 copy-done
  62.5 22.2 %all-to-all-done = f32[16,96,128]{2,1,0:T(8,128)S(1)} async-done(((f32[16,96,128]{2,1,0:T(8,128)}), f32[16,96,128]{2,1,0:T(8,128)S(1)}, u32[]{:S(2)}, u32[]{:S(2)}) %all-to-all-start) | async-done | bytes 786464 | tf_op jit(solution)/shard_map/all_to_all | solution.py:219
  84.7 0.0 copy-start.1
  84.7 0.6 pick_rows.1
  85.3 48.7 %all_to_all.20 = f32[16,96,128]{2,1,0:T(8,128)S(1)} all-to-all(f32[16,96,128]{2,1,0:T(8,128)S(1)} %bitcast.19), channel_id=1, replica_groups=mesh['job'=2,'tq'=8,'tp'=2,'xyz'=8,'src'=2] {'tq','tp'}, dimensions={0} | all-to-all | bytes 1572864 | tf_op jit(solution)/shard_map/all_to_all | solution.py:244
  134.1 0.0 copy-done.1
  134.1 1.5 product.1
  135.5 19.8 %all_to_all.21 = f32[32,2,8,128]{3,2,1,0:T(8,128)S(1)} all-to-all(f32[32,2,8,128]{3,2,1,0:T(8,128)S(1)} %bitcast.20), channel_id=1, replica_groups=mesh['job'=2,'tq'=8,'tp'=2,'xyz'=8,'src'=2] {'tp','xyz','src'}, dimensions={0} | all-to-all | bytes 524288 | tf_op jit(solution)/shard_map/all_to_all | solution.py:259
  155.3 0.6 sum_over_xyz.1
  155.9 23.8 %all_to_all.22 = f32[16,2,2,8,128]{4,3,2,1,0:T(8,128)S(1)} all-to-all(f32[16,2,2,8,128]{4,3,2,1,0:T(8,128)S(1)} %bitcast.22), channel_id=1, replica_groups=mesh['job'=2,'tq'=8,'tp'=2,'xyz'=8,'src'=2] {'tq','tp'}, dimensions={0} | all-to-all | bytes 524288 | tf_op jit(solution)/shard_map/all_to_all | solution.py:270
  179.7 1.3 final.1
  (4 shorter events, 0.0 us)
Async XLA Ops:
  0.0 45.8 %copy-start.3 = (s32[32]{0:T(128)S(1)}, s32[32]{0:T(128)}, u32[]{:S(2)}) copy-start(s32[32]{0:T(128)} %param.7) | copy-start | bytes 388
  2.1 82.6 %all-to-all-start = ((f32[16,96,128]{2,1,0:T(8,128)}), f32[16,96,128]{2,1,0:T(8,128)S(1)}, u32[]{:S(2)}, u32[]{:S(2)}) async-start(f32[16,96,128]{2,1,0:T(8,128)} %share.1), calls=%async_computation | async-start | bytes 1572864 | tf_op jit(solution)/shard_map/all_to_all | solution.py:219
  50.8 4.9 %copy-start.4 = (s32[32]{0:T(128)S(1)}, s32[32]{0:T(128)}, u32[]{:S(2)}) copy-start(s32[32]{0:T(128)} %param.6) | copy-start | bytes 388
  53.7 2.4 %copy-start.2 = (f32[2,2,128,768]{3,2,1,0:T(8,128)}, f32[2,2,128,768]{3,2,1,0:T(8,128)S(1)}, u32[]{:S(2)}) copy-start(f32[2,2,128,768]{3,2,1,0:T(8,128)S(1)} %reshape.45.own_ref) | copy-start | bytes 4718596
  53.7 5.5 %collective-permute-start = (f32[2,2,128,768]{3,2,1,0:T(8,128)S(1)}, f32[2,2,128,768]{3,2,1,0:T(8,128)}, u32[]{:S(2)}, u32[]{:S(2)}) collective-permute-start(f32[2,2,128,768]{3,2,1,0:T(8,128)S(1)} %reshape.45.own_ref), channel_id=1, source_target_pairs={{0,1},{1,0},{2,3},{3,2},{4,5},{5,4},{6,7},{7,6},{8,9},{9,8},{10,11... | collective-permute-start | bytes 4718600 | tf_op jit(solution)/shard_map/ppermute | solution.py:223
  61.6 0.9 copy-start
  84.7 49.4 %copy-start.1 = (bf16[2,256,768]{2,1,0:T(8,128)(2,1)S(1)}, bf16[2,256,768]{2,1,0:T(8,128)(2,1)}, u32[]{:S(2)}) copy-start(bf16[2,256,768]{2,1,0:T(8,128)(2,1)} %copy-done) | copy-start | bytes 2359300

commit v12 on v10

--- a/solution.py
+++ b/solution.py
@@ -148,6 +148,7 @@
 
 def sum_kernel(index_ref, in_ref, out_ref, held):
     near, nx, nsrc, tl = in_ref.shape[:4]
+    nta, _, rows = out_ref.shape[:3]
     for z in range(near):
         total = in_ref[z, 0]
         for x in range(1, nx):
@@ -155,12 +156,15 @@
         for t in range(tl):
             for core in range(nsrc):
                 held[z * tl + t, core] = total[core, t]
-    for row in range(out_ref.shape[0]):
-        out_ref[row] = held[index_ref[row]]
+    for ta in range(nta):
+        for row in range(rows):
+            value = held[index_ref[ta * rows + row]]
+            for core in range(nsrc):
+                out_ref[ta, core, row] = value[core]
 
 
 def final_kernel(per_group, order_ref, in_ref, out_ref):
-    _, nq, rows, nsrc, piece, _ = in_ref.shape
+    _, nq, nsrc, rows, piece, _ = in_ref.shape
     ns, n = out_ref.shape[2], out_ref.shape[4]
     parts = nq // 2
     for row in range(rows):
@@ -168,7 +172,7 @@
         for core in range(nsrc):
             for ri in range(2):
                 for part in range(parts):
-                    value = in_ref[group, ri * parts + part, row, core]
+                    value = in_ref[group, ri * parts + part, core, row]
                     first = (core * parts + part) * piece
                     for s in range(ns):
                         out_ref[row, ri, s, first : first + piece, :] = value[
@@ -255,11 +259,11 @@
         name="product",
     )(sent, *cut)
 
-    pair = pair.reshape(near * nx * nsrc, tl, piece, ns * n)
-    got = lax.all_to_all(pair, ("tp", "xyz", "src"), 0, 0, tiled=True)
+    pair = pair.reshape(near * nx, nsrc, tl, piece, ns * n)
+    got = lax.all_to_all(pair, ("tp", "xyz"), 0, 0, tiled=True)
     back = pl.pallas_call(
         sum_kernel,
-        out_shape=jax.ShapeDtypeStruct((nta * rows, nsrc, piece, ns * n), jnp.float32),
+        out_shape=jax.ShapeDtypeStruct((nta, nsrc, rows, piece, ns * n), jnp.float32),
         in_specs=[smem, vmem],
         out_specs=vmem,
         scratch_shapes=[pltpu.VMEM((near * tl, nsrc, piece, ns * n), jnp.float32)],
@@ -267,8 +271,9 @@
         name="sum_over_xyz",
     )(here, got.reshape(near, nx, nsrc, tl, piece, ns * n))
 
-    home = lax.all_to_all(back.reshape(nta, rows, nsrc, piece, ns * n), TA, 0, 0, tiled=True)
-    home = home.reshape(nta // near, near, rows, nsrc, piece, ns * n)
+    back = back.reshape(nta * nsrc, rows, piece, ns * n)
+    home = lax.all_to_all(back, (*TA, "src"), 0, 0, tiled=True)
+    home = home.reshape(nta // near, near, nsrc, rows, piece, ns * n)
     out = pl.pallas_call(
         functools.partial(final_kernel, near * tl),
         out_shape=jax.ShapeDtypeStruct((rows, 2, ns, nsrc * per_x, n), jnp.float32),

time: 181 us -> 182 us (level)
  no operation moved by 1% of the time
where the time goes in v12:
time: 182 us
  blocking collectives  92.9 us (51%)
  starting transfers between devices  45.6 us (25%)
  waiting for transfers between devices  25.3 us (14%)
  local copies, waits for them, and re-layouts  8.7 us (5%)
  Pallas kernels  8.51 us (5%)
    all_to_all x1, blocking collectives, local(): lax.all_to_all(picked.reshape(nta, tl * lines, LANES), TA, 0, 0, tiled=True)  48.7 us
    all_to_all x1, starting transfers between devices, local(): spread = lax.all_to_all(share, TA, 0, 0, tiled=True)  43.7 us
    all_to_all x1, blocking collectives, local(): home = lax.all_to_all(back, (*TA, 'src'), 0, 0, tiled=True)  22.5 us
    all_to_all x1, waiting for transfers between devices, local(): spread = lax.all_to_all(share, TA, 0, 0, tiled=True)  22.2 us
    all_to_all x1, blocking collectives, local(): got = lax.all_to_all(pair, ('tp', 'xyz'), 0, 0, tiled=True)  21.6 us
  transfers between devices with their start and end apart: 2, of which 2 were waited for; matrix products, arithmetic and copies ran while one was open for 5% of the time, Pallas kernels for 1%

profile of v12, /device:TPU:80, one launch (start us, length us, event | category | flops | bytes accessed | tf_op | source)
XLA Modules:
  0.0 181.6 jit_solution(16092539016063576160)
XLA Ops:
  0.0 0.0 copy-start.3
  0.0 2.1 %share.1 = f32[16,96,128]{2,1,0:T(8,128)} custom-call(s32[1]{0:T(128)} %bitcast.core_ref, f32[2,4,2,2,8,3,2,256]{7,6,5,4,3,2,1,0:T(2,128)} %bitcast.25), custom_call_target="tpu_custom_call" | custom-call | tf_op jit(solution)/shard_map/share/pallas_call | solution.py:204
  2.1 43.7 %all-to-all-start = ((f32[16,96,128]{2,1,0:T(8,128)}), f32[16,96,128]{2,1,0:T(8,128)S(1)}, u32[]{:S(2)}, u32[]{:S(2)}) async-start(f32[16,96,128]{2,1,0:T(8,128)} %share.1), calls=%async_computation | async-start | bytes 1572864 | tf_op jit(solution)/shard_map/all_to_all | solution.py:223
  45.8 0.0 copy-done.3
  45.8 0.1 select_reduce_fusion
  46.0 2.9 %gather_fusion = f32[32,2,2,4,3,256]{5,3,4,2,1,0:T(4,128)S(1)} fusion(f32[32,2,2,4,3,256]{5,3,4,2,1,0:T(4,128)} %param.4, s32[1024]{0:T(1024)S(1)} %pad_clamp_fusion), kind=kCustom, calls=%fused_computation | custom fusion | bytes 3145856 | tf_op jit(solution)/shard_map/gather | solution.py:225
  48.9 1.9 %copy.7 = f32[2,2,4,32,3,256]{5,4,3,2,1,0:T(4,128)} copy(f32[2,2,4,32,3,256]{5,2,4,1,0,3:T(4,128)S(1)} %bitcast.24) | data formatting | bytes 3145728 | tf_op jit(solution)/shard_map/transpose | solution.py:226
  50.8 0.0 copy-start.4
  50.8 2.9 %reshape.45.own_ref = f32[2,2,128,768]{3,2,1,0:T(8,128)S(1)} reshape(f32[2,2,4,32,3,256]{5,4,3,2,1,0:T(4,128)} %copy.7) | data formatting | bytes 3145728 | tf_op jit(solution)/shard_map/reshape | solution.py:226
  53.7 0.0 copy-start.2
  53.7 2.0 %collective-permute-start = (f32[2,2,128,768]{3,2,1,0:T(8,128)S(1)}, f32[2,2,128,768]{3,2,1,0:T(8,128)}, u32[]{:S(2)}, u32[]{:S(2)}) collective-permute-start(f32[2,2,128,768]{3,2,1,0:T(8,128)S(1)} %reshape.45.own_ref), channel_id=1, source_target_pairs={{0,1},{1,0},{2,3},{3,2},{4,5},{5,4},{6,7},{7,6},{8,9},{9,8},{10,11... | collective-permute-start | bytes 4718600 | tf_op jit(solution)/shard_map/ppermute | solution.py:227
  55.7 0.0 copy-done.4
  55.7 0.2 convert_reduce_fusion.index_ref
  55.9 0.1 select_reduce_fusion.1
  56.0 0.1 dynamic_slice.3.order_ref
  56.1 0.0 copy-done.2
  56.1 3.1 %collective-permute-done.other_ref = f32[2,2,128,768]{3,2,1,0:T(8,128)} collective-permute-done((f32[2,2,128,768]{3,2,1,0:T(8,128)S(1)}, f32[2,2,128,768]{3,2,1,0:T(8,128)}, u32[]{:S(2)}, u32[]{:S(2)}) %collective-permute-start) | collective-permute-done | bytes 1572896 | tf_op jit(solution)/shard_map/ppermute | solution.py:227
  59.2 2.4 %split.1 = (bf16[2,256,768]{2,1,0:T(8,128)(2,1)S(1)}, bf16[2,256,768]{2,1,0:T(8,128)(2,1)S(1)}, bf16[2,256,768]{2,1,0:T(8,128)(2,1)S(1)}, bf16[2,256,768]{2,1,0:T(8,128)(2,1)S(1)}) custom-call(s32[1]{0:T(128)} %bitcast.core_ref, f32[2,2,128,768]{3,2,1,0:T(8,128)} %copy-done.2, f32[2,2,128,768]{3,2,1,0:T(8,128)} %collective-permute-done.other_ref), custom_call_target="tpu_custom_call" | custom-call | tf_op jit(solution)/shard_map/split/pallas_call | solution.py:232
  61.6 0.0 copy-start
  61.6 0.9 copy-done
  62.5 22.2 %all-to-all-done = f32[16,96,128]{2,1,0:T(8,128)S(1)} async-done(((f32[16,96,128]{2,1,0:T(8,128)}), f32[16,96,128]{2,1,0:T(8,128)S(1)}, u32[]{:S(2)}, u32[]{:S(2)}) %all-to-all-start) | async-done | bytes 786464 | tf_op jit(solution)/shard_map/all_to_all | solution.py:223
  84.7 0.0 copy-start.1
  84.7 0.6 pick_rows.1
  85.3 48.7 %all_to_all.20 = f32[16,96,128]{2,1,0:T(8,128)S(1)} all-to-all(f32[16,96,128]{2,1,0:T(8,128)S(1)} %bitcast.19), channel_id=1, replica_groups=mesh['job'=2,'tq'=4,'tp'=4,'xyz'=8,'src'=2] {'tq','tp'}, dimensions={0} | all-to-all | bytes 1572864 | tf_op jit(solution)/shard_map/all_to_all | solution.py:248
  134.1 0.0 copy-done.1
  134.1 1.5 product.1
  135.5 21.6 %all_to_all.21 = f32[32,2,2,4,128]{4,3,2,1,0:T(4,128)S(1)} all-to-all(f32[32,2,2,4,128]{4,3,2,1,0:T(4,128)S(1)} %bitcast.20), channel_id=1, replica_groups=mesh['job'=2,'tq'=4,'tp'=4,'xyz'=8,'src'=2] {'tp','xyz'}, dimensions={0} | all-to-all | bytes 524288 | tf_op jit(solution)/shard_map/all_to_all | solution.py:263
  157.2 0.6 sum_over_xyz.1
  157.8 22.5 %all_to_all.22 = f32[32,2,4,128]{3,2,1,0:T(4,128)S(1)} all-to-all(f32[32,2,4,128]{3,2,1,0:T(4,128)S(1)} %bitcast.22), channel_id=1, replica_groups=mesh['job'=2,'tq'=4,'tp'=4,'xyz'=8,'src'=2] {'tq','tp','src'}, dimensions={0} | all-to-all | bytes 262144 | tf_op jit(solution)/shard_map/all_to_all | solution.py:275
  180.3 1.3 final.1
  (4 shorter events, 0.0 us)
Async XLA Ops:
  0.0 45.8 %copy-start.3 = (s32[32]{0:T(128)S(1)}, s32[32]{0:T(128)}, u32[]{:S(2)}) copy-start(s32[32]{0:T(128)} %param.7) | copy-start | bytes 388
  2.1 82.6 %all-to-all-start = ((f32[16,96,128]{2,1,0:T(8,128)}), f32[16,96,128]{2,1,0:T(8,128)S(1)}, u32[]{:S(2)}, u32[]{:S(2)}) async-start(f32[16,96,128]{2,1,0:T(8,128)} %share.1), calls=%async_computation | async-start | bytes 1572864 | tf_op jit(solution)/shard_map/all_to_all | solution.py:223
  50.8 4.9 %copy-start.4 = (s32[32]{0:T(128)S(1)}, s32[32]{0:T(128)}, u32[]{:S(2)}) copy-start(s32[32]{0:T(128)} %param.6) | copy-start | bytes 388
  53.7 2.4 %copy-start.2 = (f32[2,2,128,768]{3,2,1,0:T(8,128)}, f32[2,2,128,768]{3,2,1,0:T(8,128)S(1)}, u32[]{:S(2)}) copy-start(f32[2,2,128,768]{3,2,1,0:T(8,128)S(1)} %reshape.45.own_ref) | copy-start | bytes 4718596
  53.7 5.5 %collective-permute-start = (f32[2,2,128,768]{3,2,1,0:T(8,128)S(1)}, f32[2,2,128,768]{3,2,1,0:T(8,128)}, u32[]{:S(2)}, u32[]{:S(2)}) collective-permute-start(f32[2,2,128,768]{3,2,1,0:T(8,128)S(1)} %reshape.45.own_ref), channel_id=1, source_target_pairs={{0,1},{1,0},{2,3},{3,2},{4,5},{5,4},{6,7},{7,6},{8,9},{9,8},{10,11... | collective-permute-start | bytes 4718600 | tf_op jit(solution)/shard_map/ppermute | solution.py:227
  61.6 0.9 copy-start
  84.7 49.4 %copy-start.1 = (bf16[2,256,768]{2,1,0:T(8,128)(2,1)S(1)}, bf16[2,256,768]{2,1,0:T(8,128)(2,1)}, u32[]{:S(2)}) copy-start(bf16[2,256,768]{2,1,0:T(8,128)(2,1)} %copy-done) | copy-start | bytes 2359300

commit v13 on v10

--- a/solution.py
+++ b/solution.py
@@ -193,7 +193,6 @@
     fold = nta // per_x
 
     rank = rank_of(group_of)
-    ordering = inverse_of(rank)
 
     tail = (nc, 2, sites)
     lines = part * nc * 2 * sites // LANES
@@ -234,15 +233,16 @@
         name="split",
     )(core[None], held, other)
 
-    here = jnp.clip(ordering - (ta // near) * (near * tl), 0, near * tl - 1)
-    wanted = lax.dynamic_slice_in_dim(ordering, ta * rows, rows, 0)
-    spread, rank, here, wanted, *cut = lax.optimization_barrier(
-        (spread, rank, here, wanted, *cut)
-    )
+    spread, rank, *cut = lax.optimization_barrier((spread, rank, *cut))
 
     picked = pick_rows(spread.reshape(nta * rows, lines, LANES), rank)
     sent = lax.all_to_all(picked.reshape(nta, tl * lines, LANES), TA, 0, 0, tiled=True)
     sent = sent.reshape(nta * tl * lines, LANES)
+
+    order = inverse_of(rank)
+    here = jnp.clip(order - (ta // near) * (near * tl), 0, near * tl - 1)
+    wanted = lax.dynamic_slice_in_dim(order, ta * rows, rows, 0)
+    sent, here, wanted = lax.optimization_barrier((sent, here, wanted))
 
     piece = 2 * per_x // near
     pair = pl.pallas_call(

time: 181 us -> 184 us (1.017)
  blocking collectives: 91.8 us -> 45.4 us
  waiting for transfers between devices: 25.3 us -> 61.5 us
  starting transfers between devices: 45.6 us -> 53.6 us
  local copies, waits for them, and re-layouts: 8.7 us -> 12.5 us
    all_to_all x1 -> x0, blocking collectives: 48.7 us -> none  [local(): lax.all_to_all(picked.reshape(nta, tl * lines, LANES), TA, 0, 0, tiled=True)]
    all_to_all x0 -> x1, waiting for transfers between devices: none -> 38.7 us  [local(): lax.all_to_all(picked.reshape(nta, tl * lines, LANES), TA, 0, 0, tiled=True)]
    all_to_all x0 -> x1, starting transfers between devices: none -> 7.95 us  [local(): lax.all_to_all(picked.reshape(nta, tl * lines, LANES), TA, 0, 0, tiled=True)]
    unnamed x10 -> x22, local copies, waits for them, and re-layouts: 0.89 us -> 4.69 us
    all_to_all x1, waiting for transfers between devices: 22.2 us -> 19.5 us  [local(): spread = lax.all_to_all(share, TA, 0, 0, tiled=True)]
    all_to_all x1, blocking collectives: 19.2 us -> 21.4 us  [local(): lax.all_to_all(back.reshape(nta, rows, nsrc, piece, ns * n), TA, 0, 0, ti...]
  transfers between devices with their start and end apart: 2 -> 3, of which waited for: 2 -> 3; matrix products, arithmetic and copies ran while one was open for 5% -> 4% of each run, Pallas kernels for 1% -> 1%
where the time goes in v13:
time: 184 us; the launch traced here: 183 us
  waiting for transfers between devices  61.5 us (33%)
  starting transfers between devices  53.6 us (29%)
  blocking collectives  45.4 us (25%)
  local copies, waits for them, and re-layouts  12.5 us (7%)
  Pallas kernels  9.38 us (5%)
    all_to_all x1, starting transfers between devices, local(): spread = lax.all_to_all(share, TA, 0, 0, tiled=True)  43.7 us
    all_to_all x1, waiting for transfers between devices, local(): lax.all_to_all(picked.reshape(nta, tl * lines, LANES), TA, 0, 0, tiled=True)  38.7 us
    all_to_all x1, blocking collectives, local(): got = lax.all_to_all(pair, ('tp', 'xyz', 'src'), 0, 0, tiled=True)  24 us
    all_to_all x1, blocking collectives, local(): lax.all_to_all(back.reshape(nta, rows, nsrc, piece, ns * n), TA, 0, 0, ti...  21.4 us
    all_to_all x1, waiting for transfers between devices, local(): spread = lax.all_to_all(share, TA, 0, 0, tiled=True)  19.5 us
    all_to_all x1, starting transfers between devices, local(): lax.all_to_all(picked.reshape(nta, tl * lines, LANES), TA, 0, 0, tiled=True)  7.95 us
    unnamed x22, local copies, waits for them, and re-layouts  4.69 us
  transfers between devices with their start and end apart: 3, of which 3 were waited for; matrix products, arithmetic and copies ran while one was open for 4% of the time, Pallas kernels for 1%

profile of v13, /device:TPU:80, one launch (start us, length us, event | category | flops | bytes accessed | tf_op | source)
XLA Modules:
  0.0 183.0 jit_solution(76677336901977235)
XLA Ops:
  0.0 2.1 %share.1 = f32[16,96,128]{2,1,0:T(8,128)} custom-call(s32[1]{0:T(128)} %bitcast.core_ref, f32[2,4,2,2,8,3,2,256]{7,6,5,4,3,2,1,0:T(2,128)} %bitcast.24), custom_call_target="tpu_custom_call" | custom-call | tf_op jit(solution)/shard_map/share/pallas_call | solution.py:199
  2.1 43.7 %all-to-all-start = ((f32[16,96,128]{2,1,0:T(8,128)}), f32[16,96,128]{2,1,0:T(8,128)S(1)}, u32[]{:S(2)}, u32[]{:S(2)}) async-start(f32[16,96,128]{2,1,0:T(8,128)} %share.1), calls=%async_computation | async-start | bytes 1572864 | tf_op jit(solution)/shard_map/all_to_all | solution.py:218
  45.8 0.0 copy-done.9
  45.8 0.1 select_reduce_fusion.1
  46.0 2.9 %gather_fusion = f32[32,2,2,4,3,256]{5,3,4,2,1,0:T(4,128)S(1)} fusion(f32[32,2,2,4,3,256]{5,3,4,2,1,0:T(4,128)} %param.4, s32[1024]{0:T(1024)S(1)} %pad_clamp_fusion), kind=kCustom, calls=%fused_computation | custom fusion | bytes 3145856 | tf_op jit(solution)/shard_map/gather | solution.py:220
  48.9 1.9 %copy.7 = f32[2,2,4,32,3,256]{5,4,3,2,1,0:T(4,128)} copy(f32[2,2,4,32,3,256]{5,2,4,1,0,3:T(4,128)S(1)} %bitcast.23) | data formatting | bytes 3145728 | tf_op jit(solution)/shard_map/transpose | solution.py:221
  50.8 2.9 %reshape.45.own_ref = f32[2,2,128,768]{3,2,1,0:T(8,128)S(1)} reshape(f32[2,2,4,32,3,256]{5,4,3,2,1,0:T(4,128)} %copy.7) | data formatting | bytes 3145728 | tf_op jit(solution)/shard_map/reshape | solution.py:221
  53.7 0.0 copy-start.8
  53.7 2.0 %collective-permute-start = (f32[2,2,128,768]{3,2,1,0:T(8,128)S(1)}, f32[2,2,128,768]{3,2,1,0:T(8,128)}, u32[]{:S(2)}, u32[]{:S(2)}) collective-permute-start(f32[2,2,128,768]{3,2,1,0:T(8,128)S(1)} %reshape.45.own_ref), channel_id=1, source_target_pairs={{0,1},{1,0},{2,3},{3,2},{4,5},{5,4},{6,7},{7,6},{8,9},{9,8},{10,11... | collective-permute-start | bytes 4718600 | tf_op jit(solution)/shard_map/ppermute | solution.py:222
  55.7 0.0 copy-done.10
  55.7 0.2 convert_reduce_fusion.index_ref
  55.9 0.0 copy-done.8
  55.9 3.3 %collective-permute-done.other_ref = f32[2,2,128,768]{3,2,1,0:T(8,128)} collective-permute-done((f32[2,2,128,768]{3,2,1,0:T(8,128)S(1)}, f32[2,2,128,768]{3,2,1,0:T(8,128)}, u32[]{:S(2)}, u32[]{:S(2)}) %collective-permute-start) | collective-permute-done | bytes 1572896 | tf_op jit(solution)/shard_map/ppermute | solution.py:222
  59.2 2.4 %split.1 = (bf16[2,256,768]{2,1,0:T(8,128)(2,1)S(1)}, bf16[2,256,768]{2,1,0:T(8,128)(2,1)S(1)}, bf16[2,256,768]{2,1,0:T(8,128)(2,1)S(1)}, bf16[2,256,768]{2,1,0:T(8,128)(2,1)S(1)}) custom-call(s32[1]{0:T(128)} %bitcast.core_ref, f32[2,2,128,768]{3,2,1,0:T(8,128)} %copy-done.8, f32[2,2,128,768]{3,2,1,0:T(8,128)} %collective-permute-done.other_ref), custom_call_target="tpu_custom_call" | custom-call | tf_op jit(solution)/shard_map/split/pallas_call | solution.py:227
  61.6 0.0 copy-start
  61.6 0.9 copy-done
  62.5 0.9 copy-done.2
  63.4 0.9 copy-done.4
  64.3 0.9 copy-done.6
  65.2 19.5 %all-to-all-done = f32[16,96,128]{2,1,0:T(8,128)S(1)} async-done(((f32[16,96,128]{2,1,0:T(8,128)}), f32[16,96,128]{2,1,0:T(8,128)S(1)}, u32[]{:S(2)}, u32[]{:S(2)}) %all-to-all-start) | async-done | bytes 786464 | tf_op jit(solution)/shard_map/all_to_all | solution.py:218
  84.7 1.5 pick_rows.1
  86.2 7.9 %all-to-all-start.1 = ((f32[16,96,128]{2,1,0:T(8,128)}), f32[16,96,128]{2,1,0:T(8,128)S(1)}, u32[]{:S(2)}, u32[]{:S(2)}) async-start(f32[16,96,128]{2,1,0:T(8,128)} %bitcast.7), calls=%async_computation.1 | async-start | bytes 1572864 | tf_op jit(solution)/shard_map/all_to_all | solution.py:239
  94.1 0.1 select_reduce_fusion
  94.3 0.1 dynamic_slice.3.order_ref
  94.3 38.7 %all-to-all-done.1 = f32[16,96,128]{2,1,0:T(8,128)S(1)} async-done(((f32[16,96,128]{2,1,0:T(8,128)}), f32[16,96,128]{2,1,0:T(8,128)S(1)}, u32[]{:S(2)}, u32[]{:S(2)}) %all-to-all-start.1) | async-done | bytes 786464 | tf_op jit(solution)/shard_map/all_to_all | solution.py:239
  133.0 0.0 copy-done.3
  133.0 1.1 copy-done.7
  134.2 1.5 product.1
  135.6 24.0 %all_to_all.20 = f32[64,2,4,128]{3,2,1,0:T(4,128)S(1)} all-to-all(f32[64,2,4,128]{3,2,1,0:T(4,128)S(1)} %bitcast.19), channel_id=1, replica_groups=mesh['job'=2,'tq'=4,'tp'=4,'xyz'=8,'src'=2] {'tp','xyz','src'}, dimensions={0} | all-to-all | bytes 524288 | tf_op jit(solution)/shard_map/all_to_all | solution.py:259
  159.6 0.6 sum_over_xyz.1
  160.2 21.4 %all_to_all.21 = f32[16,2,2,4,128]{4,3,2,1,0:T(4,128)S(1)} all-to-all(f32[16,2,2,4,128]{4,3,2,1,0:T(4,128)S(1)} %bitcast.21), channel_id=1, replica_groups=mesh['job'=2,'tq'=4,'tp'=4,'xyz'=8,'src'=2] {'tq','tp'}, dimensions={0} | all-to-all | bytes 262144 | tf_op jit(solution)/shard_map/all_to_all | solution.py:270
  181.7 1.3 final.1
  (15 shorter events, 0.0 us)
Async XLA Ops:
  0.0 45.8 %copy-start.9 = (s32[32]{0:T(128)S(1)}, s32[32]{0:T(128)}, u32[]{:S(2)}) copy-start(s32[32]{0:T(128)} %param.7) | copy-start | bytes 388
  2.1 82.6 %all-to-all-start = ((f32[16,96,128]{2,1,0:T(8,128)}), f32[16,96,128]{2,1,0:T(8,128)S(1)}, u32[]{:S(2)}, u32[]{:S(2)}) async-start(f32[16,96,128]{2,1,0:T(8,128)} %share.1), calls=%async_computation | async-start | bytes 1572864 | tf_op jit(solution)/shard_map/all_to_all | solution.py:218
  50.8 4.9 %copy-start.10 = (s32[32]{0:T(128)S(1)}, s32[32]{0:T(128)}, u32[]{:S(2)}) copy-start(s32[32]{0:T(128)} %param.6) | copy-start | bytes 388
  53.7 2.2 %copy-start.8 = (f32[2,2,128,768]{3,2,1,0:T(8,128)}, f32[2,2,128,768]{3,2,1,0:T(8,128)S(1)}, u32[]{:S(2)}) copy-start(f32[2,2,128,768]{3,2,1,0:T(8,128)S(1)} %reshape.45.own_ref) | copy-start | bytes 4718596
  53.7 5.5 %collective-permute-start = (f32[2,2,128,768]{3,2,1,0:T(8,128)S(1)}, f32[2,2,128,768]{3,2,1,0:T(8,128)}, u32[]{:S(2)}, u32[]{:S(2)}) collective-permute-start(f32[2,2,128,768]{3,2,1,0:T(8,128)S(1)} %reshape.45.own_ref), channel_id=1, source_target_pairs={{0,1},{1,0},{2,3},{3,2},{4,5},{5,4},{6,7},{7,6},{8,9},{9,8},{10,11... | collective-permute-start | bytes 4718600 | tf_op jit(solution)/shard_map/ppermute | solution.py:222
  61.6 0.9 copy-start
  62.5 0.9 copy-start.2
  63.4 0.9 copy-start.4
  64.3 0.9 copy-start.6
  84.7 48.3 %copy-start.1 = (bf16[2,256,768]{2,1,0:T(8,128)(2,1)S(1)}, bf16[2,256,768]{2,1,0:T(8,128)(2,1)}, u32[]{:S(2)}) copy-start(bf16[2,256,768]{2,1,0:T(8,128)(2,1)} %copy-done) | copy-start | bytes 2359300
  84.7 48.3 %copy-start.3 = (bf16[2,256,768]{2,1,0:T(8,128)(2,1)S(1)}, bf16[2,256,768]{2,1,0:T(8,128)(2,1)}, u32[]{:S(2)}) copy-start(bf16[2,256,768]{2,1,0:T(8,128)(2,1)} %copy-done.2) | copy-start | bytes 2359300
  86.2 46.8 %copy-start.5 = (bf16[2,256,768]{2,1,0:T(8,128)(2,1)S(1)}, bf16[2,256,768]{2,1,0:T(8,128)(2,1)}, u32[]{:S(2)}) copy-start(bf16[2,256,768]{2,1,0:T(8,128)(2,1)} %copy-done.4) | copy-start | bytes 2359300
  86.2 46.8 %all-to-all-start.1 = ((f32[16,96,128]{2,1,0:T(8,128)}), f32[16,96,128]{2,1,0:T(8,128)S(1)}, u32[]{:S(2)}, u32[]{:S(2)}) async-start(f32[16,96,128]{2,1,0:T(8,128)} %bitcast.7), calls=%async_computation.1 | async-start | bytes 1572864 | tf_op jit(solution)/shard_map/all_to_all | solution.py:239
  133.0 1.1 copy-start.7

commit v14 on v10

--- a/solution.py
+++ b/solution.py
@@ -107,7 +107,7 @@
 def product_kernel(parts, tl, v_ref, *refs):
     p_hi, p_lo = refs[:tl], refs[tl : 2 * tl]
     out_ref, a_ref, b_ref = refs[2 * tl :]
-    nq, nx, nsrc, _, piece, width = out_ref.shape
+    nx, nq, nsrc, _, piece, width = out_ref.shape
     cols = p_hi[0].shape[2] // LANES
     half = a_ref.shape[1] // 4
     nz = half // parts
@@ -141,17 +141,17 @@
             for x in range(nx):
                 first = ri * half + x * per + part * piece
                 for slot in range(nsrc):
-                    out_ref[q, x, slot, t] = total[
+                    out_ref[x, q, slot, t] = total[
                         first : first + piece, slot * width : (slot + 1) * width
                     ]
 
 
 def sum_kernel(index_ref, in_ref, out_ref, held):
-    near, nx, nsrc, tl = in_ref.shape[:4]
+    nx, near, nsrc, tl = in_ref.shape[:4]
     for z in range(near):
-        total = in_ref[z, 0]
+        total = in_ref[0, z]
         for x in range(1, nx):
-            total += in_ref[z, x]
+            total += in_ref[x, z]
         for t in range(tl):
             for core in range(nsrc):
                 held[z * tl + t, core] = total[core, t]
@@ -247,7 +247,7 @@
     piece = 2 * per_x // near
     pair = pl.pallas_call(
         functools.partial(product_kernel, part, tl),
-        out_shape=jax.ShapeDtypeStruct((near, nx, nsrc, tl, piece, ns * n), jnp.float32),
+        out_shape=jax.ShapeDtypeStruct((nx, near, nsrc, tl, piece, ns * n), jnp.float32),
         in_specs=[vmem] * (1 + 2 * tl),
         out_specs=vmem,
         scratch_shapes=[pltpu.VMEM((tl, 4 * mine, wide), jnp.bfloat16)] * 2,
@@ -255,8 +255,8 @@
         name="product",
     )(sent, *cut)
 
-    pair = pair.reshape(near * nx * nsrc, tl, piece, ns * n)
-    got = lax.all_to_all(pair, ("tp", "xyz", "src"), 0, 0, tiled=True)
+    pair = pair.reshape(nx * near * nsrc, tl, piece, ns * n)
+    got = lax.all_to_all(pair, ("xyz", "tp", "src"), 0, 0, tiled=True)
     back = pl.pallas_call(
         sum_kernel,
         out_shape=jax.ShapeDtypeStruct((nta * rows, nsrc, piece, ns * n), jnp.float32),
@@ -265,7 +265,7 @@
         scratch_shapes=[pltpu.VMEM((near * tl, nsrc, piece, ns * n), jnp.float32)],
         compiler_params=small(4),
         name="sum_over_xyz",
-    )(here, got.reshape(near, nx, nsrc, tl, piece, ns * n))
+    )(here, got.reshape(nx, near, nsrc, tl, piece, ns * n))
 
     home = lax.all_to_all(back.reshape(nta, rows, nsrc, piece, ns * n), TA, 0, 0, tiled=True)
     home = home.reshape(nta // near, near, rows, nsrc, piece, ns * n)

time: 181 us -> 182 us (level)
  no operation moved by 1% of the time
where the time goes in v14:
time: 182 us
  blocking collectives  92.9 us (51%)
  starting transfers between devices  45.6 us (25%)
  waiting for transfers between devices  25.3 us (14%)
  local copies, waits for them, and re-layouts  8.7 us (5%)
  Pallas kernels  8.5 us (5%)
    all_to_all x1, blocking collectives, local(): lax.all_to_all(picked.reshape(nta, tl * lines, LANES), TA, 0, 0, tiled=True)  48.7 us
    all_to_all x1, starting transfers between devices, local(): spread = lax.all_to_all(share, TA, 0, 0, tiled=True)  43.7 us
    all_to_all x1, blocking collectives, local(): got = lax.all_to_all(pair, ('xyz', 'tp', 'src'), 0, 0, tiled=True)  24.6 us
    all_to_all x1, waiting for transfers between devices, local(): spread = lax.all_to_all(share, TA, 0, 0, tiled=True)  22.2 us
    all_to_all x1, blocking collectives, local(): lax.all_to_all(back.reshape(nta, rows, nsrc, piece, ns * n), TA, 0, 0, ti...  19.6 us
  transfers between devices with their start and end apart: 2, of which 2 were waited for; matrix products, arithmetic and copies ran while one was open for 5% of the time, Pallas kernels for 1%

profile of v14, /device:TPU:80, one launch (start us, length us, event | category | flops | bytes accessed | tf_op | source)
XLA Modules:
  0.0 181.6 jit_solution(1421208026984400793)
XLA Ops:
  0.0 0.0 copy-start.3
  0.0 2.1 %share.1 = f32[16,96,128]{2,1,0:T(8,128)} custom-call(s32[1]{0:T(128)} %bitcast.core_ref, f32[2,4,2,2,8,3,2,256]{7,6,5,4,3,2,1,0:T(2,128)} %bitcast.25), custom_call_target="tpu_custom_call" | custom-call | tf_op jit(solution)/shard_map/share/pallas_call | solution.py:200
  2.1 43.7 %all-to-all-start = ((f32[16,96,128]{2,1,0:T(8,128)}), f32[16,96,128]{2,1,0:T(8,128)S(1)}, u32[]{:S(2)}, u32[]{:S(2)}) async-start(f32[16,96,128]{2,1,0:T(8,128)} %share.1), calls=%async_computation | async-start | bytes 1572864 | tf_op jit(solution)/shard_map/all_to_all | solution.py:219
  45.8 0.0 copy-done.3
  45.8 0.1 select_reduce_fusion
  46.0 2.9 %gather_fusion = f32[32,2,2,4,3,256]{5,3,4,2,1,0:T(4,128)S(1)} fusion(f32[32,2,2,4,3,256]{5,3,4,2,1,0:T(4,128)} %param.4, s32[1024]{0:T(1024)S(1)} %pad_clamp_fusion), kind=kCustom, calls=%fused_computation | custom fusion | bytes 3145856 | tf_op jit(solution)/shard_map/gather | solution.py:221
  48.9 1.9 %copy.7 = f32[2,2,4,32,3,256]{5,4,3,2,1,0:T(4,128)} copy(f32[2,2,4,32,3,256]{5,2,4,1,0,3:T(4,128)S(1)} %bitcast.24) | data formatting | bytes 3145728 | tf_op jit(solution)/shard_map/transpose | solution.py:222
  50.8 0.0 copy-start.4
  50.8 2.9 %reshape.45.own_ref = f32[2,2,128,768]{3,2,1,0:T(8,128)S(1)} reshape(f32[2,2,4,32,3,256]{5,4,3,2,1,0:T(4,128)} %copy.7) | data formatting | bytes 3145728 | tf_op jit(solution)/shard_map/reshape | solution.py:222
  53.7 0.0 copy-start.2
  53.7 2.0 %collective-permute-start = (f32[2,2,128,768]{3,2,1,0:T(8,128)S(1)}, f32[2,2,128,768]{3,2,1,0:T(8,128)}, u32[]{:S(2)}, u32[]{:S(2)}) collective-permute-start(f32[2,2,128,768]{3,2,1,0:T(8,128)S(1)} %reshape.45.own_ref), channel_id=1, source_target_pairs={{0,1},{1,0},{2,3},{3,2},{4,5},{5,4},{6,7},{7,6},{8,9},{9,8},{10,11... | collective-permute-start | bytes 4718600 | tf_op jit(solution)/shard_map/ppermute | solution.py:223
  55.7 0.0 copy-done.4
  55.7 0.2 convert_reduce_fusion.index_ref
  55.9 0.1 select_reduce_fusion.1
  56.0 0.1 dynamic_slice.3.order_ref
  56.1 0.0 copy-done.2
  56.1 3.1 %collective-permute-done.other_ref = f32[2,2,128,768]{3,2,1,0:T(8,128)} collective-permute-done((f32[2,2,128,768]{3,2,1,0:T(8,128)S(1)}, f32[2,2,128,768]{3,2,1,0:T(8,128)}, u32[]{:S(2)}, u32[]{:S(2)}) %collective-permute-start) | collective-permute-done | bytes 1572896 | tf_op jit(solution)/shard_map/ppermute | solution.py:223
  59.2 2.4 %split.1 = (bf16[2,256,768]{2,1,0:T(8,128)(2,1)S(1)}, bf16[2,256,768]{2,1,0:T(8,128)(2,1)S(1)}, bf16[2,256,768]{2,1,0:T(8,128)(2,1)S(1)}, bf16[2,256,768]{2,1,0:T(8,128)(2,1)S(1)}) custom-call(s32[1]{0:T(128)} %bitcast.core_ref, f32[2,2,128,768]{3,2,1,0:T(8,128)} %copy-done.2, f32[2,2,128,768]{3,2,1,0:T(8,128)} %collective-permute-done.other_ref), custom_call_target="tpu_custom_call" | custom-call | tf_op jit(solution)/shard_map/split/pallas_call | solution.py:228
  61.6 0.0 copy-start
  61.6 0.9 copy-done
  62.5 22.2 %all-to-all-done = f32[16,96,128]{2,1,0:T(8,128)S(1)} async-done(((f32[16,96,128]{2,1,0:T(8,128)}), f32[16,96,128]{2,1,0:T(8,128)S(1)}, u32[]{:S(2)}, u32[]{:S(2)}) %all-to-all-start) | async-done | bytes 786464 | tf_op jit(solution)/shard_map/all_to_all | solution.py:219
  84.7 0.0 copy-start.1
  84.7 0.6 pick_rows.1
  85.3 48.7 %all_to_all.20 = f32[16,96,128]{2,1,0:T(8,128)S(1)} all-to-all(f32[16,96,128]{2,1,0:T(8,128)S(1)} %bitcast.19), channel_id=1, replica_groups=mesh['job'=2,'tq'=4,'tp'=4,'xyz'=8,'src'=2] {'tq','tp'}, dimensions={0} | all-to-all | bytes 1572864 | tf_op jit(solution)/shard_map/all_to_all | solution.py:244
  134.1 0.0 copy-done.1
  134.1 1.5 product.1
  135.5 24.6 %all_to_all.21 = f32[64,2,4,128]{3,2,1,0:T(4,128)S(1)} all-to-all(f32[64,2,4,128]{3,2,1,0:T(4,128)S(1)} %bitcast.20), channel_id=1, replica_groups=mesh['job'=2,'tq'=4,'tp'=4,'xyz'=8,'src'=2] {'xyz','tp','src'}, dimensions={0} | all-to-all | bytes 524288 | tf_op jit(solution)/shard_map/all_to_all | solution.py:259
  160.1 0.6 sum_over_xyz.1
  160.7 19.6 %all_to_all.22 = f32[16,2,2,4,128]{4,3,2,1,0:T(4,128)S(1)} all-to-all(f32[16,2,2,4,128]{4,3,2,1,0:T(4,128)S(1)} %bitcast.22), channel_id=1, replica_groups=mesh['job'=2,'tq'=4,'tp'=4,'xyz'=8,'src'=2] {'tq','tp'}, dimensions={0} | all-to-all | bytes 262144 | tf_op jit(solution)/shard_map/all_to_all | solution.py:270
  180.3 1.3 final.1
  (4 shorter events, 0.0 us)
Async XLA Ops:
  0.0 45.8 %copy-start.3 = (s32[32]{0:T(128)S(1)}, s32[32]{0:T(128)}, u32[]{:S(2)}) copy-start(s32[32]{0:T(128)} %param.7) | copy-start | bytes 388
  2.1 82.6 %all-to-all-start = ((f32[16,96,128]{2,1,0:T(8,128)}), f32[16,96,128]{2,1,0:T(8,128)S(1)}, u32[]{:S(2)}, u32[]{:S(2)}) async-start(f32[16,96,128]{2,1,0:T(8,128)} %share.1), calls=%async_computation | async-start | bytes 1572864 | tf_op jit(solution)/shard_map/all_to_all | solution.py:219
  50.8 4.9 %copy-start.4 = (s32[32]{0:T(128)S(1)}, s32[32]{0:T(128)}, u32[]{:S(2)}) copy-start(s32[32]{0:T(128)} %param.6) | copy-start | bytes 388
  53.7 2.4 %copy-start.2 = (f32[2,2,128,768]{3,2,1,0:T(8,128)}, f32[2,2,128,768]{3,2,1,0:T(8,128)S(1)}, u32[]{:S(2)}) copy-start(f32[2,2,128,768]{3,2,1,0:T(8,128)S(1)} %reshape.45.own_ref) | copy-start | bytes 4718596
  53.7 5.5 %collective-permute-start = (f32[2,2,128,768]{3,2,1,0:T(8,128)S(1)}, f32[2,2,128,768]{3,2,1,0:T(8,128)}, u32[]{:S(2)}, u32[]{:S(2)}) collective-permute-start(f32[2,2,128,768]{3,2,1,0:T(8,128)S(1)} %reshape.45.own_ref), channel_id=1, source_target_pairs={{0,1},{1,0},{2,3},{3,2},{4,5},{5,4},{6,7},{7,6},{8,9},{9,8},{10,11... | collective-permute-start | bytes 4718600 | tf_op jit(solution)/shard_map/ppermute | solution.py:223
  61.6 0.9 copy-start
  84.7 49.4 %copy-start.1 = (bf16[2,256,768]{2,1,0:T(8,128)(2,1)S(1)}, bf16[2,256,768]{2,1,0:T(8,128)(2,1)}, u32[]{:S(2)}) copy-start(bf16[2,256,768]{2,1,0:T(8,128)(2,1)} %copy-done) | copy-start | bytes 2359300

commit v15 on v10

--- a/solution.py
+++ b/solution.py
@@ -44,24 +44,23 @@
     ]
     for copy in copies:
         copy.start()
-    lines = out_ref.shape[1] // rows
     sends = []
-    for r in range(rows):
-        line = r * lines
-        for i in range(parts):
-            p = r * parts + i
-            copies[p].wait()
-            for c in range(nc):
-                for lane in range(0, sites, LANES):
-                    for f in range(folds):
-                        value = held[p, f, :, c, :, lane : lane + LANES]
-                        packed[f * per_x : (f + 1) * per_x, line : line + 2, :] = value
-                    line += 2
-        span = pl.ds(r * lines, lines)
-        sends.append(
-            pltpu.make_async_copy(packed.at[:, span], out_ref.at[:, span], out_sem.at[r])
-        )
-        sends[-1].start()
+    line = sent = 0
+    for p, copy in enumerate(copies):
+        copy.wait()
+        for c in range(nc):
+            for lane in range(0, sites, LANES):
+                for f in range(folds):
+                    value = held[p, f, :, c, :, lane : lane + LANES]
+                    packed[f * per_x : (f + 1) * per_x, line : line + 2, :] = value
+                line += 2
+        if line % 8 == 0:
+            span = pl.ds(sent, line - sent)
+            sends.append(
+                pltpu.make_async_copy(packed.at[:, span], out_ref.at[:, span], out_sem.at[p])
+            )
+            sends[-1].start()
+            sent = line
     for send in sends:
         send.wait()
 
@@ -209,7 +208,7 @@
             pltpu.VMEM((rows * part, fold, per_x, *tail), jnp.float32),
             pltpu.VMEM((nta, lines * rows, LANES), jnp.float32),
             pltpu.SemaphoreType.DMA((rows * part,)),
-            pltpu.SemaphoreType.DMA((rows,)),
+            pltpu.SemaphoreType.DMA((rows * part,)),
         ],
         name="share",
     )(

time: 181 us -> 181 us (level)
  no operation moved by 1% of the time
where the time goes in v15:
time: 181 us; the launch traced here: 180 us
  blocking collectives  91.8 us (51%)
  starting transfers between devices  45.6 us (25%)
  waiting for transfers between devices  25.3 us (14%)
  local copies, waits for them, and re-layouts  8.7 us (5%)
  Pallas kernels  8.48 us (5%)
    all_to_all x1, blocking collectives, local(): lax.all_to_all(picked.reshape(nta, tl * lines, LANES), TA, 0, 0, tiled=True)  48.7 us
    all_to_all x1, starting transfers between devices, local(): spread = lax.all_to_all(share, TA, 0, 0, tiled=True)  43.7 us
    all_to_all x1, blocking collectives, local(): got = lax.all_to_all(pair, ('tp', 'xyz', 'src'), 0, 0, tiled=True)  23.9 us
    all_to_all x1, waiting for transfers between devices, local(): spread = lax.all_to_all(share, TA, 0, 0, tiled=True)  22.2 us
    all_to_all x1, blocking collectives, local(): lax.all_to_all(back.reshape(nta, rows, nsrc, piece, ns * n), TA, 0, 0, ti...  19.2 us
  transfers between devices with their start and end apart: 2, of which 2 were waited for; matrix products, arithmetic and copies ran while one was open for 5% of the time, Pallas kernels for 1%

profile of v15, /device:TPU:80, one launch (start us, length us, event | category | flops | bytes accessed | tf_op | source)
XLA Modules:
  0.0 180.5 jit_solution(6864378954869384601)
XLA Ops:
  0.0 0.0 copy-start.3
  0.0 2.1 %share.1 = f32[16,96,128]{2,1,0:T(8,128)} custom-call(s32[1]{0:T(128)} %bitcast.core_ref, f32[2,4,2,2,8,3,2,256]{7,6,5,4,3,2,1,0:T(2,128)} %bitcast.25), custom_call_target="tpu_custom_call" | custom-call | tf_op jit(solution)/shard_map/share/pallas_call | solution.py:199
  2.1 43.7 %all-to-all-start = ((f32[16,96,128]{2,1,0:T(8,128)}), f32[16,96,128]{2,1,0:T(8,128)S(1)}, u32[]{:S(2)}, u32[]{:S(2)}) async-start(f32[16,96,128]{2,1,0:T(8,128)} %share.1), calls=%async_computation | async-start | bytes 1572864 | tf_op jit(solution)/shard_map/all_to_all | solution.py:218
  45.8 0.0 copy-done.3
  45.8 0.1 select_reduce_fusion
  46.0 2.9 %gather_fusion = f32[32,2,2,4,3,256]{5,3,4,2,1,0:T(4,128)S(1)} fusion(f32[32,2,2,4,3,256]{5,3,4,2,1,0:T(4,128)} %param.4, s32[1024]{0:T(1024)S(1)} %pad_clamp_fusion), kind=kCustom, calls=%fused_computation | custom fusion | bytes 3145856 | tf_op jit(solution)/shard_map/gather | solution.py:220
  48.9 1.9 %copy.7 = f32[2,2,4,32,3,256]{5,4,3,2,1,0:T(4,128)} copy(f32[2,2,4,32,3,256]{5,2,4,1,0,3:T(4,128)S(1)} %bitcast.24) | data formatting | bytes 3145728 | tf_op jit(solution)/shard_map/transpose | solution.py:221
  50.8 0.0 copy-start.4
  50.8 2.9 %reshape.45.own_ref = f32[2,2,128,768]{3,2,1,0:T(8,128)S(1)} reshape(f32[2,2,4,32,3,256]{5,4,3,2,1,0:T(4,128)} %copy.7) | data formatting | bytes 3145728 | tf_op jit(solution)/shard_map/reshape | solution.py:221
  53.7 0.0 copy-start.2
  53.7 2.0 %collective-permute-start = (f32[2,2,128,768]{3,2,1,0:T(8,128)S(1)}, f32[2,2,128,768]{3,2,1,0:T(8,128)}, u32[]{:S(2)}, u32[]{:S(2)}) collective-permute-start(f32[2,2,128,768]{3,2,1,0:T(8,128)S(1)} %reshape.45.own_ref), channel_id=1, source_target_pairs={{0,1},{1,0},{2,3},{3,2},{4,5},{5,4},{6,7},{7,6},{8,9},{9,8},{10,11... | collective-permute-start | bytes 4718600 | tf_op jit(solution)/shard_map/ppermute | solution.py:222
  55.7 0.0 copy-done.4
  55.7 0.2 convert_reduce_fusion.index_ref
  55.9 0.1 select_reduce_fusion.1
  56.0 0.1 dynamic_slice.3.order_ref
  56.1 0.0 copy-done.2
  56.1 3.1 %collective-permute-done.other_ref = f32[2,2,128,768]{3,2,1,0:T(8,128)} collective-permute-done((f32[2,2,128,768]{3,2,1,0:T(8,128)S(1)}, f32[2,2,128,768]{3,2,1,0:T(8,128)}, u32[]{:S(2)}, u32[]{:S(2)}) %collective-permute-start) | collective-permute-done | bytes 1572896 | tf_op jit(solution)/shard_map/ppermute | solution.py:222
  59.2 2.4 %split.1 = (bf16[2,256,768]{2,1,0:T(8,128)(2,1)S(1)}, bf16[2,256,768]{2,1,0:T(8,128)(2,1)S(1)}, bf16[2,256,768]{2,1,0:T(8,128)(2,1)S(1)}, bf16[2,256,768]{2,1,0:T(8,128)(2,1)S(1)}) custom-call(s32[1]{0:T(128)} %bitcast.core_ref, f32[2,2,128,768]{3,2,1,0:T(8,128)} %copy-done.2, f32[2,2,128,768]{3,2,1,0:T(8,128)} %collective-permute-done.other_ref), custom_call_target="tpu_custom_call" | custom-call | tf_op jit(solution)/shard_map/split/pallas_call | solution.py:227
  61.6 0.0 copy-start
  61.6 0.9 copy-done
  62.5 22.2 %all-to-all-done = f32[16,96,128]{2,1,0:T(8,128)S(1)} async-done(((f32[16,96,128]{2,1,0:T(8,128)}), f32[16,96,128]{2,1,0:T(8,128)S(1)}, u32[]{:S(2)}, u32[]{:S(2)}) %all-to-all-start) | async-done | bytes 786464 | tf_op jit(solution)/shard_map/all_to_all | solution.py:218
  84.7 0.0 copy-start.1
  84.7 0.6 pick_rows.1
  85.3 48.7 %all_to_all.20 = f32[16,96,128]{2,1,0:T(8,128)S(1)} all-to-all(f32[16,96,128]{2,1,0:T(8,128)S(1)} %bitcast.19), channel_id=1, replica_groups=mesh['job'=2,'tq'=4,'tp'=4,'xyz'=8,'src'=2] {'tq','tp'}, dimensions={0} | all-to-all | bytes 1572864 | tf_op jit(solution)/shard_map/all_to_all | solution.py:243
  134.0 0.0 copy-done.1
  134.0 1.5 product.1
  135.5 23.9 %all_to_all.21 = f32[64,2,4,128]{3,2,1,0:T(4,128)S(1)} all-to-all(f32[64,2,4,128]{3,2,1,0:T(4,128)S(1)} %bitcast.20), channel_id=1, replica_groups=mesh['job'=2,'tq'=4,'tp'=4,'xyz'=8,'src'=2] {'tp','xyz','src'}, dimensions={0} | all-to-all | bytes 524288 | tf_op jit(solution)/shard_map/all_to_all | solution.py:258
  159.4 0.6 sum_over_xyz.1
  160.0 19.2 %all_to_all.22 = f32[16,2,2,4,128]{4,3,2,1,0:T(4,128)S(1)} all-to-all(f32[16,2,2,4,128]{4,3,2,1,0:T(4,128)S(1)} %bitcast.22), channel_id=1, replica_groups=mesh['job'=2,'tq'=4,'tp'=4,'xyz'=8,'src'=2] {'tq','tp'}, dimensions={0} | all-to-all | bytes 262144 | tf_op jit(solution)/shard_map/all_to_all | solution.py:269
  179.2 1.3 final.1
  (4 shorter events, 0.0 us)
Async XLA Ops:
  0.0 45.8 %copy-start.3 = (s32[32]{0:T(128)S(1)}, s32[32]{0:T(128)}, u32[]{:S(2)}) copy-start(s32[32]{0:T(128)} %param.7) | copy-start | bytes 388
  2.1 82.6 %all-to-all-start = ((f32[16,96,128]{2,1,0:T(8,128)}), f32[16,96,128]{2,1,0:T(8,128)S(1)}, u32[]{:S(2)}, u32[]{:S(2)}) async-start(f32[16,96,128]{2,1,0:T(8,128)} %share.1), calls=%async_computation | async-start | bytes 1572864 | tf_op jit(solution)/shard_map/all_to_all | solution.py:218
  50.8 4.9 %copy-start.4 = (s32[32]{0:T(128)S(1)}, s32[32]{0:T(128)}, u32[]{:S(2)}) copy-start(s32[32]{0:T(128)} %param.6) | copy-start | bytes 388
  53.7 2.4 %copy-start.2 = (f32[2,2,128,768]{3,2,1,0:T(8,128)}, f32[2,2,128,768]{3,2,1,0:T(8,128)S(1)}, u32[]{:S(2)}) copy-start(f32[2,2,128,768]{3,2,1,0:T(8,128)S(1)} %reshape.45.own_ref) | copy-start | bytes 4718596
  53.7 5.5 %collective-permute-start = (f32[2,2,128,768]{3,2,1,0:T(8,128)S(1)}, f32[2,2,128,768]{3,2,1,0:T(8,128)}, u32[]{:S(2)}, u32[]{:S(2)}) collective-permute-start(f32[2,2,128,768]{3,2,1,0:T(8,128)S(1)} %reshape.45.own_ref), channel_id=1, source_target_pairs={{0,1},{1,0},{2,3},{3,2},{4,5},{5,4},{6,7},{7,6},{8,9},{9,8},{10,11... | collective-permute-start | bytes 4718600 | tf_op jit(solution)/shard_map/ppermute | solution.py:222
  61.6 0.9 copy-start
  84.7 49.4 %copy-start.1 = (bf16[2,256,768]{2,1,0:T(8,128)(2,1)S(1)}, bf16[2,256,768]{2,1,0:T(8,128)(2,1)}, u32[]{:S(2)}) copy-start(bf16[2,256,768]{2,1,0:T(8,128)(2,1)} %copy-done) | copy-start | bytes 2359300
